TPU v7x, 512 devices: a whole 4x8x8 slice. The times are simulated.
512 devices in a mesh: gx: 4 (over x), gy: 16 (over z_hi, y), gz: 8 (over z_lo, core).
Axes of the slice: x: 4, y: 8, z: 8 (z_hi: 2, z_lo: 4; z = z_hi * 4 + z_lo), core: 2. Of those that a mesh axis runs over, the one named last changes fastest.
Arguments:
- displacement: bfloat16 [16, 16, 16, 12, 3, 32, 128], P('gx', 'gy', 'gz'), may hold values from -96 to 96
- dof_weight: bfloat16 [16, 16, 16, 12, 128], P('gx', 'gy', 'gz'), may hold values from 0.099609375 to 10
- coarse_matrix: float32 [16, 16, 16, 27, 36, 36], P('gx', 'gy', 'gz'), may hold values from -48 to 48, as said below
- block_inverse: float32 [16, 16, 16, 36, 36], P('gx', 'gy', 'gz'), may hold values from -12 to 12, as said below
Outputs:
- edge_average: float32 [16, 16, 16, 12, 3, 32], P('gx', 'gy', 'gz')
- coarse_solution: float32 [16, 16, 16, 36, 32], P('gx', 'gy', 'gz')
Inputs may be any that keep to these rules, and one draw needn't show every extreme that they name: coarse_matrix is the replicated form of one operator over edge unknowns: rows of the same edge seen from its four subdomains are equal, and each column of an edge is stored at exactly one of that edge's subdomains (zeros at the others). block_inverse[p] is block-diagonal in 3 x 3 blocks, each the inverse of the matching diagonal 3 x 3 block of coarse_matrix[p, 13].
All inputs are finite; a program needn't handle non-finite values.
Results may differ from a plain program's by a relative error of at most 0.0003.
Values sent between devices are 32-bit elements; how exact they have to be, the bound alone decides.
No kernel may reach another device: no remote copies, remote signals or barrier semaphores. Data moves between devices by JAX's collectives and lax.ppermute only.
A program may use at most 64 MiB of HBM per device.

v0:
```python
import jax
import jax.numpy as jnp
from jax import lax
from jax.sharding import PartitionSpec as P

SWEEPS = 4
COARSE = 36


def passed_along(block, axis, distance):
    devices = range(lax.axis_size(axis))
    route = [((i - distance) % len(devices), i) for i in devices]
    return lax.ppermute(block, axis, route)


def with_halo(cells, sides, width):
    for axis, dim in sides:
        count = lax.axis_size(axis)
        head = lax.slice_in_dim(cells, 0, width, axis=dim)
        tail = lax.slice_in_dim(cells, cells.shape[dim] - width, cells.shape[dim], axis=dim)
        cells = jnp.concatenate(
            [
                lax.ppermute(tail, axis, [(i, (i + 1) % count) for i in range(count)]),
                cells,
                lax.ppermute(head, axis, [((i + 1) % count, i) for i in range(count)]),
            ],
            axis=dim,
        )
    return cells


def apply_matrix(padded, coarse_matrix, size_x, size_y, size_z):
    total = jnp.zeros((size_x, size_y, size_z) + padded.shape[3:], jnp.float32)
    for offset in range(27):
        start_x = offset // 9
        start_y = offset // 3 % 3
        start_z = offset % 3
        piece = padded[
            start_x : start_x + size_x, start_y : start_y + size_y, start_z : start_z + size_z
        ]
        total = total + jnp.einsum(
            "xyzij,xyzjr->xyzir",
            coarse_matrix[:, :, :, offset],
            piece,
            precision=lax.Precision.HIGHEST,
        )
    return total


def upper_border(array, dim):
    count = array.shape[dim]
    return lax.slice_in_dim(array, count - 1, count, axis=dim)


def lower_border(array, dim):
    return lax.slice_in_dim(array, 0, 1, axis=dim)


def from_below(array, received, dim):
    count = array.shape[dim]
    return jnp.concatenate([received, lax.slice_in_dim(array, 0, count - 1, axis=dim)], axis=dim)


def from_above(array, received, dim):
    count = array.shape[dim]
    return jnp.concatenate([lax.slice_in_dim(array, 1, count, axis=dim), received], axis=dim)


def body(displacement, dof_weight, coarse_matrix, block_inverse):
    size_x, size_y, size_z = (displacement.shape[0], displacement.shape[1], displacement.shape[2])
    numers = jnp.einsum(
        "xyzecrk,xyzek->xyzecr", displacement, dof_weight, preferred_element_type=jnp.float32
    )
    weights = jnp.sum(dof_weight.astype(jnp.float32), axis=-1)
    sources = [6, 7, 10, 11]
    targets = [4, 5, 8, 9]
    moving_numer = numers[:, :, :, sources]
    moving_weight = weights[:, :, :, sources]
    got_numer, got_weight = passed_along(
        (upper_border(moving_numer, 0), upper_border(moving_weight, 0)), "gx", 1
    )
    numers = numers.at[:, :, :, targets].add(from_below(moving_numer, got_numer, 0))
    weights = weights.at[:, :, :, targets].add(from_below(moving_weight, got_weight, 0))
    sources = [2, 3, 9]
    targets = [0, 1, 8]
    moving_numer = numers[:, :, :, sources]
    moving_weight = weights[:, :, :, sources]
    got_numer, got_weight = passed_along(
        (upper_border(moving_numer, 1), upper_border(moving_weight, 1)), "gy", 1
    )
    numers = numers.at[:, :, :, targets].add(from_below(moving_numer, got_numer, 1))
    weights = weights.at[:, :, :, targets].add(from_below(moving_weight, got_weight, 1))
    sources = [1, 5]
    targets = [0, 4]
    moving_numer = numers[:, :, :, sources]
    moving_weight = weights[:, :, :, sources]
    got_numer, got_weight = passed_along(
        (upper_border(moving_numer, 2), upper_border(moving_weight, 2)), "gz", 1
    )
    numers = numers.at[:, :, :, targets].add(from_below(moving_numer, got_numer, 2))
    weights = weights.at[:, :, :, targets].add(from_below(moving_weight, got_weight, 2))
    averages = numers / weights[..., None, None]
    moving = averages[:, :, :, [0, 4]]
    received = passed_along(lower_border(moving, 2), "gz", -1)
    averages = averages.at[:, :, :, [1, 5]].set(from_above(moving, received, 2))
    moving = averages[:, :, :, [0, 1, 8]]
    received = passed_along(lower_border(moving, 1), "gy", -1)
    averages = averages.at[:, :, :, [2, 3, 9]].set(from_above(moving, received, 1))
    moving = averages[:, :, :, [4, 5, 8, 9]]
    received = passed_along(lower_border(moving, 0), "gx", -1)
    averages = averages.at[:, :, :, [6, 7, 10, 11]].set(from_above(moving, received, 0))
    rhs_rows = averages.reshape(size_x, size_y, size_z, COARSE, averages.shape[-1])
    iterate = jnp.einsum(
        "xyzij,xyzjr->xyzir", block_inverse, rhs_rows, precision=lax.Precision.HIGHEST
    )
    for sweep in range(SWEEPS - 1):
        padded = with_halo(iterate, (("gx", 0), ("gy", 1), ("gz", 2)), 1)
        product = apply_matrix(padded, coarse_matrix, size_x, size_y, size_z)
        iterate = iterate + jnp.einsum(
            "xyzij,xyzjr->xyzir", block_inverse, rhs_rows - product, precision=lax.Precision.HIGHEST
        )
    return (averages, iterate)


def solution(mesh):
    placed = (
        P("gx", "gy", "gz", None, None, None, None),
        P("gx", "gy", "gz", None, None),
        P("gx", "gy", "gz", None, None, None),
        P("gx", "gy", "gz", None, None),
    )
    return jax.shard_map(
        body,
        mesh=mesh,
        in_specs=placed,
        out_specs=(P("gx", "gy", "gz", None, None, None), P("gx", "gy", "gz", None, None)),
        check_vma=False,
    )
```

profile of v0, /device:TPU:56, one launch (start us, length us, event | category | flops | bytes accessed | tf_op | source)
XLA Modules:
  0.0 245.6 jit_solution(9698699629595356704)
XLA Ops:
  3.3 3.4 %collective-permute-start.3 = (f32[1,1,2,4]{3,2,1,0:T(2,128)S(1)}, f32[1,1,2,4]{3,2,1,0:T(2,128)S(1)}, u32[]{:S(2)}, u32[]{:S(2)}) collective-permute-start(f32[1,1,2,4]{3,2,1,0:T(2,128)S(1)} %bitcast.691), channel_id=1, source_target_pairs={{384,0},{0,128},{128,256},{256,384},{385,1},{1,129},{129,257},{257... | collective-permute-start | bytes 104 | tf_op jit(solution)/shard_map/ppermute | solution.py:13
  6.7 3.3 %fusion = f32[4,2,12,1,3,32]{5,3,4,2,1,0:T(1,128)S(1)} fusion(bf16[4,1,2,12,3,32,128]{6,5,4,3,2,1,0:T(8,128)(2,1)S(1)} %copy-done, bf16[4,2,12,128,1,1]{3,1,2,0,4,5:T(2,128)(2,1)} %bitcast.675), kind=kOutput, calls=%fused_computation.18 | convolution fusion | flops 2359296 | bytes 2420736 | tf_op jit(solution)/shard_map/xyzecrk,xyzek->xyzecr/dot_general | solution.py:71
  12.2 3.4 %collective-permute-start = (f32[1,1,2,4,3,32]{5,0,4,2,3,1:T(1,128)S(1)}, f32[1,1,2,4,3,32]{5,0,4,2,3,1:T(1,128)S(1)}, u32[]{:S(2)}, u32[]{:S(2)}) collective-permute-start(f32[1,1,2,4,3,32]{5,0,4,2,3,1:T(1,128)S(1)} %copy.129), channel_id=1, source_target_pairs={{384,0},{0,128},{128,256},{256,384},{385,1},{1,129},{129,257},{257... | collective-permute-start | bytes 9224 | tf_op jit(solution)/shard_map/ppermute | solution.py:13
  15.8 3.2 %fusion.94 = (f32[4,1,2,1,36,36]{5,2,4,3,1,0:T(2,128)}, f32[4,1,2,1,36,36]{5,2,4,3,1,0:T(2,128)}, f32[4,1,2,1,36,36]{5,2,4,3,1,0:T(2,128)S(1)}, f32[4,1,2,1,36,3...) fusion(f32[4,1,2,27,36,36]{5,2,4,3,1,0:T(2,128)} %param.24), kind=kLoop, calls=%fused_computation.322 | loop fusion | bytes 1575936 | tf_op jit(solution)/shard_map/slice | solution.py:43
  20.4 10.1 %collective-permute-start.4 = (f32[4,1,2,3]{0,2,3,1:T(2,128)S(1)}, f32[4,1,2,3]{0,2,3,1:T(2,128)S(1)}, u32[]{:S(2)}, u32[]{:S(2)}) collective-permute-start(f32[4,1,2,3]{0,2,3,1:T(2,128)S(1)} %bitcast.690), channel_id=1, source_target_pairs={{120,0},{0,8},{8,16},{16,24},{24,32},{32,40},{40,48},{48,56},{56,6... | collective-permute-start | bytes 296 | tf_op jit(solution)/shard_map/ppermute | solution.py:13
  33.1 2.0 scatter_fusion
  36.5 10.2 %collective-permute-start.1 = (f32[4,1,2,3,3,32]{5,0,4,2,3,1:T(4,128)S(1)}, f32[4,1,2,3,3,32]{5,0,4,2,3,1:T(4,128)S(1)}, u32[]{:S(2)}, u32[]{:S(2)}) collective-permute-start(f32[4,1,2,3,3,32]{5,0,4,2,3,1:T(4,128)S(1)} %bitcast.678), channel_id=1, source_target_pairs={{120,0},{0,8},{8,16},{16,24},{24,32},{32,40},{40,48},{48,56},{56,6... | collective-permute-start | bytes 27656 | tf_op jit(solution)/shard_map/ppermute | solution.py:13
  48.7 2.0 scatter_fusion.1
  52.2 3.5 %collective-permute-start.2 = (f32[4,1,1,2,3,32]{5,0,4,2,3,1:T(4,128)S(1)}, f32[4,1,1,2,3,32]{5,0,4,2,3,1:T(4,128)S(1)}, u32[]{:S(2)}, u32[]{:S(2)}) collective-permute-start(f32[4,1,1,2,3,32]{5,0,4,2,3,1:T(4,128)S(1)} %get-tuple-element.57), channel_id=1, source_target_pairs={{7,0},{0,1},{1,2},{2,3},{3,4},{4,5},{5,6},{6,7},{15,8},{8,9},{9,10... | collective-permute-start | bytes 9224 | tf_op jit(solution)/shard_map/ppermute | solution.py:13
  56.3 2.7 %collective-permute-done.2 = f32[4,1,1,2,3,32]{5,0,4,2,3,1:T(4,128)S(1)} collective-permute-done((f32[4,1,1,2,3,32]{5,0,4,2,3,1:T(4,128)S(1)}, f32[4,1,1,2,3,32]{5,0,4,2,3,1:T(4,128)S(1)}, u32[]{:S(2)}, u32[]{:S(2)}) %collective-permute-start.2) | collective-permute-done | bytes 3104 | tf_op jit(solution)/shard_map/ppermute | solution.py:13
  69.0 10.3 %collective-permute-done.7 = f32[4,1,2,3,3,32]{5,0,4,2,3,1:T(4,128)S(1)} collective-permute-done((f32[4,1,2,3,3,32]{5,0,4,2,3,1:T(4,128)S(1)}, f32[4,1,2,3,3,32]{5,0,4,2,3,1:T(4,128)S(1)}, u32[]{:S(2)}, u32[]{:S(2)}) %collective-permute-start.7) | collective-permute-done | bytes 9248 | tf_op jit(solution)/shard_map/ppermute | solution.py:13
  80.6 3.7 %collective-permute-start.8 = (f32[1,1,2,4,3,32]{5,0,4,2,3,1:T(1,128)S(1)}, f32[1,1,2,4,3,32]{5,0,4,2,3,1:T(1,128)S(1)}, u32[]{:S(2)}, u32[]{:S(2)}) collective-permute-start(f32[1,1,2,4,3,32]{5,0,4,2,3,1:T(1,128)S(1)} %copy.140), channel_id=1, source_target_pairs={{128,0},{256,128},{384,256},{0,384},{129,1},{257,129},{385,257},{1... | collective-permute-start | bytes 9224 | tf_op jit(solution)/shard_map/ppermute | solution.py:13
  89.1 4.9 %collective-permute-start.10 = (f32[1,1,2,36,32]{3,4,2,1,0:T(8,128)S(1)}, f32[1,1,2,36,32]{3,4,2,1,0:T(8,128)S(1)}, u32[]{:S(2)}, u32[]{:S(2)}) collective-permute-start(f32[1,1,2,36,32]{3,4,2,1,0:T(8,128)S(1)} %get-tuple-element.54), channel_id=1, source_target_pairs={{128,0},{256,128},{384,256},{0,384},{129,1},{257,129},{385,257},{1... | collective-permute-start | bytes 27656 | tf_op jit(solution)/shard_map/ppermute | solution.py:25
  97.4 3.6 %collective-permute-done.9 = f32[1,1,2,36,32]{3,4,2,0,1:T(8,128)S(1)} collective-permute-done((f32[1,1,2,36,32]{3,4,2,0,1:T(8,128)S(1)}, f32[1,1,2,36,32]{3,4,2,0,1:T(8,128)S(1)}, u32[]{:S(2)}, u32[]{:S(2)}) %collective-permute-start.9) | collective-permute-done | bytes 9248 | tf_op jit(solution)/shard_map/ppermute | solution.py:23
  101.0 3.9 %collective-permute-start.11 = (f32[6,1,2,36,32]{3,4,2,0,1:T(8,128)S(1)}, f32[6,1,2,36,32]{3,4,2,0,1:T(8,128)S(1)}, u32[]{:S(2)}, u32[]{:S(2)}) collective-permute-start(f32[6,1,2,36,32]{3,4,2,0,1:T(8,128)S(1)} %pad_maximum_fusion.6), channel_id=1, source_target_pairs={{0,8},{8,16},{16,24},{24,32},{32,40},{40,48},{48,56},{56,64},{64,7... | collective-permute-start | bytes 165896 | tf_op jit(solution)/shard_map/ppermute | solution.py:23
  108.6 11.2 %collective-permute-done.12 = f32[6,1,2,36,32]{3,4,2,0,1:T(8,128)S(1)} collective-permute-done((f32[6,1,2,36,32]{3,4,2,0,1:T(8,128)S(1)}, f32[6,1,2,36,32]{3,4,2,0,1:T(8,128)S(1)}, u32[]{:S(2)}, u32[]{:S(2)}) %collective-permute-start.12) | collective-permute-done | bytes 55328 | tf_op jit(solution)/shard_map/ppermute | solution.py:25
  119.9 2.1 collective-permute-start.13
  122.0 5.6 %collective-permute-start.14 = (f32[6,3,1,36,32]{3,4,2,0,1:T(8,128)S(1)}, f32[6,3,1,36,32]{3,4,2,0,1:T(8,128)S(1)}, u32[]{:S(2)}, u32[]{:S(2)}) collective-permute-start(f32[6,3,1,36,32]{3,4,2,0,1:T(8,128)S(1)} %get-tuple-element.48), channel_id=1, source_target_pairs={{1,0},{2,1},{3,2},{4,3},{5,4},{6,5},{7,6},{0,7},{9,8},{10,9},{11,1... | collective-permute-start | bytes 248840 | tf_op jit(solution)/shard_map/ppermute | solution.py:25
  141.4 2.7 %collective-permute-start.16 = (f32[1,1,2,36,32]{3,4,2,1,0:T(8,128)S(1)}, f32[1,1,2,36,32]{3,4,2,1,0:T(8,128)S(1)}, u32[]{:S(2)}, u32[]{:S(2)}) collective-permute-start(f32[1,1,2,36,32]{3,4,2,1,0:T(8,128)S(1)} %get-tuple-element.52), channel_id=1, source_target_pairs={{128,0},{256,128},{384,256},{0,384},{129,1},{257,129},{385,257},{1... | collective-permute-start | bytes 27656 | tf_op jit(solution)/shard_map/ppermute | solution.py:25
  144.1 3.1 %collective-permute-start.15 = (f32[1,1,2,36,32]{3,4,2,0,1:T(8,128)S(1)}, f32[1,1,2,36,32]{3,4,2,0,1:T(8,128)S(1)}, u32[]{:S(2)}, u32[]{:S(2)}) collective-permute-start(f32[1,1,2,36,32]{3,4,2,0,1:T(8,128)S(1)} %get-tuple-element.51), channel_id=1, source_target_pairs={{0,128},{128,256},{256,384},{384,0},{1,129},{129,257},{257,385},{3... | collective-permute-start | bytes 27656 | tf_op jit(solution)/shard_map/ppermute | solution.py:23
  147.3 4.2 %collective-permute-done.15 = f32[1,1,2,36,32]{3,4,2,0,1:T(8,128)S(1)} collective-permute-done((f32[1,1,2,36,32]{3,4,2,0,1:T(8,128)S(1)}, f32[1,1,2,36,32]{3,4,2,0,1:T(8,128)S(1)}, u32[]{:S(2)}, u32[]{:S(2)}) %collective-permute-start.15) | collective-permute-done | bytes 9248 | tf_op jit(solution)/shard_map/ppermute | solution.py:23
  153.4 3.9 %collective-permute-start.18 = (f32[6,1,2,36,32]{3,4,2,0,1:T(8,128)S(1)}, f32[6,1,2,36,32]{3,4,2,0,1:T(8,128)S(1)}, u32[]{:S(2)}, u32[]{:S(2)}) collective-permute-start(f32[6,1,2,36,32]{3,4,2,0,1:T(8,128)S(1)} %pad_maximum_fusion.7), channel_id=1, source_target_pairs={{8,0},{16,8},{24,16},{32,24},{40,32},{48,40},{56,48},{64,56},{72,6... | collective-permute-start | bytes 165896 | tf_op jit(solution)/shard_map/ppermute | solution.py:25
  157.7 2.6 %collective-permute-done.17 = f32[6,1,2,36,32]{3,4,2,0,1:T(8,128)S(1)} collective-permute-done((f32[6,1,2,36,32]{3,4,2,0,1:T(8,128)S(1)}, f32[6,1,2,36,32]{3,4,2,0,1:T(8,128)S(1)}, u32[]{:S(2)}, u32[]{:S(2)}) %collective-permute-start.17) | collective-permute-done | bytes 55328 | tf_op jit(solution)/shard_map/ppermute | solution.py:23
  160.3 12.0 %collective-permute-done.18 = f32[6,1,2,36,32]{3,4,2,0,1:T(8,128)S(1)} collective-permute-done((f32[6,1,2,36,32]{3,4,2,0,1:T(8,128)S(1)}, f32[6,1,2,36,32]{3,4,2,0,1:T(8,128)S(1)}, u32[]{:S(2)}, u32[]{:S(2)}) %collective-permute-start.18) | collective-permute-done | bytes 55328 | tf_op jit(solution)/shard_map/ppermute | solution.py:25
  174.3 5.7 %collective-permute-start.20 = (f32[6,3,1,36,32]{3,4,2,0,1:T(8,128)S(1)}, f32[6,3,1,36,32]{3,4,2,0,1:T(8,128)S(1)}, u32[]{:S(2)}, u32[]{:S(2)}) collective-permute-start(f32[6,3,1,36,32]{3,4,2,0,1:T(8,128)S(1)} %get-tuple-element.44), channel_id=1, source_target_pairs={{1,0},{2,1},{3,2},{4,3},{5,4},{6,5},{7,6},{0,7},{9,8},{10,9},{11,1... | collective-permute-start | bytes 248840 | tf_op jit(solution)/shard_map/ppermute | solution.py:25
  181.2 4.2 %collective-permute-done.19 = f32[6,3,1,36,32]{3,4,2,0,1:T(8,128)S(1)} collective-permute-done((f32[6,3,1,36,32]{3,4,2,0,1:T(8,128)S(1)}, f32[6,3,1,36,32]{3,4,2,0,1:T(8,128)S(1)}, u32[]{:S(2)}, u32[]{:S(2)}) %collective-permute-start.19) | collective-permute-done | bytes 82976 | tf_op jit(solution)/shard_map/ppermute | solution.py:23
  196.9 3.9 %collective-permute-start.21 = (f32[1,1,2,36,32]{3,4,2,0,1:T(8,128)S(1)}, f32[1,1,2,36,32]{3,4,2,0,1:T(8,128)S(1)}, u32[]{:S(2)}, u32[]{:S(2)}) collective-permute-start(f32[1,1,2,36,32]{3,4,2,0,1:T(8,128)S(1)} %get-tuple-element.49), channel_id=1, source_target_pairs={{0,128},{128,256},{256,384},{384,0},{1,129},{129,257},{257,385},{3... | collective-permute-start | bytes 27656 | tf_op jit(solution)/shard_map/ppermute | solution.py:23
  201.6 2.3 collective-permute-done.21
  205.8 3.9 %collective-permute-start.24 = (f32[6,1,2,36,32]{3,4,2,0,1:T(8,128)S(1)}, f32[6,1,2,36,32]{3,4,2,0,1:T(8,128)S(1)}, u32[]{:S(2)}, u32[]{:S(2)}) collective-permute-start(f32[6,1,2,36,32]{3,4,2,0,1:T(8,128)S(1)} %pad_maximum_fusion.8), channel_id=1, source_target_pairs={{8,0},{16,8},{24,16},{32,24},{40,32},{48,40},{56,48},{64,56},{72,6... | collective-permute-start | bytes 165896 | tf_op jit(solution)/shard_map/ppermute | solution.py:25
  211.5 11.2 %collective-permute-done.24 = f32[6,1,2,36,32]{3,4,2,0,1:T(8,128)S(1)} collective-permute-done((f32[6,1,2,36,32]{3,4,2,0,1:T(8,128)S(1)}, f32[6,1,2,36,32]{3,4,2,0,1:T(8,128)S(1)}, u32[]{:S(2)}, u32[]{:S(2)}) %collective-permute-start.24) | collective-permute-done | bytes 55328 | tf_op jit(solution)/shard_map/ppermute | solution.py:25
  224.7 5.7 %collective-permute-start.26 = (f32[6,3,1,36,32]{3,4,2,0,1:T(8,128)S(1)}, f32[6,3,1,36,32]{3,4,2,0,1:T(8,128)S(1)}, u32[]{:S(2)}, u32[]{:S(2)}) collective-permute-start(f32[6,3,1,36,32]{3,4,2,0,1:T(8,128)S(1)} %get-tuple-element.40), channel_id=1, source_target_pairs={{1,0},{2,1},{3,2},{4,3},{5,4},{6,5},{7,6},{0,7},{9,8},{10,9},{11,1... | collective-permute-start | bytes 248840 | tf_op jit(solution)/shard_map/ppermute | solution.py:25
  231.6 3.9 %collective-permute-done.25 = f32[6,3,1,36,32]{3,4,2,0,1:T(8,128)S(1)} collective-permute-done((f32[6,3,1,36,32]{3,4,2,0,1:T(8,128)S(1)}, f32[6,3,1,36,32]{3,4,2,0,1:T(8,128)S(1)}, u32[]{:S(2)}, u32[]{:S(2)}) %collective-permute-start.25) | collective-permute-done | bytes 82976 | tf_op jit(solution)/shard_map/ppermute | solution.py:23
  (223 shorter events, 85.1 us)
Async XLA Ops:
  3.3 15.8 %collective-permute-start.3 = (f32[1,1,2,4]{3,2,1,0:T(2,128)S(1)}, f32[1,1,2,4]{3,2,1,0:T(2,128)S(1)}, u32[]{:S(2)}, u32[]{:S(2)}) collective-permute-start(f32[1,1,2,4]{3,2,1,0:T(2,128)S(1)} %bitcast.691), channel_id=1, source_target_pairs={{384,0},{0,128},{128,256},{256,384},{385,1},{1,129},{129,257},{257... | collective-permute-start | bytes 104 | tf_op jit(solution)/shard_map/ppermute | solution.py:13
  12.2 20.8 %collective-permute-start = (f32[1,1,2,4,3,32]{5,0,4,2,3,1:T(1,128)S(1)}, f32[1,1,2,4,3,32]{5,0,4,2,3,1:T(1,128)S(1)}, u32[]{:S(2)}, u32[]{:S(2)}) collective-permute-start(f32[1,1,2,4,3,32]{5,0,4,2,3,1:T(1,128)S(1)} %copy.129), channel_id=1, source_target_pairs={{384,0},{0,128},{128,256},{256,384},{385,1},{1,129},{129,257},{257... | collective-permute-start | bytes 9224 | tf_op jit(solution)/shard_map/ppermute | solution.py:13
  15.8 16.0 %copy-start.17 = (s32[3]{0:T(128)S(1)}, s32[3]{0:T(128)}, u32[]{:S(2)}) copy-start(s32[3]{0:T(128)} %constant.55) | copy-start | bytes 40
  15.8 70.5 %copy-start.18 = (s32[4]{0:T(128)S(1)}, s32[4]{0:T(128)}, u32[]{:S(2)}) copy-start(s32[4]{0:T(128)} %constant.54) | copy-start | bytes 52
  19.0 69.7 %copy-start.1 = (f32[4,1,2,36,36]{4,2,3,1,0:T(2,128)S(1)}, f32[4,1,2,36,36]{4,2,3,1,0:T(2,128)}, u32[]{:S(2)}) copy-start(f32[4,1,2,36,36]{4,2,3,1,0:T(2,128)} %param.25) | copy-start | bytes 124420
  20.4 11.4 %collective-permute-start.4 = (f32[4,1,2,3]{0,2,3,1:T(2,128)S(1)}, f32[4,1,2,3]{0,2,3,1:T(2,128)S(1)}, u32[]{:S(2)}, u32[]{:S(2)}) collective-permute-start(f32[4,1,2,3]{0,2,3,1:T(2,128)S(1)} %bitcast.690), channel_id=1, source_target_pairs={{120,0},{0,8},{8,16},{16,24},{24,32},{32,40},{40,48},{48,56},{56,6... | collective-permute-start | bytes 296 | tf_op jit(solution)/shard_map/ppermute | solution.py:13
  36.5 12.2 %collective-permute-start.1 = (f32[4,1,2,3,3,32]{5,0,4,2,3,1:T(4,128)S(1)}, f32[4,1,2,3,3,32]{5,0,4,2,3,1:T(4,128)S(1)}, u32[]{:S(2)}, u32[]{:S(2)}) collective-permute-start(f32[4,1,2,3,3,32]{5,0,4,2,3,1:T(4,128)S(1)} %bitcast.678), channel_id=1, source_target_pairs={{120,0},{0,8},{8,16},{16,24},{24,32},{32,40},{40,48},{48,56},{56,6... | collective-permute-start | bytes 27656 | tf_op jit(solution)/shard_map/ppermute | solution.py:13
  46.8 8.9 %collective-permute-start.5 = (f32[4,1,1,2]{0,3,2,1:T(2,128)S(1)}, f32[4,1,1,2]{0,3,2,1:T(2,128)S(1)}, u32[]{:S(2)}, u32[]{:S(2)}) collective-permute-start(f32[4,1,1,2]{0,3,2,1:T(2,128)S(1)} %get-tuple-element.59), channel_id=1, source_target_pairs={{7,0},{0,1},{1,2},{2,3},{3,4},{4,5},{5,6},{6,7},{15,8},{8,9},{9,10... | collective-permute-start | bytes 104 | tf_op jit(solution)/shard_map/ppermute | solution.py:13
  52.2 6.8 %collective-permute-start.2 = (f32[4,1,1,2,3,32]{5,0,4,2,3,1:T(4,128)S(1)}, f32[4,1,1,2,3,32]{5,0,4,2,3,1:T(4,128)S(1)}, u32[]{:S(2)}, u32[]{:S(2)}) collective-permute-start(f32[4,1,1,2,3,32]{5,0,4,2,3,1:T(4,128)S(1)} %get-tuple-element.57), channel_id=1, source_target_pairs={{7,0},{0,1},{1,2},{2,3},{3,4},{4,5},{5,6},{6,7},{15,8},{8,9},{9,10... | collective-permute-start | bytes 9224 | tf_op jit(solution)/shard_map/ppermute | solution.py:13
  62.5 3.3 %collective-permute-start.6 = (f32[4,1,1,2,3,32]{5,0,4,2,3,1:T(4,128)S(1)}, f32[4,1,1,2,3,32]{5,0,4,2,3,1:T(4,128)S(1)}, u32[]{:S(2)}, u32[]{:S(2)}) collective-permute-start(f32[4,1,1,2,3,32]{5,0,4,2,3,1:T(4,128)S(1)} %get-tuple-element.56), channel_id=1, source_target_pairs={{1,0},{2,1},{3,2},{4,3},{5,4},{6,5},{7,6},{0,7},{9,8},{10,9},{11,1... | collective-permute-start | bytes 9224 | tf_op jit(solution)/shard_map/ppermute | solution.py:13
  67.0 12.2 %collective-permute-start.7 = (f32[4,1,2,3,3,32]{5,0,4,2,3,1:T(4,128)S(1)}, f32[4,1,2,3,3,32]{5,0,4,2,3,1:T(4,128)S(1)}, u32[]{:S(2)}, u32[]{:S(2)}) collective-permute-start(f32[4,1,2,3,3,32]{5,0,4,2,3,1:T(4,128)S(1)} %bitcast.679), channel_id=1, source_target_pairs={{8,0},{16,8},{24,16},{32,24},{40,32},{48,40},{56,48},{64,56},{72,6... | collective-permute-start | bytes 27656 | tf_op jit(solution)/shard_map/ppermute | solution.py:13
  80.6 5.6 %collective-permute-start.8 = (f32[1,1,2,4,3,32]{5,0,4,2,3,1:T(1,128)S(1)}, f32[1,1,2,4,3,32]{5,0,4,2,3,1:T(1,128)S(1)}, u32[]{:S(2)}, u32[]{:S(2)}) collective-permute-start(f32[1,1,2,4,3,32]{5,0,4,2,3,1:T(1,128)S(1)} %copy.140), channel_id=1, source_target_pairs={{128,0},{256,128},{384,256},{0,384},{129,1},{257,129},{385,257},{1... | collective-permute-start | bytes 9224 | tf_op jit(solution)/shard_map/ppermute | solution.py:13
  89.1 8.3 %collective-permute-start.10 = (f32[1,1,2,36,32]{3,4,2,1,0:T(8,128)S(1)}, f32[1,1,2,36,32]{3,4,2,1,0:T(8,128)S(1)}, u32[]{:S(2)}, u32[]{:S(2)}) collective-permute-start(f32[1,1,2,36,32]{3,4,2,1,0:T(8,128)S(1)} %get-tuple-element.54), channel_id=1, source_target_pairs={{128,0},{256,128},{384,256},{0,384},{129,1},{257,129},{385,257},{1... | collective-permute-start | bytes 27656 | tf_op jit(solution)/shard_map/ppermute | solution.py:25
  94.0 7.0 %collective-permute-start.9 = (f32[1,1,2,36,32]{3,4,2,0,1:T(8,128)S(1)}, f32[1,1,2,36,32]{3,4,2,0,1:T(8,128)S(1)}, u32[]{:S(2)}, u32[]{:S(2)}) collective-permute-start(f32[1,1,2,36,32]{3,4,2,0,1:T(8,128)S(1)} %get-tuple-element.53), channel_id=1, source_target_pairs={{0,128},{128,256},{256,384},{384,0},{1,129},{129,257},{257,385},{3... | collective-permute-start | bytes 27656 | tf_op jit(solution)/shard_map/ppermute | solution.py:23
  97.4 30.6 %copy-start.6 = (f32[4,1,2,1,36,36]{5,2,4,3,1,0:T(2,128)S(1)}, f32[4,1,2,1,36,36]{5,2,4,3,1,0:T(2,128)}, u32[]{:S(2)}) copy-start(f32[4,1,2,1,36,36]{5,2,4,3,1,0:T(2,128)} %get-tuple-element.11) | copy-start | bytes 124420
  97.4 31.0 %copy-start.5 = (f32[4,1,2,1,36,36]{5,2,4,3,1,0:T(2,128)S(1)}, f32[4,1,2,1,36,36]{5,2,4,3,1,0:T(2,128)}, u32[]{:S(2)}) copy-start(f32[4,1,2,1,36,36]{5,2,4,3,1,0:T(2,128)} %get-tuple-element.17) | copy-start | bytes 124420
  101.0 7.6 %collective-permute-start.11 = (f32[6,1,2,36,32]{3,4,2,0,1:T(8,128)S(1)}, f32[6,1,2,36,32]{3,4,2,0,1:T(8,128)S(1)}, u32[]{:S(2)}, u32[]{:S(2)}) collective-permute-start(f32[6,1,2,36,32]{3,4,2,0,1:T(8,128)S(1)} %pad_maximum_fusion.6), channel_id=1, source_target_pairs={{0,8},{8,16},{16,24},{24,32},{32,40},{40,48},{48,56},{56,64},{64,7... | collective-permute-start | bytes 165896 | tf_op jit(solution)/shard_map/ppermute | solution.py:23
  105.0 14.8 %collective-permute-start.12 = (f32[6,1,2,36,32]{3,4,2,0,1:T(8,128)S(1)}, f32[6,1,2,36,32]{3,4,2,0,1:T(8,128)S(1)}, u32[]{:S(2)}, u32[]{:S(2)}) collective-permute-start(f32[6,1,2,36,32]{3,4,2,0,1:T(8,128)S(1)} %pad_maximum_fusion.6), channel_id=1, source_target_pairs={{8,0},{16,8},{24,16},{32,24},{40,32},{48,40},{56,48},{64,56},{72,6... | collective-permute-start | bytes 165896 | tf_op jit(solution)/shard_map/ppermute | solution.py:25
  119.9 10.6 %collective-permute-start.13 = (f32[6,3,1,36,32]{3,4,2,0,1:T(8,128)S(1)}, f32[6,3,1,36,32]{3,4,2,0,1:T(8,128)S(1)}, u32[]{:S(2)}, u32[]{:S(2)}) collective-permute-start(f32[6,3,1,36,32]{3,4,2,0,1:T(8,128)S(1)} %get-tuple-element.47), channel_id=1, source_target_pairs={{0,1},{1,2},{2,3},{3,4},{4,5},{5,6},{6,7},{7,0},{8,9},{9,10},{10,1... | collective-permute-start | bytes 248840 | tf_op jit(solution)/shard_map/ppermute | solution.py:23
  122.0 9.7 %collective-permute-start.14 = (f32[6,3,1,36,32]{3,4,2,0,1:T(8,128)S(1)}, f32[6,3,1,36,32]{3,4,2,0,1:T(8,128)S(1)}, u32[]{:S(2)}, u32[]{:S(2)}) collective-permute-start(f32[6,3,1,36,32]{3,4,2,0,1:T(8,128)S(1)} %get-tuple-element.48), channel_id=1, source_target_pairs={{1,0},{2,1},{3,2},{4,3},{5,4},{6,5},{7,6},{0,7},{9,8},{10,9},{11,1... | collective-permute-start | bytes 248840 | tf_op jit(solution)/shard_map/ppermute | solution.py:25
  141.4 5.9 %collective-permute-start.16 = (f32[1,1,2,36,32]{3,4,2,1,0:T(8,128)S(1)}, f32[1,1,2,36,32]{3,4,2,1,0:T(8,128)S(1)}, u32[]{:S(2)}, u32[]{:S(2)}) collective-permute-start(f32[1,1,2,36,32]{3,4,2,1,0:T(8,128)S(1)} %get-tuple-element.52), channel_id=1, source_target_pairs={{128,0},{256,128},{384,256},{0,384},{129,1},{257,129},{385,257},{1... | collective-permute-start | bytes 27656 | tf_op jit(solution)/shard_map/ppermute | solution.py:25
  144.1 7.3 %collective-permute-start.15 = (f32[1,1,2,36,32]{3,4,2,0,1:T(8,128)S(1)}, f32[1,1,2,36,32]{3,4,2,0,1:T(8,128)S(1)}, u32[]{:S(2)}, u32[]{:S(2)}) collective-permute-start(f32[1,1,2,36,32]{3,4,2,0,1:T(8,128)S(1)} %get-tuple-element.51), channel_id=1, source_target_pairs={{0,128},{128,256},{256,384},{384,0},{1,129},{129,257},{257,385},{3... | collective-permute-start | bytes 27656 | tf_op jit(solution)/shard_map/ppermute | solution.py:23
  151.5 8.8 %collective-permute-start.17 = (f32[6,1,2,36,32]{3,4,2,0,1:T(8,128)S(1)}, f32[6,1,2,36,32]{3,4,2,0,1:T(8,128)S(1)}, u32[]{:S(2)}, u32[]{:S(2)}) collective-permute-start(f32[6,1,2,36,32]{3,4,2,0,1:T(8,128)S(1)} %pad_maximum_fusion.7), channel_id=1, source_target_pairs={{0,8},{8,16},{16,24},{24,32},{32,40},{40,48},{48,56},{56,64},{64,7... | collective-permute-start | bytes 165896 | tf_op jit(solution)/shard_map/ppermute | solution.py:23
  153.4 18.9 %collective-permute-start.18 = (f32[6,1,2,36,32]{3,4,2,0,1:T(8,128)S(1)}, f32[6,1,2,36,32]{3,4,2,0,1:T(8,128)S(1)}, u32[]{:S(2)}, u32[]{:S(2)}) collective-permute-start(f32[6,1,2,36,32]{3,4,2,0,1:T(8,128)S(1)} %pad_maximum_fusion.7), channel_id=1, source_target_pairs={{8,0},{16,8},{24,16},{32,24},{40,32},{48,40},{56,48},{64,56},{72,6... | collective-permute-start | bytes 165896 | tf_op jit(solution)/shard_map/ppermute | solution.py:25
  172.4 13.0 %collective-permute-start.19 = (f32[6,3,1,36,32]{3,4,2,0,1:T(8,128)S(1)}, f32[6,3,1,36,32]{3,4,2,0,1:T(8,128)S(1)}, u32[]{:S(2)}, u32[]{:S(2)}) collective-permute-start(f32[6,3,1,36,32]{3,4,2,0,1:T(8,128)S(1)} %get-tuple-element.43), channel_id=1, source_target_pairs={{0,1},{1,2},{2,3},{3,4},{4,5},{5,6},{6,7},{7,0},{8,9},{9,10},{10,1... | collective-permute-start | bytes 248840 | tf_op jit(solution)/shard_map/ppermute | solution.py:23
  174.3 11.1 %collective-permute-start.20 = (f32[6,3,1,36,32]{3,4,2,0,1:T(8,128)S(1)}, f32[6,3,1,36,32]{3,4,2,0,1:T(8,128)S(1)}, u32[]{:S(2)}, u32[]{:S(2)}) collective-permute-start(f32[6,3,1,36,32]{3,4,2,0,1:T(8,128)S(1)} %get-tuple-element.44), channel_id=1, source_target_pairs={{1,0},{2,1},{3,2},{4,3},{5,4},{6,5},{7,6},{0,7},{9,8},{10,9},{11,1... | collective-permute-start | bytes 248840 | tf_op jit(solution)/shard_map/ppermute | solution.py:25
  194.9 6.6 %collective-permute-start.22 = (f32[1,1,2,36,32]{3,4,2,1,0:T(8,128)S(1)}, f32[1,1,2,36,32]{3,4,2,1,0:T(8,128)S(1)}, u32[]{:S(2)}, u32[]{:S(2)}) collective-permute-start(f32[1,1,2,36,32]{3,4,2,1,0:T(8,128)S(1)} %get-tuple-element.50), channel_id=1, source_target_pairs={{128,0},{256,128},{384,256},{0,384},{129,1},{257,129},{385,257},{1... | collective-permute-start | bytes 27656 | tf_op jit(solution)/shard_map/ppermute | solution.py:25
  196.9 7.0 %collective-permute-start.21 = (f32[1,1,2,36,32]{3,4,2,0,1:T(8,128)S(1)}, f32[1,1,2,36,32]{3,4,2,0,1:T(8,128)S(1)}, u32[]{:S(2)}, u32[]{:S(2)}) collective-permute-start(f32[1,1,2,36,32]{3,4,2,0,1:T(8,128)S(1)} %get-tuple-element.49), channel_id=1, source_target_pairs={{0,128},{128,256},{256,384},{384,0},{1,129},{129,257},{257,385},{3... | collective-permute-start | bytes 27656 | tf_op jit(solution)/shard_map/ppermute | solution.py:23
  203.9 7.6 %collective-permute-start.23 = (f32[6,1,2,36,32]{3,4,2,0,1:T(8,128)S(1)}, f32[6,1,2,36,32]{3,4,2,0,1:T(8,128)S(1)}, u32[]{:S(2)}, u32[]{:S(2)}) collective-permute-start(f32[6,1,2,36,32]{3,4,2,0,1:T(8,128)S(1)} %pad_maximum_fusion.8), channel_id=1, source_target_pairs={{0,8},{8,16},{16,24},{24,32},{32,40},{40,48},{48,56},{56,64},{64,7... | collective-permute-start | bytes 165896 | tf_op jit(solution)/shard_map/ppermute | solution.py:23
  205.8 16.8 %collective-permute-start.24 = (f32[6,1,2,36,32]{3,4,2,0,1:T(8,128)S(1)}, f32[6,1,2,36,32]{3,4,2,0,1:T(8,128)S(1)}, u32[]{:S(2)}, u32[]{:S(2)}) collective-permute-start(f32[6,1,2,36,32]{3,4,2,0,1:T(8,128)S(1)} %pad_maximum_fusion.8), channel_id=1, source_target_pairs={{8,0},{16,8},{24,16},{32,24},{40,32},{48,40},{56,48},{64,56},{72,6... | collective-permute-start | bytes 165896 | tf_op jit(solution)/shard_map/ppermute | solution.py:25
  222.8 12.7 %collective-permute-start.25 = (f32[6,3,1,36,32]{3,4,2,0,1:T(8,128)S(1)}, f32[6,3,1,36,32]{3,4,2,0,1:T(8,128)S(1)}, u32[]{:S(2)}, u32[]{:S(2)}) collective-permute-start(f32[6,3,1,36,32]{3,4,2,0,1:T(8,128)S(1)} %get-tuple-element.39), channel_id=1, source_target_pairs={{0,1},{1,2},{2,3},{3,4},{4,5},{5,6},{6,7},{7,0},{8,9},{9,10},{10,1... | collective-permute-start | bytes 248840 | tf_op jit(solution)/shard_map/ppermute | solution.py:23
  224.7 10.8 %collective-permute-start.26 = (f32[6,3,1,36,32]{3,4,2,0,1:T(8,128)S(1)}, f32[6,3,1,36,32]{3,4,2,0,1:T(8,128)S(1)}, u32[]{:S(2)}, u32[]{:S(2)}) collective-permute-start(f32[6,3,1,36,32]{3,4,2,0,1:T(8,128)S(1)} %get-tuple-element.40), channel_id=1, source_target_pairs={{1,0},{2,1},{3,2},{4,3},{5,4},{6,5},{7,6},{0,7},{9,8},{10,9},{11,1... | collective-permute-start | bytes 248840 | tf_op jit(solution)/shard_map/ppermute | solution.py:25
  (16 other events, 90.2 us)
where the time goes:
time: 247 us; the launch traced here: 246 us
  starting transfers between devices  98.9 us (40%)
  waiting for transfers between devices  78.4 us (32%)
  matrix products  36 us (15%)
  local copies, waits for them, and re-layouts  18.7 us (8%)
  other arithmetic  11.5 us (5%)
    ppermute x9, starting transfers between devices, passed_along(): return lax.ppermute(block, axis, route)  40 us
    ppermute x9, starting transfers between devices, with_halo(): lax.ppermute(head, axis, [((i + 1) % count, i) for i in range(count)])  36.3 us
    ppermute x9, waiting for transfers between devices, with_halo(): lax.ppermute(head, axis, [((i + 1) % count, i) for i in range(count)])  35.7 us
    dot_general x81, matrix products, apply_matrix(): jnp.einsum('xyzij,xyzjr->xyzir', coarse_matrix[:, :, :, offset], piece, p...  30.6 us
    ppermute x9, waiting for transfers between devices, with_halo(): lax.ppermute(tail, axis, [(i, (i + 1) % count) for i in range(count)])  25.2 us
    ppermute x9, starting transfers between devices, with_halo(): lax.ppermute(tail, axis, [(i, (i + 1) % count) for i in range(count)])  22.6 us
    ppermute x9, waiting for transfers between devices, passed_along(): return lax.ppermute(block, axis, route)  17.5 us
  transfers between devices with their start and end apart: 27, of which 18 were waited for; matrix products, arithmetic and copies ran while one was open for 9% of the time, Pallas kernels for 0%

commit v1 on v0

v1 whole, which is shorter than its diff:
```python
import functools

import jax
import jax.numpy as jnp
import numpy as np
from jax import lax
from jax.experimental import pallas as pl
from jax.experimental.pallas import tpu as pltpu
from jax.sharding import PartitionSpec as P

F32 = jnp.float32
BF16 = jnp.bfloat16
OFFSETS = (
    (0, 0, 0), (0, 0, 1), (0, 1, 0), (0, 1, 1),
    (0, 0, 0), (0, 0, 1), (1, 0, 0), (1, 0, 1),
    (0, 0, 0), (0, 1, 0), (1, 0, 0), (1, 1, 0),
)
SLOT_EDGES = (0, 2, 4, 8, 9)


def slot_of(edge):
    direction = edge // 4
    upper = OFFSETS[edge][1]
    return (0 + upper, 2, 3 + upper)[direction]


def placement():
    table = np.zeros((1024, 768), np.float32)
    for offset in range(27):
        dx, dy, dz = offset // 9 - 1, offset // 3 % 3 - 1, offset % 3 - 1
        for edge in range(12):
            ox, oy, oz = OFFSETS[edge]
            direction = edge // 4
            if direction == 1:
                group, slot = {-1: (1, 2), 0: (0, 2), 1: (2, 2)}[dy + oy]
            else:
                base = 0 if direction == 0 else 3
                group, slot = {-1: (1, base), 0: (0, base), 1: (0, base + 1), 2: (2, base + 1)}[dy + oy]
            for comp in range(3):
                row = 16 * group + 3 * slot + comp
                table[36 * offset + 3 * edge + comp, 192 * (dx + ox + 1) + 48 * (dz + oz + 1) + row] = 1.0
    return table


def shifted(block, axis, distance):
    count = lax.axis_size(axis)
    return lax.ppermute(block, axis, [((i - distance) % count, i) for i in range(count)])


def lanes(shape):
    return lax.broadcasted_iota(jnp.int32, shape, len(shape) - 1)


def split(value):
    high = value.astype(BF16)
    return high, (value - high.astype(F32)).astype(BF16)


def dot(a, b):
    return jnp.dot(a, b, preferred_element_type=F32)


def own_lanes(value):
    group = lanes((40, 128)) // 32
    total = jnp.where(group == 0, value[0:40], 0.0)
    for x in range(1, 4):
        total = total + jnp.where(group == x, value[40 * x : 40 * x + 40], 0.0)
    return total


def call(kernel, outs, scratch=(), flops=1_000_000, **options):
    return pl.pallas_call(
        kernel,
        out_shape=outs,
        scratch_shapes=list(scratch),
        cost_estimate=pl.CostEstimate(flops=flops, bytes_accessed=1_000_000, transcendentals=0),
        compiler_params=pltpu.CompilerParams(vmem_limit_bytes=40 * 1024 * 1024),
        **options,
    )


def shape(*dims, dtype=F32):
    return jax.ShapeDtypeStruct(dims, dtype)


def numer_kernel(disp_ref, weight_ref, sums_ref, moving_ref):
    ones = jnp.ones((128, 128), BF16)
    group = (lanes((4, 512)) % 128) // 32
    keep = group == lax.broadcasted_iota(jnp.int32, (4, 512), 0)
    for edge in range(12):
        for z in range(2):
            parts = [disp_ref[x, z, edge, c] for c in range(3) for x in range(4)]
            right = jnp.concatenate(parts + [ones], axis=0)
            left = weight_ref[edge, z]
            found = lax.dot_general(left, right, (((1,), (1,)), ((), ())), preferred_element_type=F32)
            row = jnp.sum(jnp.where(keep, found, 0.0), axis=0, keepdims=True)
            for c in range(4):
                piece = row[:, 128 * c : 128 * c + 128]
                sums_ref[z, 4 * edge + c : 4 * edge + c + 1, :] = piece
                if edge in (6, 7, 10, 11):
                    place = 4 * (6, 7, 10, 11).index(edge) + c
                    moving_ref[z, place : place + 1, :] = piece


def sum_x_kernel(sums_ref, moving_ref, left_ref, out_ref, up_ref):
    for z in range(2):
        last = lanes((16, 128)) >= 96
        below = pltpu.roll(jnp.where(last, left_ref[z], moving_ref[z]), 32, 1)
        out_ref[z, 0:16] = sums_ref[z, 0:16]
        out_ref[z, 16:24] = sums_ref[z, 16:24] + below[0:8]
        out_ref[z, 24:32] = sums_ref[z, 32:40] + below[8:16]
    up_ref[...] = out_ref[1, 0:24]


def sum_z_kernel(sums_ref, left_ref, lower_ref, upper_ref, middle_ref):
    for z in range(2):
        below = left_ref if z == 0 else sums_ref.at[0]
        lower_ref[z, 0:4] = sums_ref[z, 0:4] + below[4:8]
        lower_ref[z, 4:8] = sums_ref[z, 24:28]
        upper_ref[z, 0:4] = sums_ref[z, 8:12] + below[12:16]
        upper_ref[z, 4:8] = sums_ref[z, 28:32]
        middle_ref[z, 0:4] = sums_ref[z, 16:20] + below[20:24]
        middle_ref[z, 4:8] = sums_ref[z, 16:20]


def solve(block_high, block_low, rows_ref):
    high, low = split(rows_ref[...])
    found = dot(block_high, high) + dot(block_high, low) + dot(block_low, high)
    return own_lanes(found)


def first_kernel(lower_ref, upper_ref, middle_ref, below_ref, above_ref, bh_ref, bl_ref, out_ref, x_ref, rows, found):
    for z in range(2):
        rows[...] = jnp.zeros((48, 128), F32)
        out_ref[z] = jnp.zeros((32, 128), F32)
        x_ref[z] = jnp.zeros((16, 128), F32)
        node = lower_ref[z] + below_ref[z]
        top = upper_ref[z] + above_ref[z]
        middle = middle_ref[z]
        for slot, (source, at) in enumerate(((node, 0), (top, 0), (middle, 0), (node, 4), (top, 4))):
            average = source[at : at + 3] / source[at + 3 : at + 4]
            edge = SLOT_EDGES[slot]
            rows[3 * edge : 3 * edge + 3] = average
            out_ref[z, 16 + 3 * slot : 19 + 3 * slot] = average
        found[...] = solve(bh_ref[z, :, 0:48], bl_ref[z, :, 0:48], rows)
        for slot, edge in enumerate(SLOT_EDGES):
            value = found[3 * edge : 3 * edge + 3]
            out_ref[z, 3 * slot : 3 * slot + 3] = value
            x_ref[z, 3 * slot : 3 * slot + 3] = value


def prepare_kernel(matrix_ref, block_ref, place_ref, ah_ref, al_ref, bh_ref, bl_ref, packed, stacked):
    packed[7] = jnp.zeros((72, 128), F32)
    for offset in range(27):
        start, tile = 36 * offset % 128, 36 * offset // 128
        size = min(36, 128 - start)
        packed[tile, :, start : start + size] = matrix_ref[0, offset, :, 0:size]
        if size < 36:
            packed[tile + 1, :, 0 : 36 - size] = matrix_ref[0, offset, :, size:36]
    for z in range(2):
        high, low = split(jnp.concatenate([packed[k, pl.ds(z, 36, stride=2), :] for k in range(8)], axis=1))
        pad = jnp.zeros((4, 1024), BF16)
        stacked[40 * z : 40 * z + 40] = jnp.concatenate([high, pad], axis=0)
        stacked[80 + 40 * z : 120 + 40 * z] = jnp.concatenate([low, pad], axis=0)
    found = dot(stacked[...], place_ref[...]).astype(BF16)
    for z in range(2):
        ah_ref[z, 0] = found[40 * z : 40 * z + 40]
        al_ref[z, 0] = found[80 + 40 * z : 120 + 40 * z]
    packed[0] = jnp.zeros((72, 128), F32)
    packed[0, :, 0:36] = block_ref[0]
    for z in range(2):
        high, low = split(packed[0, pl.ds(z, 36, stride=2), :])
        pad = jnp.zeros((4, 128), BF16)
        bh_ref[z, 0] = jnp.concatenate([high, pad], axis=0)
        bl_ref[z, 0] = jnp.concatenate([low, pad], axis=0)


def prepare(matrix, block):
    table = jnp.asarray(placement(), BF16)
    outs = (shape(2, 4, 40, 768, dtype=BF16),) * 2 + (shape(2, 4, 40, 128, dtype=BF16),) * 2
    wide = pl.BlockSpec((2, 1, 40, 768), lambda i: (0, i, 0, 0))
    slim = pl.BlockSpec((2, 1, 40, 128), lambda i: (0, i, 0, 0))
    ah, al, bh, bl = call(
        prepare_kernel,
        outs,
        (pltpu.VMEM((8, 72, 128), F32), pltpu.VMEM((160, 1024), BF16)),
        flops=20_000_000,
        grid=(4,),
        in_specs=[
            pl.BlockSpec((1, 27, 72, 36), lambda i: (i, 0, 0, 0)),
            pl.BlockSpec((1, 72, 36), lambda i: (i, 0, 0)),
            pl.BlockSpec((1024, 768), lambda i: (0, 0)),
        ],
        out_specs=(wide, wide, slim, slim),
    )(matrix, block, table)
    return (
        ah.reshape(2, 160, 768), al.reshape(2, 160, 768),
        bh.reshape(2, 160, 128), bl.reshape(2, 160, 128),
    )


def views(near, far):
    lane = lanes(near.shape)
    return (
        pltpu.roll(jnp.where(lane >= 96, far, near), 32, 1),
        near,
        pltpu.roll(jnp.where(lane < 32, far, near), 96, 1),
        pltpu.roll(jnp.where(lane < 64, far, near), 64, 1),
    )


def product(high, low, kh_ref, kl_ref, z):
    kept = jnp.concatenate([h[48 * z : 48 * z + 192] for h in high], axis=0)
    rest = jnp.concatenate([h[48 * z : 48 * z + 192] for h in low], axis=0)
    both = dot(kh_ref[z], jnp.concatenate([kept, rest], axis=1))
    return own_lanes(both[:, 0:128] + both[:, 128:256] + dot(kl_ref[z], kept))


def gathered(own_ref, left_ref, right_ref):
    near = jnp.concatenate(
        [left_ref[:, 0:128], own_ref[0, :, 0:128], own_ref[1, :, 0:128], right_ref[0:96, 0:128]], axis=0
    )
    far = jnp.concatenate(
        [left_ref[:, 128:256], own_ref[0, :, 128:256], own_ref[1, :, 128:256], right_ref[0:96, 128:256]], axis=0
    )
    return views(near, far)


def sweep_kernel(own_ref, left_ref, right_ref, g_ref, ah_ref, al_ref, bh_ref, bl_ref, x_ref, rows, found):
    pairs = [split(view) for view in gathered(own_ref, left_ref, right_ref)]
    high, low = [p[0] for p in pairs], [p[1] for p in pairs]
    for z in range(2):
        found[...] = product(high, low, ah_ref, al_ref, z)
        rows[...] = jnp.zeros((48, 128), F32)
        for slot, edge in enumerate(SLOT_EDGES):
            rows[3 * edge : 3 * edge + 3] = g_ref[z, 3 * slot : 3 * slot + 3, 0:128] - found[3 * edge : 3 * edge + 3]
        found[...] = solve(bh_ref[z, :, 0:48], bl_ref[z, :, 0:48], rows)
        x_ref[z] = jnp.zeros((16, 128), F32)
        for slot, edge in enumerate(SLOT_EDGES):
            x_ref[z, 3 * slot : 3 * slot + 3] = (
                own_ref[z, 3 * slot : 3 * slot + 3, 0:128] + found[3 * edge : 3 * edge + 3]
            )


def average_kernel(g_ref, right_ref, wide_ref, out_ref, ahead):
    for z in range(3):
        source = g_ref.at[z] if z < 2 else right_ref.at[96:112]
        ahead[z, 0:16] = source[:, 0:128]
        ahead[z, 16:32] = views(source[:, 0:128], source[:, 128:256])[2]
    for z in range(2):
        wide_ref[z] = jnp.zeros((48, 128), F32)
        for edge in range(12):
            ox, _, oz = OFFSETS[edge]
            start = 16 * ox + 3 * slot_of(edge)
            value = ahead[z + oz, start : start + 3]
            wide_ref[z, 3 * edge : 3 * edge + 3] = value
        write(out_ref, z, wide_ref[z, 0:36])


def write(out_ref, z, value):
    for x in range(4):
        out_ref[x, z] = value[:, 32 * x : 32 * x + 32]


def last_kernel(own_ref, left_ref, right_ref, wide_ref, ah_ref, al_ref, bh_ref, bl_ref, out_ref, rows, ahead, state):
    seen = gathered(own_ref, left_ref, right_ref)
    pairs = [split(view) for view in seen]
    high, low = [p[0] for p in pairs], [p[1] for p in pairs]
    for z in range(3):
        ahead[z, 0:16] = seen[1][48 * z + 48 : 48 * z + 64]
        ahead[z, 16:32] = seen[2][48 * z + 48 : 48 * z + 64]
    for z in range(2):
        for edge in range(12):
            ox, _, oz = OFFSETS[edge]
            start = 16 * ox + 3 * slot_of(edge)
            state[3 * edge : 3 * edge + 3] = ahead[z + oz, start : start + 3]
        rows[...] = jnp.zeros((48, 128), F32)
        rows[0:36] = wide_ref[z, 0:36] - product(high, low, ah_ref, al_ref, z)[0:36]
        write(out_ref, z, state[0:36] + solve(bh_ref[z, :, 0:48], bl_ref[z, :, 0:48], rows)[0:36])


def body(displacement, dof_weight, coarse_matrix, block_inverse):
    lane = lanes((2, 16, 128))
    weights = jnp.transpose(dof_weight[:, 0], (2, 1, 0, 3))
    sums, moving = call(numer_kernel, (shape(2, 48, 128), shape(2, 16, 128)), flops=20_000_000)(
        displacement[:, 0], weights
    )
    matrix = jnp.transpose(coarse_matrix[:, 0], (0, 2, 3, 1, 4)).reshape(4, 27, 72, 36)
    block = jnp.transpose(block_inverse[:, 0], (0, 2, 1, 3)).reshape(4, 72, 36)
    ah, al, bh, bl = prepare(matrix, block)
    left = shifted(moving, "gx", 1)
    sums, up = call(sum_x_kernel, (shape(2, 32, 128), shape(24, 128)))(sums, moving, left)
    left = shifted(up, "gz", 1)
    lower, upper, middle = call(sum_z_kernel, (shape(2, 8, 128),) * 3)(sums, left)
    below, above = shifted(upper, "gy", 1), shifted(lower, "gy", -1)
    both, x = call(
        first_kernel,
        (shape(2, 32, 128), shape(2, 16, 128)),
        (pltpu.VMEM((48, 128), F32), pltpu.VMEM((40, 128), F32)),
    )(lower, upper, middle, below, above, bh, bl)
    average = None
    for sweep in range(3):
        left = shifted(x, "gx", 1)
        right = shifted(both if sweep == 0 else x, "gx", -1)
        x = jnp.concatenate([x, jnp.where(lane < 64, right[:, 0:16], left)], axis=2)
        if sweep == 0:
            g = jnp.concatenate([both[:, 16:32], right[:, 16:32]], axis=2)
        below, above = shifted(x, "gy", 1), shifted(x, "gy", -1)
        own = jnp.concatenate([x, below, above], axis=1)
        left = shifted(own[1], "gz", 1)
        moving = own.reshape(96, 256)
        if sweep == 0:
            moving = jnp.concatenate([moving, g[0]], axis=0)
        right = shifted(moving, "gz", -1)
        if sweep == 0:
            wide, average = call(
                average_kernel, (shape(2, 48, 128), shape(4, 2, 36, 32)), (pltpu.VMEM((3, 32, 128), F32),)
            )(g, right)
        small = (pltpu.VMEM((48, 128), F32), pltpu.VMEM((40, 128), F32))
        if sweep < 2:
            x = call(sweep_kernel, shape(2, 16, 128), small, flops=10_000_000)(
                own, left, right, g, ah, al, bh, bl
            )
        else:
            x = call(
                last_kernel,
                shape(4, 2, 36, 32),
                (pltpu.VMEM((48, 128), F32), pltpu.VMEM((3, 32, 128), F32), pltpu.VMEM((40, 128), F32)),
                flops=10_000_000,
            )(own, left, right, wide, ah, al, bh, bl)
    return average.reshape(4, 1, 2, 12, 3, 32), x.reshape(4, 1, 2, 36, 32)


def solution(mesh):
    placed = (
        P("gx", "gy", "gz", None, None, None, None),
        P("gx", "gy", "gz", None, None),
        P("gx", "gy", "gz", None, None, None),
        P("gx", "gy", "gz", None, None),
    )
    return jax.shard_map(
        body,
        mesh=mesh,
        in_specs=placed,
        out_specs=(P("gx", "gy", "gz", None, None, None), P("gx", "gy", "gz", None, None)),
        check_vma=False,
    )
```

time: 247 us -> 147 us (0.60)
  the two profiles are of different devices: /device:TPU:56 before, /device:TPU:6 now
where the time goes in v1:
time: 147 us; the launch traced here: 146 us
  starting transfers between devices  71.7 us (49%)
  waiting for transfers between devices  60.2 us (41%)
  Pallas kernels  7.32 us (5%)
  local copies, waits for them, and re-layouts  6.08 us (4%)
    ppermute x22, starting transfers between devices, shifted(): lax.ppermute(block, axis, [((i - distance) % count, i) for i in range(cou...  71.7 us
    ppermute x22, waiting for transfers between devices, shifted(): lax.ppermute(block, axis, [((i - distance) % count, i) for i in range(cou...  60.2 us
    unnamed x10, local copies, waits for them, and re-layouts  5.32 us
    pallas_call x1, Pallas kernels, prepare(): call(prepare_kernel, outs, (pltpu.VMEM((8, 72, 128), F32), pltpu.VMEM((16...  3.24 us
  transfers between devices with their start and end apart: 22, of which 12 were waited for; matrix products, arithmetic and copies ran while one was open for 1% of the time, Pallas kernels for 2%

profile of v1, /device:TPU:6, one launch (start us, length us, event | category | flops | bytes accessed | tf_op | source)
XLA Modules:
  0.0 146.4 jit_solution(9893635739413512096)
XLA Ops:
  4.0 7.7 %collective-permute-start = (f32[2,16,128]{2,1,0:T(8,128)S(1)}, f32[2,16,128]{2,1,0:T(8,128)S(1)}, u32[]{:S(2)}, u32[]{:S(2)}) collective-permute-start(f32[2,16,128]{2,1,0:T(8,128)S(1)} %get-tuple-element.18.moving_ref), channel_id=1, source_target_pairs={{384,0},{0,128},{128,256},{256,384},{385,1},{1,129},{129,257},{257... | collective-permute-start | bytes 49160 | tf_op jit(solution)/shard_map/ppermute | solution.py:47
  15.1 4.9 %collective-permute-done.1.left_ref = f32[24,128]{1,0:T(8,128)S(1)} collective-permute-done((f32[24,128]{1,0:T(8,128)S(1)}, f32[24,128]{1,0:T(8,128)S(1)}, u32[]{:S(2)}, u32[]{:S(2)}) %collective-permute-start.1) | collective-permute-done | bytes 12320 | tf_op jit(solution)/shard_map/ppermute | solution.py:47
  20.0 10.3 %collective-permute-start.3 = (f32[2,8,128]{2,1,0:T(8,128)S(1)}, f32[2,8,128]{2,1,0:T(8,128)S(1)}, u32[]{:S(2)}, u32[]{:S(2)}) collective-permute-start(f32[2,8,128]{2,1,0:T(8,128)S(1)} %get-tuple-element.21.lower_ref), channel_id=1, source_target_pairs={{8,0},{16,8},{24,16},{32,24},{40,32},{48,40},{56,48},{64,56},{72,6... | collective-permute-start | bytes 24584 | tf_op jit(solution)/shard_map/ppermute | solution.py:47
  30.3 1.9 %collective-permute-start.2 = (f32[2,8,128]{2,1,0:T(8,128)S(1)}, f32[2,8,128]{2,1,0:T(8,128)S(1)}, u32[]{:S(2)}, u32[]{:S(2)}) collective-permute-start(f32[2,8,128]{2,1,0:T(8,128)S(1)} %get-tuple-element.22.upper_ref), channel_id=1, source_target_pairs={{120,0},{0,8},{8,16},{16,24},{24,32},{32,40},{40,48},{48,56},{56,6... | collective-permute-start | bytes 24584 | tf_op jit(solution)/shard_map/ppermute | solution.py:47
  32.3 2.1 %copy-done = f32[4,1,2,27,36,36]{5,2,4,3,1,0:T(2,128)S(1)} copy-done((f32[4,1,2,27,36,36]{5,2,4,3,1,0:T(2,128)S(1)}, f32[4,1,2,27,36,36]{5,2,4,3,1,0:T(2,128)}, u32[]{:S(2)}) %copy-start) | copy-done | bytes 1119768
  34.4 3.2 %shard_map.71 = (bf16[2,4,40,768]{3,2,1,0:T(8,128)(2,1)S(1)}, bf16[2,4,40,768]{3,2,1,0:T(8,128)(2,1)S(1)}, bf16[2,4,40,128]{3,2,1,0:T(8,128)(2,1)S(1)}, bf16[2,4,40,128]{3,2,1,0:T(8,128)(2,1)S(1)}) custom-call(f32[4,27,72,36]{3,2,1,0:T(8,128)S(1)} %bitcast.41, f32[4,72,36]{2,1,0:T(8,128)S(1)} %bitcast.55, bf16[1024,768]{1,0:T(8,128)(2,1)S(1)} %copy-done.2), custom_call_target="tpu_custom_call" | custom-call | flops 20000000 | bytes 1000000 | tf_op jit(solution)/shard_map/pallas_call | solution.py:183
  37.7 4.2 %collective-permute-done.2.below_ref = f32[2,8,128]{2,1,0:T(8,128)S(1)} collective-permute-done((f32[2,8,128]{2,1,0:T(8,128)S(1)}, f32[2,8,128]{2,1,0:T(8,128)S(1)}, u32[]{:S(2)}, u32[]{:S(2)}) %collective-permute-start.2) | collective-permute-done | bytes 8224 | tf_op jit(solution)/shard_map/ppermute | solution.py:47
  42.1 3.6 %collective-permute-start.5 = (f32[2,16,128]{2,1,0:T(8,128)S(1)}, f32[2,16,128]{2,1,0:T(8,128)S(1)}, u32[]{:S(2)}, u32[]{:S(2)}) collective-permute-start(f32[2,16,128]{2,1,0:T(8,128)S(1)} %get-tuple-element.27), channel_id=1, source_target_pairs={{384,0},{0,128},{128,256},{256,384},{385,1},{1,129},{129,257},{257... | collective-permute-start | bytes 49160 | tf_op jit(solution)/shard_map/ppermute | solution.py:47
  45.7 2.2 %collective-permute-start.4 = (f32[2,32,128]{2,1,0:T(8,128)S(1)}, f32[2,32,128]{2,1,0:T(8,128)S(1)}, u32[]{:S(2)}, u32[]{:S(2)}) collective-permute-start(f32[2,32,128]{2,1,0:T(8,128)S(1)} %get-tuple-element.26), channel_id=1, source_target_pairs={{128,0},{256,128},{384,256},{0,384},{129,1},{257,129},{385,257},{1... | collective-permute-start | bytes 98312 | tf_op jit(solution)/shard_map/ppermute | solution.py:47
  48.0 4.7 %collective-permute-done.4 = f32[2,32,128]{2,1,0:T(8,128)S(1)} collective-permute-done((f32[2,32,128]{2,1,0:T(8,128)S(1)}, f32[2,32,128]{2,1,0:T(8,128)S(1)}, u32[]{:S(2)}, u32[]{:S(2)}) %collective-permute-start.4) | collective-permute-done | bytes 32800 | tf_op jit(solution)/shard_map/ppermute | solution.py:47
  52.8 5.7 %collective-permute-start.7 = (f32[2,16,256]{2,1,0:T(8,128)S(1)}, f32[2,16,256]{2,1,0:T(8,128)S(1)}, u32[]{:S(2)}, u32[]{:S(2)}) collective-permute-start(f32[2,16,256]{2,1,0:T(8,128)S(1)} %pad_maximum_fusion.5), channel_id=1, source_target_pairs={{8,0},{16,8},{24,16},{32,24},{40,32},{48,40},{56,48},{64,56},{72,6... | collective-permute-start | bytes 98312 | tf_op jit(solution)/shard_map/ppermute | solution.py:47
  58.5 1.9 %collective-permute-start.6 = (f32[2,16,256]{2,1,0:T(8,128)S(1)}, f32[2,16,256]{2,1,0:T(8,128)S(1)}, u32[]{:S(2)}, u32[]{:S(2)}) collective-permute-start(f32[2,16,256]{2,1,0:T(8,128)S(1)} %pad_maximum_fusion.5), channel_id=1, source_target_pairs={{120,0},{0,8},{8,16},{16,24},{24,32},{32,40},{40,48},{48,56},{56,6... | collective-permute-start | bytes 98312 | tf_op jit(solution)/shard_map/ppermute | solution.py:47
  60.4 9.9 %collective-permute-done.6 = f32[2,16,256]{2,1,0:T(8,128)S(1)} collective-permute-done((f32[2,16,256]{2,1,0:T(8,128)S(1)}, f32[2,16,256]{2,1,0:T(8,128)S(1)}, u32[]{:S(2)}, u32[]{:S(2)}) %collective-permute-start.6) | collective-permute-done | bytes 32800 | tf_op jit(solution)/shard_map/ppermute | solution.py:47
  70.4 1.9 %collective-permute-start.8 = (f32[112,256]{1,0:T(8,128)S(1)}, f32[112,256]{1,0:T(8,128)S(1)}, u32[]{:S(2)}, u32[]{:S(2)}) collective-permute-start(f32[112,256]{1,0:T(8,128)S(1)} %pad_maximum_fusion), channel_id=1, source_target_pairs={{1,0},{2,1},{3,2},{4,3},{5,4},{6,5},{7,6},{0,7},{9,8},{10,9},{11,1... | collective-permute-start | bytes 344072 | tf_op jit(solution)/shard_map/ppermute | solution.py:47
  72.3 2.4 %collective-permute-start.9 = (f32[48,256]{1,0:T(8,128)S(1)}, f32[48,256]{1,0:T(8,128)S(1)}, u32[]{:S(2)}, u32[]{:S(2)}) collective-permute-start(f32[48,256]{1,0:T(8,128)S(1)} %slice_bitcast_fusion.2), channel_id=1, source_target_pairs={{7,0},{0,1},{1,2},{2,3},{3,4},{4,5},{5,6},{6,7},{15,8},{8,9},{9,10... | collective-permute-start | bytes 147464 | tf_op jit(solution)/shard_map/ppermute | solution.py:47
  74.7 4.8 %collective-permute-done.9.left_ref = f32[48,256]{1,0:T(8,128)S(1)} collective-permute-done((f32[48,256]{1,0:T(8,128)S(1)}, f32[48,256]{1,0:T(8,128)S(1)}, u32[]{:S(2)}, u32[]{:S(2)}) %collective-permute-start.9) | collective-permute-done | bytes 49184 | tf_op jit(solution)/shard_map/ppermute | solution.py:47
  82.3 3.9 %collective-permute-start.10 = (f32[2,16,128]{2,1,0:T(8,128)S(1)}, f32[2,16,128]{2,1,0:T(8,128)S(1)}, u32[]{:S(2)}, u32[]{:S(2)}) collective-permute-start(f32[2,16,128]{2,1,0:T(8,128)S(1)} %shard_map.74), channel_id=1, source_target_pairs={{128,0},{256,128},{384,256},{0,384},{129,1},{257,129},{385,257},{1... | collective-permute-start | bytes 49160 | tf_op jit(solution)/shard_map/ppermute | solution.py:47
  86.2 2.9 %collective-permute-done.10 = f32[2,16,128]{2,1,0:T(8,128)S(1)} collective-permute-done((f32[2,16,128]{2,1,0:T(8,128)S(1)}, f32[2,16,128]{2,1,0:T(8,128)S(1)}, u32[]{:S(2)}, u32[]{:S(2)}) %collective-permute-start.10) | collective-permute-done | bytes 16416 | tf_op jit(solution)/shard_map/ppermute | solution.py:47
  91.1 3.9 %collective-permute-start.12 = (f32[2,16,256]{2,1,0:T(8,128)S(1)}, f32[2,16,256]{2,1,0:T(8,128)S(1)}, u32[]{:S(2)}, u32[]{:S(2)}) collective-permute-start(f32[2,16,256]{2,1,0:T(8,128)S(1)} %pad_maximum_fusion.6), channel_id=1, source_target_pairs={{120,0},{0,8},{8,16},{16,24},{24,32},{32,40},{40,48},{48,56},{56,6... | collective-permute-start | bytes 98312 | tf_op jit(solution)/shard_map/ppermute | solution.py:47
  95.0 7.9 %collective-permute-done.12 = f32[2,16,256]{2,1,0:T(8,128)S(1)} collective-permute-done((f32[2,16,256]{2,1,0:T(8,128)S(1)}, f32[2,16,256]{2,1,0:T(8,128)S(1)}, u32[]{:S(2)}, u32[]{:S(2)}) %collective-permute-start.12) | collective-permute-done | bytes 32800 | tf_op jit(solution)/shard_map/ppermute | solution.py:47
  102.9 1.9 %collective-permute-start.15 = (f32[96,256]{1,0:T(8,128)S(1)}, f32[96,256]{1,0:T(8,128)S(1)}, u32[]{:S(2)}, u32[]{:S(2)}) collective-permute-start(f32[96,256]{1,0:T(8,128)S(1)} %bitcast.54), channel_id=1, source_target_pairs={{1,0},{2,1},{3,2},{4,3},{5,4},{6,5},{7,6},{0,7},{9,8},{10,9},{11,1... | collective-permute-start | bytes 294920 | tf_op jit(solution)/shard_map/ppermute | solution.py:47
  104.9 2.4 %collective-permute-start.14 = (f32[48,256]{1,0:T(8,128)S(1)}, f32[48,256]{1,0:T(8,128)S(1)}, u32[]{:S(2)}, u32[]{:S(2)}) collective-permute-start(f32[48,256]{1,0:T(8,128)S(1)} %slice_bitcast_fusion.1), channel_id=1, source_target_pairs={{7,0},{0,1},{1,2},{2,3},{3,4},{4,5},{5,6},{6,7},{15,8},{8,9},{9,10... | collective-permute-start | bytes 147464 | tf_op jit(solution)/shard_map/ppermute | solution.py:47
  107.3 4.8 %collective-permute-done.14.left_ref = f32[48,256]{1,0:T(8,128)S(1)} collective-permute-done((f32[48,256]{1,0:T(8,128)S(1)}, f32[48,256]{1,0:T(8,128)S(1)}, u32[]{:S(2)}, u32[]{:S(2)}) %collective-permute-start.14) | collective-permute-done | bytes 49184 | tf_op jit(solution)/shard_map/ppermute | solution.py:47
  113.0 1.9 %collective-permute-start.17 = (f32[2,16,128]{2,1,0:T(8,128)S(1)}, f32[2,16,128]{2,1,0:T(8,128)S(1)}, u32[]{:S(2)}, u32[]{:S(2)}) collective-permute-start(f32[2,16,128]{2,1,0:T(8,128)S(1)} %shard_map.75), channel_id=1, source_target_pairs={{384,0},{0,128},{128,256},{256,384},{385,1},{1,129},{129,257},{257... | collective-permute-start | bytes 49160 | tf_op jit(solution)/shard_map/ppermute | solution.py:47
  114.9 3.9 %collective-permute-start.16 = (f32[2,16,128]{2,1,0:T(8,128)S(1)}, f32[2,16,128]{2,1,0:T(8,128)S(1)}, u32[]{:S(2)}, u32[]{:S(2)}) collective-permute-start(f32[2,16,128]{2,1,0:T(8,128)S(1)} %shard_map.75), channel_id=1, source_target_pairs={{128,0},{256,128},{384,256},{0,384},{129,1},{257,129},{385,257},{1... | collective-permute-start | bytes 49160 | tf_op jit(solution)/shard_map/ppermute | solution.py:47
  118.8 2.9 %collective-permute-done.16 = f32[2,16,128]{2,1,0:T(8,128)S(1)} collective-permute-done((f32[2,16,128]{2,1,0:T(8,128)S(1)}, f32[2,16,128]{2,1,0:T(8,128)S(1)}, u32[]{:S(2)}, u32[]{:S(2)}) %collective-permute-start.16) | collective-permute-done | bytes 16416 | tf_op jit(solution)/shard_map/ppermute | solution.py:47
  121.7 1.9 %collective-permute-start.19 = (f32[2,16,256]{2,1,0:T(8,128)S(1)}, f32[2,16,256]{2,1,0:T(8,128)S(1)}, u32[]{:S(2)}, u32[]{:S(2)}) collective-permute-start(f32[2,16,256]{2,1,0:T(8,128)S(1)} %pad_maximum_fusion.7), channel_id=1, source_target_pairs={{8,0},{16,8},{24,16},{32,24},{40,32},{48,40},{56,48},{64,56},{72,6... | collective-permute-start | bytes 98312 | tf_op jit(solution)/shard_map/ppermute | solution.py:47
  123.7 3.9 %collective-permute-start.18 = (f32[2,16,256]{2,1,0:T(8,128)S(1)}, f32[2,16,256]{2,1,0:T(8,128)S(1)}, u32[]{:S(2)}, u32[]{:S(2)}) collective-permute-start(f32[2,16,256]{2,1,0:T(8,128)S(1)} %pad_maximum_fusion.7), channel_id=1, source_target_pairs={{120,0},{0,8},{8,16},{16,24},{24,32},{32,40},{40,48},{48,56},{56,6... | collective-permute-start | bytes 98312 | tf_op jit(solution)/shard_map/ppermute | solution.py:47
  127.6 7.9 %collective-permute-done.18 = f32[2,16,256]{2,1,0:T(8,128)S(1)} collective-permute-done((f32[2,16,256]{2,1,0:T(8,128)S(1)}, f32[2,16,256]{2,1,0:T(8,128)S(1)}, u32[]{:S(2)}, u32[]{:S(2)}) %collective-permute-start.18) | collective-permute-done | bytes 32800 | tf_op jit(solution)/shard_map/ppermute | solution.py:47
  135.5 1.9 %collective-permute-start.21 = (f32[96,256]{1,0:T(8,128)S(1)}, f32[96,256]{1,0:T(8,128)S(1)}, u32[]{:S(2)}, u32[]{:S(2)}) collective-permute-start(f32[96,256]{1,0:T(8,128)S(1)} %bitcast.53), channel_id=1, source_target_pairs={{1,0},{2,1},{3,2},{4,3},{5,4},{6,5},{7,6},{0,7},{9,8},{10,9},{11,1... | collective-permute-start | bytes 294920 | tf_op jit(solution)/shard_map/ppermute | solution.py:47
  137.4 2.4 %collective-permute-start.20 = (f32[48,256]{1,0:T(8,128)S(1)}, f32[48,256]{1,0:T(8,128)S(1)}, u32[]{:S(2)}, u32[]{:S(2)}) collective-permute-start(f32[48,256]{1,0:T(8,128)S(1)} %slice_bitcast_fusion), channel_id=1, source_target_pairs={{7,0},{0,1},{1,2},{2,3},{3,4},{4,5},{5,6},{6,7},{15,8},{8,9},{9,10... | collective-permute-start | bytes 147464 | tf_op jit(solution)/shard_map/ppermute | solution.py:47
  140.8 3.9 %collective-permute-done.20.left_ref = f32[48,256]{1,0:T(8,128)S(1)} collective-permute-done((f32[48,256]{1,0:T(8,128)S(1)}, f32[48,256]{1,0:T(8,128)S(1)}, u32[]{:S(2)}, u32[]{:S(2)}) %collective-permute-start.20) | collective-permute-done | bytes 49184 | tf_op jit(solution)/shard_map/ppermute | solution.py:47
  (49 shorter events, 15.3 us)
Async XLA Ops:
  1.4 1.7 %copy-start.1 = (bf16[4,1,2,12,3,32,128]{6,5,4,3,2,1,0:T(8,128)(2,1)S(1)}, bf16[4,1,2,12,3,32,128]{6,5,4,3,2,1,0:T(8,128)(2,1)}, u32[]{:S(2)}) copy-start(bf16[4,1,2,12,3,32,128]{6,5,4,3,2,1,0:T(8,128)(2,1)} %param.5) | copy-start | bytes 7077892
  3.0 29.2 %copy-start.2 = (bf16[1024,768]{1,0:T(8,128)(2,1)S(1)}, bf16[1024,768]{1,0:T(8,128)(2,1)}, u32[]{:S(2)}) copy-start(bf16[1024,768]{1,0:T(8,128)(2,1)} %constant.4.clone.place_ref) | copy-start | bytes 4718596
  3.1 29.2 %copy-start.3 = (f32[4,1,2,36,36]{4,2,3,1,0:T(2,128)S(1)}, f32[4,1,2,36,36]{4,2,3,1,0:T(2,128)}, u32[]{:S(2)}) copy-start(f32[4,1,2,36,36]{4,2,3,1,0:T(2,128)} %param.8) | copy-start | bytes 124420
  4.0 9.2 %collective-permute-start = (f32[2,16,128]{2,1,0:T(8,128)S(1)}, f32[2,16,128]{2,1,0:T(8,128)S(1)}, u32[]{:S(2)}, u32[]{:S(2)}) collective-permute-start(f32[2,16,128]{2,1,0:T(8,128)S(1)} %get-tuple-element.18.moving_ref), channel_id=1, source_target_pairs={{384,0},{0,128},{128,256},{256,384},{385,1},{1,129},{129,257},{257... | collective-permute-start | bytes 49160 | tf_op jit(solution)/shard_map/ppermute | solution.py:47
  13.2 6.8 %collective-permute-start.1 = (f32[24,128]{1,0:T(8,128)S(1)}, f32[24,128]{1,0:T(8,128)S(1)}, u32[]{:S(2)}, u32[]{:S(2)}) collective-permute-start(f32[24,128]{1,0:T(8,128)S(1)} %get-tuple-element.20), channel_id=1, source_target_pairs={{7,0},{0,1},{1,2},{2,3},{3,4},{4,5},{5,6},{6,7},{15,8},{8,9},{9,10... | collective-permute-start | bytes 36872 | tf_op jit(solution)/shard_map/ppermute | solution.py:47
  20.0 17.6 %collective-permute-start.3 = (f32[2,8,128]{2,1,0:T(8,128)S(1)}, f32[2,8,128]{2,1,0:T(8,128)S(1)}, u32[]{:S(2)}, u32[]{:S(2)}) collective-permute-start(f32[2,8,128]{2,1,0:T(8,128)S(1)} %get-tuple-element.21.lower_ref), channel_id=1, source_target_pairs={{8,0},{16,8},{24,16},{32,24},{40,32},{48,40},{56,48},{64,56},{72,6... | collective-permute-start | bytes 24584 | tf_op jit(solution)/shard_map/ppermute | solution.py:47
  30.3 11.6 %collective-permute-start.2 = (f32[2,8,128]{2,1,0:T(8,128)S(1)}, f32[2,8,128]{2,1,0:T(8,128)S(1)}, u32[]{:S(2)}, u32[]{:S(2)}) collective-permute-start(f32[2,8,128]{2,1,0:T(8,128)S(1)} %get-tuple-element.22.upper_ref), channel_id=1, source_target_pairs={{120,0},{0,8},{8,16},{16,24},{24,32},{32,40},{40,48},{48,56},{56,6... | collective-permute-start | bytes 24584 | tf_op jit(solution)/shard_map/ppermute | solution.py:47
  32.3 2.1 %copy-start = (f32[4,1,2,27,36,36]{5,2,4,3,1,0:T(2,128)S(1)}, f32[4,1,2,27,36,36]{5,2,4,3,1,0:T(2,128)}, u32[]{:S(2)}) copy-start(f32[4,1,2,27,36,36]{5,2,4,3,1,0:T(2,128)} %param.7) | copy-start | bytes 3359236
  42.1 5.9 %collective-permute-start.5 = (f32[2,16,128]{2,1,0:T(8,128)S(1)}, f32[2,16,128]{2,1,0:T(8,128)S(1)}, u32[]{:S(2)}, u32[]{:S(2)}) collective-permute-start(f32[2,16,128]{2,1,0:T(8,128)S(1)} %get-tuple-element.27), channel_id=1, source_target_pairs={{384,0},{0,128},{128,256},{256,384},{385,1},{1,129},{129,257},{257... | collective-permute-start | bytes 49160 | tf_op jit(solution)/shard_map/ppermute | solution.py:47
  45.7 7.0 %collective-permute-start.4 = (f32[2,32,128]{2,1,0:T(8,128)S(1)}, f32[2,32,128]{2,1,0:T(8,128)S(1)}, u32[]{:S(2)}, u32[]{:S(2)}) collective-permute-start(f32[2,32,128]{2,1,0:T(8,128)S(1)} %get-tuple-element.26), channel_id=1, source_target_pairs={{128,0},{256,128},{384,256},{0,384},{129,1},{257,129},{385,257},{1... | collective-permute-start | bytes 98312 | tf_op jit(solution)/shard_map/ppermute | solution.py:47
  52.8 7.7 %collective-permute-start.7 = (f32[2,16,256]{2,1,0:T(8,128)S(1)}, f32[2,16,256]{2,1,0:T(8,128)S(1)}, u32[]{:S(2)}, u32[]{:S(2)}) collective-permute-start(f32[2,16,256]{2,1,0:T(8,128)S(1)} %pad_maximum_fusion.5), channel_id=1, source_target_pairs={{8,0},{16,8},{24,16},{32,24},{40,32},{48,40},{56,48},{64,56},{72,6... | collective-permute-start | bytes 98312 | tf_op jit(solution)/shard_map/ppermute | solution.py:47
  58.5 11.8 %collective-permute-start.6 = (f32[2,16,256]{2,1,0:T(8,128)S(1)}, f32[2,16,256]{2,1,0:T(8,128)S(1)}, u32[]{:S(2)}, u32[]{:S(2)}) collective-permute-start(f32[2,16,256]{2,1,0:T(8,128)S(1)} %pad_maximum_fusion.5), channel_id=1, source_target_pairs={{120,0},{0,8},{8,16},{16,24},{24,32},{32,40},{40,48},{48,56},{56,6... | collective-permute-start | bytes 98312 | tf_op jit(solution)/shard_map/ppermute | solution.py:47
  70.4 9.2 %collective-permute-start.8 = (f32[112,256]{1,0:T(8,128)S(1)}, f32[112,256]{1,0:T(8,128)S(1)}, u32[]{:S(2)}, u32[]{:S(2)}) collective-permute-start(f32[112,256]{1,0:T(8,128)S(1)} %pad_maximum_fusion), channel_id=1, source_target_pairs={{1,0},{2,1},{3,2},{4,3},{5,4},{6,5},{7,6},{0,7},{9,8},{10,9},{11,1... | collective-permute-start | bytes 344072 | tf_op jit(solution)/shard_map/ppermute | solution.py:47
  72.3 7.2 %collective-permute-start.9 = (f32[48,256]{1,0:T(8,128)S(1)}, f32[48,256]{1,0:T(8,128)S(1)}, u32[]{:S(2)}, u32[]{:S(2)}) collective-permute-start(f32[48,256]{1,0:T(8,128)S(1)} %slice_bitcast_fusion.2), channel_id=1, source_target_pairs={{7,0},{0,1},{1,2},{2,3},{3,4},{4,5},{5,6},{6,7},{15,8},{8,9},{9,10... | collective-permute-start | bytes 147464 | tf_op jit(solution)/shard_map/ppermute | solution.py:47
  80.4 5.9 %collective-permute-start.11 = (f32[2,16,128]{2,1,0:T(8,128)S(1)}, f32[2,16,128]{2,1,0:T(8,128)S(1)}, u32[]{:S(2)}, u32[]{:S(2)}) collective-permute-start(f32[2,16,128]{2,1,0:T(8,128)S(1)} %shard_map.74), channel_id=1, source_target_pairs={{384,0},{0,128},{128,256},{256,384},{385,1},{1,129},{129,257},{257... | collective-permute-start | bytes 49160 | tf_op jit(solution)/shard_map/ppermute | solution.py:47
  82.3 6.8 %collective-permute-start.10 = (f32[2,16,128]{2,1,0:T(8,128)S(1)}, f32[2,16,128]{2,1,0:T(8,128)S(1)}, u32[]{:S(2)}, u32[]{:S(2)}) collective-permute-start(f32[2,16,128]{2,1,0:T(8,128)S(1)} %shard_map.74), channel_id=1, source_target_pairs={{128,0},{256,128},{384,256},{0,384},{129,1},{257,129},{385,257},{1... | collective-permute-start | bytes 49160 | tf_op jit(solution)/shard_map/ppermute | solution.py:47
  89.2 5.9 %collective-permute-start.13 = (f32[2,16,256]{2,1,0:T(8,128)S(1)}, f32[2,16,256]{2,1,0:T(8,128)S(1)}, u32[]{:S(2)}, u32[]{:S(2)}) collective-permute-start(f32[2,16,256]{2,1,0:T(8,128)S(1)} %pad_maximum_fusion.6), channel_id=1, source_target_pairs={{8,0},{16,8},{24,16},{32,24},{40,32},{48,40},{56,48},{64,56},{72,6... | collective-permute-start | bytes 98312 | tf_op jit(solution)/shard_map/ppermute | solution.py:47
  91.1 11.8 %collective-permute-start.12 = (f32[2,16,256]{2,1,0:T(8,128)S(1)}, f32[2,16,256]{2,1,0:T(8,128)S(1)}, u32[]{:S(2)}, u32[]{:S(2)}) collective-permute-start(f32[2,16,256]{2,1,0:T(8,128)S(1)} %pad_maximum_fusion.6), channel_id=1, source_target_pairs={{120,0},{0,8},{8,16},{16,24},{24,32},{32,40},{40,48},{48,56},{56,6... | collective-permute-start | bytes 98312 | tf_op jit(solution)/shard_map/ppermute | solution.py:47
  102.9 9.2 %collective-permute-start.15 = (f32[96,256]{1,0:T(8,128)S(1)}, f32[96,256]{1,0:T(8,128)S(1)}, u32[]{:S(2)}, u32[]{:S(2)}) collective-permute-start(f32[96,256]{1,0:T(8,128)S(1)} %bitcast.54), channel_id=1, source_target_pairs={{1,0},{2,1},{3,2},{4,3},{5,4},{6,5},{7,6},{0,7},{9,8},{10,9},{11,1... | collective-permute-start | bytes 294920 | tf_op jit(solution)/shard_map/ppermute | solution.py:47
  104.9 7.2 %collective-permute-start.14 = (f32[48,256]{1,0:T(8,128)S(1)}, f32[48,256]{1,0:T(8,128)S(1)}, u32[]{:S(2)}, u32[]{:S(2)}) collective-permute-start(f32[48,256]{1,0:T(8,128)S(1)} %slice_bitcast_fusion.1), channel_id=1, source_target_pairs={{7,0},{0,1},{1,2},{2,3},{3,4},{4,5},{5,6},{6,7},{15,8},{8,9},{9,10... | collective-permute-start | bytes 147464 | tf_op jit(solution)/shard_map/ppermute | solution.py:47
  113.0 5.9 %collective-permute-start.17 = (f32[2,16,128]{2,1,0:T(8,128)S(1)}, f32[2,16,128]{2,1,0:T(8,128)S(1)}, u32[]{:S(2)}, u32[]{:S(2)}) collective-permute-start(f32[2,16,128]{2,1,0:T(8,128)S(1)} %shard_map.75), channel_id=1, source_target_pairs={{384,0},{0,128},{128,256},{256,384},{385,1},{1,129},{129,257},{257... | collective-permute-start | bytes 49160 | tf_op jit(solution)/shard_map/ppermute | solution.py:47
  114.9 6.8 %collective-permute-start.16 = (f32[2,16,128]{2,1,0:T(8,128)S(1)}, f32[2,16,128]{2,1,0:T(8,128)S(1)}, u32[]{:S(2)}, u32[]{:S(2)}) collective-permute-start(f32[2,16,128]{2,1,0:T(8,128)S(1)} %shard_map.75), channel_id=1, source_target_pairs={{128,0},{256,128},{384,256},{0,384},{129,1},{257,129},{385,257},{1... | collective-permute-start | bytes 49160 | tf_op jit(solution)/shard_map/ppermute | solution.py:47
  121.7 5.9 %collective-permute-start.19 = (f32[2,16,256]{2,1,0:T(8,128)S(1)}, f32[2,16,256]{2,1,0:T(8,128)S(1)}, u32[]{:S(2)}, u32[]{:S(2)}) collective-permute-start(f32[2,16,256]{2,1,0:T(8,128)S(1)} %pad_maximum_fusion.7), channel_id=1, source_target_pairs={{8,0},{16,8},{24,16},{32,24},{40,32},{48,40},{56,48},{64,56},{72,6... | collective-permute-start | bytes 98312 | tf_op jit(solution)/shard_map/ppermute | solution.py:47
  123.7 11.8 %collective-permute-start.18 = (f32[2,16,256]{2,1,0:T(8,128)S(1)}, f32[2,16,256]{2,1,0:T(8,128)S(1)}, u32[]{:S(2)}, u32[]{:S(2)}) collective-permute-start(f32[2,16,256]{2,1,0:T(8,128)S(1)} %pad_maximum_fusion.7), channel_id=1, source_target_pairs={{120,0},{0,8},{8,16},{16,24},{24,32},{32,40},{40,48},{48,56},{56,6... | collective-permute-start | bytes 98312 | tf_op jit(solution)/shard_map/ppermute | solution.py:47
  135.5 9.2 %collective-permute-start.21 = (f32[96,256]{1,0:T(8,128)S(1)}, f32[96,256]{1,0:T(8,128)S(1)}, u32[]{:S(2)}, u32[]{:S(2)}) collective-permute-start(f32[96,256]{1,0:T(8,128)S(1)} %bitcast.53), channel_id=1, source_target_pairs={{1,0},{2,1},{3,2},{4,3},{5,4},{6,5},{7,6},{0,7},{9,8},{10,9},{11,1... | collective-permute-start | bytes 294920 | tf_op jit(solution)/shard_map/ppermute | solution.py:47
  137.4 7.2 %collective-permute-start.20 = (f32[48,256]{1,0:T(8,128)S(1)}, f32[48,256]{1,0:T(8,128)S(1)}, u32[]{:S(2)}, u32[]{:S(2)}) collective-permute-start(f32[48,256]{1,0:T(8,128)S(1)} %slice_bitcast_fusion), channel_id=1, source_target_pairs={{7,0},{0,1},{1,2},{2,3},{3,4},{4,5},{5,6},{6,7},{15,8},{8,9},{9,10... | collective-permute-start | bytes 147464 | tf_op jit(solution)/shard_map/ppermute | solution.py:47

commit v2 on v1

--- a/solution.py
+++ b/solution.py
@@ -16,6 +16,7 @@
     (0, 0, 0), (0, 1, 0), (1, 0, 0), (1, 1, 0),
 )
 SLOT_EDGES = (0, 2, 4, 8, 9)
+WIDE_EDGES = (0, 2, 4, 8, 9, 6, 10, 11)
 
 
 def slot_of(edge):
@@ -42,6 +43,14 @@
     return table
 
 
+def choice():
+    table = np.zeros((128, 128), np.float32)
+    for place, edge in enumerate(WIDE_EDGES):
+        for comp in range(3):
+            table[3 * edge + comp, 3 * place + comp] = 1.0
+    return table
+
+
 def shifted(block, axis, distance):
     count = lax.axis_size(axis)
     return lax.ppermute(block, axis, [((i - distance) % count, i) for i in range(count)])
@@ -83,7 +92,7 @@
     return jax.ShapeDtypeStruct(dims, dtype)
 
 
-def numer_kernel(disp_ref, weight_ref, sums_ref, moving_ref):
+def numer_kernel(disp_ref, weight_ref, sums_ref):
     ones = jnp.ones((128, 128), BF16)
     group = (lanes((4, 512)) % 128) // 32
     keep = group == lax.broadcasted_iota(jnp.int32, (4, 512), 0)
@@ -95,20 +104,16 @@
             found = lax.dot_general(left, right, (((1,), (1,)), ((), ())), preferred_element_type=F32)
             row = jnp.sum(jnp.where(keep, found, 0.0), axis=0, keepdims=True)
             for c in range(4):
-                piece = row[:, 128 * c : 128 * c + 128]
-                sums_ref[z, 4 * edge + c : 4 * edge + c + 1, :] = piece
-                if edge in (6, 7, 10, 11):
-                    place = 4 * (6, 7, 10, 11).index(edge) + c
-                    moving_ref[z, place : place + 1, :] = piece
-
-
-def sum_x_kernel(sums_ref, moving_ref, left_ref, out_ref, up_ref):
-    for z in range(2):
-        last = lanes((16, 128)) >= 96
-        below = pltpu.roll(jnp.where(last, left_ref[z], moving_ref[z]), 32, 1)
-        out_ref[z, 0:16] = sums_ref[z, 0:16]
-        out_ref[z, 16:24] = sums_ref[z, 16:24] + below[0:8]
-        out_ref[z, 24:32] = sums_ref[z, 32:40] + below[8:16]
+                sums_ref[z, 4 * edge + c : 4 * edge + c + 1, :] = row[:, 128 * c : 128 * c + 128]
+
+
+def sum_x_kernel(sums_ref, left_ref, right_ref, out_ref, up_ref):
+    for z in range(2):
+        all_x = jnp.concatenate([left_ref[z], sums_ref[z], right_ref[z]], axis=1)
+        below = pltpu.roll(all_x, 32, 1)
+        out_ref[z, 0:16] = all_x[0:16]
+        out_ref[z, 16:24] = all_x[16:24] + below[24:32]
+        out_ref[z, 24:32] = all_x[32:40] + below[40:48]
     up_ref[...] = out_ref[1, 0:24]
 
 
@@ -123,33 +128,47 @@
         middle_ref[z, 4:8] = sums_ref[z, 16:20]
 
 
+def by_x(value, count, rows):
+    group = lanes((rows, value.shape[1])) // 32
+    total = jnp.where(group == 0, value[0:rows], 0.0)
+    for x in range(1, count):
+        total = total + jnp.where(group == x, value[rows * x : rows * x + rows], 0.0)
+    return total
+
+
+def three(high, low, value):
+    kept, rest = split(value)
+    return dot(high, kept) + dot(high, rest) + dot(low, kept)
+
+
 def solve(block_high, block_low, rows_ref):
-    high, low = split(rows_ref[...])
-    found = dot(block_high, high) + dot(block_high, low) + dot(block_low, high)
-    return own_lanes(found)
-
-
-def first_kernel(lower_ref, upper_ref, middle_ref, below_ref, above_ref, bh_ref, bl_ref, out_ref, x_ref, rows, found):
-    for z in range(2):
-        rows[...] = jnp.zeros((48, 128), F32)
-        out_ref[z] = jnp.zeros((32, 128), F32)
-        x_ref[z] = jnp.zeros((16, 128), F32)
+    return own_lanes(three(block_high, block_low, rows_ref[...]))
+
+
+def first_kernel(lower_ref, upper_ref, middle_ref, below_ref, above_ref, bh_ref, bl_ref, g_ref, wide_ref, x_ref, rows):
+    for z in range(2):
+        rows[...] = jnp.zeros((32, 384), F32)
         node = lower_ref[z] + below_ref[z]
         top = upper_ref[z] + above_ref[z]
         middle = middle_ref[z]
         for slot, (source, at) in enumerate(((node, 0), (top, 0), (middle, 0), (node, 4), (top, 4))):
-            average = source[at : at + 3] / source[at + 3 : at + 4]
-            edge = SLOT_EDGES[slot]
-            rows[3 * edge : 3 * edge + 3] = average
-            out_ref[z, 16 + 3 * slot : 19 + 3 * slot] = average
-        found[...] = solve(bh_ref[z, :, 0:48], bl_ref[z, :, 0:48], rows)
-        for slot, edge in enumerate(SLOT_EDGES):
-            value = found[3 * edge : 3 * edge + 3]
-            out_ref[z, 3 * slot : 3 * slot + 3] = value
-            x_ref[z, 3 * slot : 3 * slot + 3] = value
-
-
-def prepare_kernel(matrix_ref, block_ref, place_ref, ah_ref, al_ref, bh_ref, bl_ref, packed, stacked):
+            rows[3 * slot : 3 * slot + 3] = source[at : at + 3] / source[at + 3 : at + 4]
+        found = by_x(three(bh_ref[z, :, 0:32], bl_ref[z, :, 0:32], rows[...]), 12, 24)
+        x_ref[z] = jnp.where(lax.broadcasted_iota(jnp.int32, (16, 384), 0) < 15, found[0:16], 0.0)
+        g_ref[z] = rows[0:16]
+        wide_ref[z, 0:16] = pltpu.roll(rows[0:16], 320, 1)[:, 0:256]
+        wide_ref[z, 15:24] = pltpu.roll(rows[0:16], 288, 1)[6:15, 0:256]
+
+
+def pick(rows_ref, value):
+    rows_ref[...] = value
+    return [rows_ref[3 * edge : 3 * edge + 3] for edge in WIDE_EDGES]
+
+
+def prepare_kernel(
+    matrix_ref, block_ref, place_ref, choice_ref, ah_ref, al_ref, bh_ref, bl_ref, out_ref, packed, stacked, full, small
+):
+    step = pl.program_id(0)
     packed[7] = jnp.zeros((72, 128), F32)
     for offset in range(27):
         start, tile = 36 * offset % 128, 36 * offset // 128
@@ -162,41 +181,67 @@
         pad = jnp.zeros((4, 1024), BF16)
         stacked[40 * z : 40 * z + 40] = jnp.concatenate([high, pad], axis=0)
         stacked[80 + 40 * z : 120 + 40 * z] = jnp.concatenate([low, pad], axis=0)
-    found = dot(stacked[...], place_ref[...]).astype(BF16)
-    for z in range(2):
-        ah_ref[z, 0] = found[40 * z : 40 * z + 40]
-        al_ref[z, 0] = found[80 + 40 * z : 120 + 40 * z]
-    packed[0] = jnp.zeros((72, 128), F32)
-    packed[0, :, 0:36] = block_ref[0]
-    for z in range(2):
-        high, low = split(packed[0, pl.ds(z, 36, stride=2), :])
-        pad = jnp.zeros((4, 128), BF16)
-        bh_ref[z, 0] = jnp.concatenate([high, pad], axis=0)
-        bl_ref[z, 0] = jnp.concatenate([low, pad], axis=0)
+    found = dot(stacked[...], place_ref[...])
+    for z in range(2):
+        high, low = found[40 * z : 40 * z + 40], found[80 + 40 * z : 120 + 40 * z]
+        ah_ref[z, 0] = high.astype(BF16)
+        al_ref[z, 0] = low.astype(BF16)
+        for place, value in enumerate(pick(full, high + low)):
+            out_ref[0, z, 3 * place : 3 * place + 3, 0:768] = value
+    for which in range(2):
+        packed[0] = jnp.zeros((72, 128), F32)
+        packed[0, :, 0:36] = block_ref[lax.rem(step + 2 * which, 4)]
+        for z in range(2):
+            high, low = split(packed[0, pl.ds(z, 36, stride=2), :])
+            pad = jnp.zeros((4, 128), BF16)
+            high, low = jnp.concatenate([high, pad], axis=0), jnp.concatenate([low, pad], axis=0)
+            if which == 0:
+                bh_ref[z, 0] = high
+                bl_ref[z, 0] = low
+            value = dot(high, choice_ref[...]) + dot(low, choice_ref[...])
+            at = 768 + 128 * which
+            for place, piece in enumerate(pick(small, value)):
+                out_ref[0, z, 3 * place : 3 * place + 3, at : at + 128] = piece
 
 
 def prepare(matrix, block):
-    table = jnp.asarray(placement(), BF16)
     outs = (shape(2, 4, 40, 768, dtype=BF16),) * 2 + (shape(2, 4, 40, 128, dtype=BF16),) * 2
+    outs = outs + (shape(4, 2, 24, 1024),)
     wide = pl.BlockSpec((2, 1, 40, 768), lambda i: (0, i, 0, 0))
     slim = pl.BlockSpec((2, 1, 40, 128), lambda i: (0, i, 0, 0))
-    ah, al, bh, bl = call(
+    ah, al, bh, bl, sent = call(
         prepare_kernel,
         outs,
-        (pltpu.VMEM((8, 72, 128), F32), pltpu.VMEM((160, 1024), BF16)),
+        (
+            pltpu.VMEM((8, 72, 128), F32),
+            pltpu.VMEM((160, 1024), BF16),
+            pltpu.VMEM((40, 768), F32),
+            pltpu.VMEM((40, 128), F32),
+        ),
         flops=20_000_000,
         grid=(4,),
         in_specs=[
             pl.BlockSpec((1, 27, 72, 36), lambda i: (i, 0, 0, 0)),
-            pl.BlockSpec((1, 72, 36), lambda i: (i, 0, 0)),
+            pl.BlockSpec((4, 72, 36), lambda i: (0, 0, 0)),
             pl.BlockSpec((1024, 768), lambda i: (0, 0)),
+            pl.BlockSpec((128, 128), lambda i: (0, 0)),
         ],
-        out_specs=(wide, wide, slim, slim),
-    )(matrix, block, table)
+        out_specs=(wide, wide, slim, slim, pl.BlockSpec((1, 2, 24, 1024), lambda i: (i, 0, 0, 0))),
+    )(matrix, block, jnp.asarray(placement(), BF16), jnp.asarray(choice(), BF16))
     return (
         ah.reshape(2, 160, 768), al.reshape(2, 160, 768),
-        bh.reshape(2, 160, 128), bl.reshape(2, 160, 128),
-    )
+        bh.reshape(2, 160, 128), bl.reshape(2, 160, 128), sent,
+    )
+
+
+def merge_kernel(own_ref, left_ref, right_ref, ah_ref, al_ref, bh_ref, bl_ref):
+    for z in range(2):
+        cells = [left_ref.at[0, z], left_ref.at[1, z]] + [own_ref.at[x, z] for x in range(4)]
+        cells = cells + [right_ref.at[0, z], right_ref.at[1, z]]
+        ah_ref[z], al_ref[z] = split(jnp.concatenate([c[:, 0:768] for c in cells], axis=0))
+        first, second = slice(768, 896), slice(896, 1024)
+        parts = [c[:, second] for c in cells[0:2]] + [c[:, first] for c in cells] + [c[:, second] for c in cells[6:8]]
+        bh_ref[z], bl_ref[z] = split(jnp.concatenate(parts, axis=0))
 
 
 def views(near, far):
@@ -226,27 +271,43 @@
     return views(near, far)
 
 
-def sweep_kernel(own_ref, left_ref, right_ref, g_ref, ah_ref, al_ref, bh_ref, bl_ref, x_ref, rows, found):
-    pairs = [split(view) for view in gathered(own_ref, left_ref, right_ref)]
-    high, low = [p[0] for p in pairs], [p[1] for p in pairs]
-    for z in range(2):
-        found[...] = product(high, low, ah_ref, al_ref, z)
-        rows[...] = jnp.zeros((48, 128), F32)
-        for slot, edge in enumerate(SLOT_EDGES):
-            rows[3 * edge : 3 * edge + 3] = g_ref[z, 3 * slot : 3 * slot + 3, 0:128] - found[3 * edge : 3 * edge + 3]
-        found[...] = solve(bh_ref[z, :, 0:48], bl_ref[z, :, 0:48], rows)
-        x_ref[z] = jnp.zeros((16, 128), F32)
-        for slot, edge in enumerate(SLOT_EDGES):
-            x_ref[z, 3 * slot : 3 * slot + 3] = (
-                own_ref[z, 3 * slot : 3 * slot + 3, 0:128] + found[3 * edge : 3 * edge + 3]
-            )
+def sweep_kernel(top, own_ref, left_ref, right_ref, g_ref, ah_ref, al_ref, bh_ref, bl_ref, x_ref, rows, closed):
+    seen = jnp.concatenate([left_ref[...], own_ref[0], own_ref[1], right_ref[0:96]], axis=0)
+    look = [pltpu.roll(seen, 384 - 32 * start, 1)[:, 0:256] for start in (1, 2, 3, 4)]
+    pairs = [split(view) for view in look]
+    rows[24:32] = jnp.zeros((8, 256), F32)
+    for z in range(2):
+        kept = jnp.concatenate([p[0][48 * z : 48 * z + 192] for p in pairs], axis=0)
+        rest = jnp.concatenate([p[1][48 * z : 48 * z + 192] for p in pairs], axis=0)
+        both = dot(ah_ref[z], jnp.concatenate([kept, rest], axis=1))
+        found = by_x(both[:, 0:256] + both[:, 256:512] + dot(al_ref[z], kept), 8, 24)
+        rows[0:24] = g_ref[z] - found
+        found = by_x(three(bh_ref[z, 48:240, 0:32], bl_ref[z, 48:240, 0:32], rows[...]), 8, 24)
+        rows[0:24] = found
+        at = 48 * z + 48
+        body_rows = look[1][at : at + 16] + rows[0:16]
+        body_rows = jnp.where(lax.broadcasted_iota(jnp.int32, (16, 256), 0) < 15, body_rows, 0.0)
+        closed[...] = jnp.zeros((16, 256), F32)
+        closed[6:15] = rows[15:24]
+        after = look[2][at : at + 16] + closed[...]
+        row = lax.broadcasted_iota(jnp.int32, (16, 256), 0)
+        after = jnp.where((row >= 6) & (row < 15), after, 0.0)
+        if top == 5:
+            pad = jnp.zeros((16, 128), F32)
+            body_rows = pltpu.roll(jnp.concatenate([body_rows, pad], axis=1), 64, 1)
+            after = pltpu.roll(jnp.concatenate([after, pad], axis=1), 96, 1)
+            x_ref[z] = jnp.where(lanes((16, 384)) // 32 == 10, after, body_rows)
+        else:
+            after = pltpu.roll(after, 32, 1)
+            use = (lanes((16, 256)) // 32 == 7) & (row >= 6)
+            x_ref[z] = pltpu.roll(jnp.where(use, after, body_rows), 192, 1)
 
 
 def average_kernel(g_ref, right_ref, wide_ref, out_ref, ahead):
     for z in range(3):
         source = g_ref.at[z] if z < 2 else right_ref.at[96:112]
-        ahead[z, 0:16] = source[:, 0:128]
-        ahead[z, 16:32] = views(source[:, 0:128], source[:, 128:256])[2]
+        ahead[z, 0:16] = source[:, 128:256]
+        ahead[z, 16:32] = views(source[:, 128:256], source[:, 256:384])[2]
     for z in range(2):
         wide_ref[z] = jnp.zeros((48, 128), F32)
         for edge in range(12):
@@ -280,54 +341,50 @@
 
 
 def body(displacement, dof_weight, coarse_matrix, block_inverse):
-    lane = lanes((2, 16, 128))
     weights = jnp.transpose(dof_weight[:, 0], (2, 1, 0, 3))
-    sums, moving = call(numer_kernel, (shape(2, 48, 128), shape(2, 16, 128)), flops=20_000_000)(
-        displacement[:, 0], weights
-    )
+    sums = call(numer_kernel, shape(2, 48, 128), flops=20_000_000)(displacement[:, 0], weights)
+    left, right = shifted(sums, "gx", 1), shifted(sums, "gx", -1)
     matrix = jnp.transpose(coarse_matrix[:, 0], (0, 2, 3, 1, 4)).reshape(4, 27, 72, 36)
     block = jnp.transpose(block_inverse[:, 0], (0, 2, 1, 3)).reshape(4, 72, 36)
-    ah, al, bh, bl = prepare(matrix, block)
-    left = shifted(moving, "gx", 1)
-    sums, up = call(sum_x_kernel, (shape(2, 32, 128), shape(24, 128)))(sums, moving, left)
+    ah, al, bh, bl, sent = prepare(matrix, block)
+    left, right, sent = lax.optimization_barrier((left, right, sent))
+    sums, up = call(sum_x_kernel, (shape(2, 32, 384), shape(24, 384)))(sums, left, right)
     left = shifted(up, "gz", 1)
-    lower, upper, middle = call(sum_z_kernel, (shape(2, 8, 128),) * 3)(sums, left)
+    rows_left, rows_right = shifted(sent[2:4], "gx", 1), shifted(sent[0:2], "gx", -1)
+    lower, upper, middle = call(sum_z_kernel, (shape(2, 8, 384),) * 3)(sums, left)
     below, above = shifted(upper, "gy", 1), shifted(lower, "gy", -1)
-    both, x = call(
+    wide = (shape(2, 192, 768, dtype=BF16),) * 2 + (shape(2, 288, 128, dtype=BF16),) * 2
+    operator = call(merge_kernel, wide, flops=10_000_000)(sent, rows_left, rows_right)
+    g, near, x = call(
         first_kernel,
-        (shape(2, 32, 128), shape(2, 16, 128)),
-        (pltpu.VMEM((48, 128), F32), pltpu.VMEM((40, 128), F32)),
-    )(lower, upper, middle, below, above, bh, bl)
-    average = None
+        (shape(2, 16, 384), shape(2, 24, 256), shape(2, 16, 384)),
+        (pltpu.VMEM((32, 384), F32),),
+    )(lower, upper, middle, below, above, operator[2], operator[3])
     for sweep in range(3):
-        left = shifted(x, "gx", 1)
-        right = shifted(both if sweep == 0 else x, "gx", -1)
-        x = jnp.concatenate([x, jnp.where(lane < 64, right[:, 0:16], left)], axis=2)
-        if sweep == 0:
-            g = jnp.concatenate([both[:, 16:32], right[:, 16:32]], axis=2)
         below, above = shifted(x, "gy", 1), shifted(x, "gy", -1)
         own = jnp.concatenate([x, below, above], axis=1)
         left = shifted(own[1], "gz", 1)
-        moving = own.reshape(96, 256)
+        moving = own.reshape(96, own.shape[2])
         if sweep == 0:
             moving = jnp.concatenate([moving, g[0]], axis=0)
         right = shifted(moving, "gz", -1)
         if sweep == 0:
-            wide, average = call(
+            every, average = call(
                 average_kernel, (shape(2, 48, 128), shape(4, 2, 36, 32)), (pltpu.VMEM((3, 32, 128), F32),)
             )(g, right)
-        small = (pltpu.VMEM((48, 128), F32), pltpu.VMEM((40, 128), F32))
         if sweep < 2:
-            x = call(sweep_kernel, shape(2, 16, 128), small, flops=10_000_000)(
-                own, left, right, g, ah, al, bh, bl
-            )
-        else:
             x = call(
-                last_kernel,
-                shape(4, 2, 36, 32),
-                (pltpu.VMEM((48, 128), F32), pltpu.VMEM((3, 32, 128), F32), pltpu.VMEM((40, 128), F32)),
-                flops=10_000_000,
-            )(own, left, right, wide, ah, al, bh, bl)
+                functools.partial(sweep_kernel, 5 - sweep),
+                shape(2, 16, 384 if sweep == 0 else 256),
+                (pltpu.VMEM((32, 256), F32), pltpu.VMEM((16, 256), F32)),
+                flops=20_000_000,
+            )(own, left, right, near, *operator)
+    x = call(
+        last_kernel,
+        shape(4, 2, 36, 32),
+        (pltpu.VMEM((48, 128), F32), pltpu.VMEM((3, 32, 128), F32), pltpu.VMEM((40, 128), F32)),
+        flops=10_000_000,
+    )(own, left, right, every, ah, al, bh, bl)
     return average.reshape(4, 1, 2, 12, 3, 32), x.reshape(4, 1, 2, 36, 32)
 
 

time: 147 us -> 133 us (0.905)
  starting transfers between devices: 71.7 us -> 62.3 us
  waiting for transfers between devices: 60.2 us -> 52.7 us
  Pallas kernels: 7.32 us -> 10.1 us
    ppermute x22 -> x19, starting transfers between devices: 71.7 us -> 62.3 us  [shifted(): lax.ppermute(block, axis, [((i - distance) % count, i) for i in range(cou...]
    ppermute x22 -> x19, waiting for transfers between devices: 60.2 us -> 52.7 us  [shifted(): lax.ppermute(block, axis, [((i - distance) % count, i) for i in range(cou...]
    pallas_call x6 -> x7, Pallas kernels: 2.99 us -> 5.6 us  [the longest x2 3.82 us: body(): call(functools.partial(sweep_kernel, 5 - sweep), shape(2, 16, 384 if swee...]
    unnamed x10 -> x14, local copies, waits for them, and re-layouts: 5.32 us -> 5.34 us
  transfers between devices with their start and end apart: 22 -> 19, of which waited for: 12 -> 9; matrix products, arithmetic and copies ran while one was open for 1% -> 1% of each run, Pallas kernels for 2% -> 3%
where the time goes in v2:
time: 133 us; the launch traced here: 132 us
  starting transfers between devices  62.3 us (47%)
  waiting for transfers between devices  52.7 us (40%)
  Pallas kernels  10.1 us (8%)
  local copies, waits for them, and re-layouts  6.16 us (5%)
    ppermute x19, starting transfers between devices, shifted(): lax.ppermute(block, axis, [((i - distance) % count, i) for i in range(cou...  62.3 us
    ppermute x19, waiting for transfers between devices, shifted(): lax.ppermute(block, axis, [((i - distance) % count, i) for i in range(cou...  52.7 us
    unnamed x14, local copies, waits for them, and re-layouts  5.34 us
    pallas_call x2, Pallas kernels, body(): call(functools.partial(sweep_kernel, 5 - sweep), shape(2, 16, 384 if swee...  3.82 us
    pallas_call x1, Pallas kernels, prepare(): call(prepare_kernel, outs, (pltpu.VMEM((8, 72, 128), F32), pltpu.VMEM((16...  3.44 us
  transfers between devices with their start and end apart: 19, of which 9 were waited for; matrix products, arithmetic and copies ran while one was open for 1% of the time, Pallas kernels for 3%

profile of v2, /device:TPU:6, one launch (start us, length us, event | category | flops | bytes accessed | tf_op | source)
XLA Modules:
  0.0 132.3 jit_solution(9702353953247464230)
XLA Ops:
  1.4 1.7 %copy-done.1 = bf16[4,1,2,12,3,32,128]{6,5,4,3,2,1,0:T(8,128)(2,1)S(1)} copy-done((bf16[4,1,2,12,3,32,128]{6,5,4,3,2,1,0:T(8,128)(2,1)S(1)}, bf16[4,1,2,12,3,32,128]{6,5,4,3,2,1,0:T(8,128)(2,1)}, u32[]{:S(2)}) %copy-start.1) | copy-done | bytes 2359320
  4.0 2.7 %collective-permute-start.1 = (f32[2,48,128]{2,1,0:T(8,128)S(1)}, f32[2,48,128]{2,1,0:T(8,128)S(1)}, u32[]{:S(2)}, u32[]{:S(2)}) collective-permute-start(f32[2,48,128]{2,1,0:T(8,128)S(1)} %shard_map.77.sums_ref), channel_id=1, source_target_pairs={{128,0},{256,128},{384,256},{0,384},{129,1},{257,129},{385,257},{1... | collective-permute-start | bytes 147464 | tf_op jit(solution)/shard_map/ppermute | solution.py:56
  6.8 6.9 %collective-permute-start = (f32[2,48,128]{2,1,0:T(8,128)S(1)}, f32[2,48,128]{2,1,0:T(8,128)S(1)}, u32[]{:S(2)}, u32[]{:S(2)}) collective-permute-start(f32[2,48,128]{2,1,0:T(8,128)S(1)} %shard_map.77.sums_ref), channel_id=1, source_target_pairs={{384,0},{0,128},{128,256},{256,384},{385,1},{1,129},{129,257},{257... | collective-permute-start | bytes 147464 | tf_op jit(solution)/shard_map/ppermute | solution.py:56
  13.7 2.1 %copy-done = f32[4,1,2,27,36,36]{5,2,4,3,1,0:T(2,128)S(1)} copy-done((f32[4,1,2,27,36,36]{5,2,4,3,1,0:T(2,128)S(1)}, f32[4,1,2,27,36,36]{5,2,4,3,1,0:T(2,128)}, u32[]{:S(2)}) %copy-start) | copy-done | bytes 1119768
  15.8 3.4 %shard_map.78 = (bf16[2,4,40,768]{3,2,1,0:T(8,128)(2,1)S(1)}, bf16[2,4,40,768]{3,2,1,0:T(8,128)(2,1)S(1)}, bf16[2,4,40,128]{3,2,1,0:T(8,128)(2,1)S(1)}, bf16[2,4...) custom-call(f32[4,27,72,36]{3,2,1,0:T(8,128)S(1)} %bitcast.35, f32[4,72,36]{2,1,0:T(8,128)S(1)} %bitcast.43, ...), custom_call_target="tpu_custom_call" | custom-call | flops 20000000 | bytes 1000000 | tf_op jit(solution)/shard_map/pallas_call | solution.py:212
  19.4 1.9 %collective-permute-start.6 = (f32[2,2,24,1024]{3,2,1,0:T(8,128)S(1)}, f32[2,2,24,1024]{3,2,1,0:T(8,128)S(1)}, u32[]{:S(2)}, u32[]{:S(2)}) collective-permute-start(f32[2,2,24,1024]{3,2,1,0:T(8,128)S(1)} %get-tuple-element.50), channel_id=1, source_target_pairs={{128,0},{256,128},{384,256},{0,384},{129,1},{257,129},{385,257},{1... | collective-permute-start | bytes 1179656 | tf_op jit(solution)/shard_map/ppermute | solution.py:56
  21.3 5.1 %collective-permute-start.5 = (f32[2,2,24,1024]{3,2,1,0:T(8,128)S(1)}, f32[2,2,24,1024]{3,2,1,0:T(8,128)S(1)}, u32[]{:S(2)}, u32[]{:S(2)}) collective-permute-start(f32[2,2,24,1024]{3,2,1,0:T(8,128)S(1)} %get-tuple-element.51), channel_id=1, source_target_pairs={{384,0},{0,128},{128,256},{256,384},{385,1},{1,129},{129,257},{257... | collective-permute-start | bytes 1179656 | tf_op jit(solution)/shard_map/ppermute | solution.py:56
  26.5 1.9 %collective-permute-start.2 = (f32[24,384]{1,0:T(8,128)S(1)}, f32[24,384]{1,0:T(8,128)S(1)}, u32[]{:S(2)}, u32[]{:S(2)}) collective-permute-start(f32[24,384]{1,0:T(8,128)S(1)} %get-tuple-element.28), channel_id=1, source_target_pairs={{7,0},{0,1},{1,2},{2,3},{3,4},{4,5},{5,6},{6,7},{15,8},{8,9},{9,10... | collective-permute-start | bytes 110600 | tf_op jit(solution)/shard_map/ppermute | solution.py:56
  28.5 5.1 %collective-permute-done.2.left_ref = f32[24,384]{1,0:T(8,128)S(1)} collective-permute-done((f32[24,384]{1,0:T(8,128)S(1)}, f32[24,384]{1,0:T(8,128)S(1)}, u32[]{:S(2)}, u32[]{:S(2)}) %collective-permute-start.2) | collective-permute-done | bytes 36896 | tf_op jit(solution)/shard_map/ppermute | solution.py:56
  33.6 11.2 %collective-permute-start.4 = (f32[2,8,384]{2,1,0:T(8,128)S(1)}, f32[2,8,384]{2,1,0:T(8,128)S(1)}, u32[]{:S(2)}, u32[]{:S(2)}) collective-permute-start(f32[2,8,384]{2,1,0:T(8,128)S(1)} %get-tuple-element.29.lower_ref), channel_id=1, source_target_pairs={{8,0},{16,8},{24,16},{32,24},{40,32},{48,40},{56,48},{64,56},{72,6... | collective-permute-start | bytes 73736 | tf_op jit(solution)/shard_map/ppermute | solution.py:56
  44.9 1.9 %collective-permute-start.3 = (f32[2,8,384]{2,1,0:T(8,128)S(1)}, f32[2,8,384]{2,1,0:T(8,128)S(1)}, u32[]{:S(2)}, u32[]{:S(2)}) collective-permute-start(f32[2,8,384]{2,1,0:T(8,128)S(1)} %get-tuple-element.30.upper_ref), channel_id=1, source_target_pairs={{120,0},{0,8},{8,16},{16,24},{24,32},{32,40},{40,48},{48,56},{56,6... | collective-permute-start | bytes 73736 | tf_op jit(solution)/shard_map/ppermute | solution.py:56
  47.1 9.5 %collective-permute-done.3.below_ref = f32[2,8,384]{2,1,0:T(8,128)S(1)} collective-permute-done((f32[2,8,384]{2,1,0:T(8,128)S(1)}, f32[2,8,384]{2,1,0:T(8,128)S(1)}, u32[]{:S(2)}, u32[]{:S(2)}) %collective-permute-start.3) | collective-permute-done | bytes 24608 | tf_op jit(solution)/shard_map/ppermute | solution.py:56
  57.1 1.9 %collective-permute-start.8 = (f32[2,16,384]{2,1,0:T(8,128)S(1)}, f32[2,16,384]{2,1,0:T(8,128)S(1)}, u32[]{:S(2)}, u32[]{:S(2)}) collective-permute-start(f32[2,16,384]{2,1,0:T(8,128)S(1)} %get-tuple-element.36), channel_id=1, source_target_pairs={{8,0},{16,8},{24,16},{32,24},{40,32},{48,40},{56,48},{64,56},{72,6... | collective-permute-start | bytes 147464 | tf_op jit(solution)/shard_map/ppermute | solution.py:56
  59.0 3.9 %collective-permute-start.7 = (f32[2,16,384]{2,1,0:T(8,128)S(1)}, f32[2,16,384]{2,1,0:T(8,128)S(1)}, u32[]{:S(2)}, u32[]{:S(2)}) collective-permute-start(f32[2,16,384]{2,1,0:T(8,128)S(1)} %get-tuple-element.36), channel_id=1, source_target_pairs={{120,0},{0,8},{8,16},{16,24},{24,32},{32,40},{40,48},{48,56},{56,6... | collective-permute-start | bytes 147464 | tf_op jit(solution)/shard_map/ppermute | solution.py:56
  63.0 8.0 %collective-permute-done.7 = f32[2,16,384]{2,1,0:T(8,128)S(1)} collective-permute-done((f32[2,16,384]{2,1,0:T(8,128)S(1)}, f32[2,16,384]{2,1,0:T(8,128)S(1)}, u32[]{:S(2)}, u32[]{:S(2)}) %collective-permute-start.7) | collective-permute-done | bytes 49184 | tf_op jit(solution)/shard_map/ppermute | solution.py:56
  71.1 1.9 %collective-permute-start.9 = (f32[112,384]{1,0:T(8,128)S(1)}, f32[112,384]{1,0:T(8,128)S(1)}, u32[]{:S(2)}, u32[]{:S(2)}) collective-permute-start(f32[112,384]{1,0:T(8,128)S(1)} %pad_maximum_fusion), channel_id=1, source_target_pairs={{1,0},{2,1},{3,2},{4,3},{5,4},{6,5},{7,6},{0,7},{9,8},{10,9},{11,1... | collective-permute-start | bytes 516104 | tf_op jit(solution)/shard_map/ppermute | solution.py:56
  73.0 2.4 %collective-permute-start.10 = (f32[48,384]{1,0:T(8,128)S(1)}, f32[48,384]{1,0:T(8,128)S(1)}, u32[]{:S(2)}, u32[]{:S(2)}) collective-permute-start(f32[48,384]{1,0:T(8,128)S(1)} %slice_bitcast_fusion.1), channel_id=1, source_target_pairs={{7,0},{0,1},{1,2},{2,3},{3,4},{4,5},{5,6},{6,7},{15,8},{8,9},{9,10... | collective-permute-start | bytes 221192 | tf_op jit(solution)/shard_map/ppermute | solution.py:56
  75.4 5.1 %collective-permute-done.10.left_ref = f32[48,384]{1,0:T(8,128)S(1)} collective-permute-done((f32[48,384]{1,0:T(8,128)S(1)}, f32[48,384]{1,0:T(8,128)S(1)}, u32[]{:S(2)}, u32[]{:S(2)}) %collective-permute-start.10) | collective-permute-done | bytes 73760 | tf_op jit(solution)/shard_map/ppermute | solution.py:56
  80.5 1.9 %shard_map.84 = f32[2,16,384]{2,1,0:T(8,128)S(1)} custom-call(f32[2,48,384]{2,1,0:T(8,128)S(1)} %constant_dynamic-update-slice_fusion.own_ref, f32[48,384]{1,0:T(8,128)S(1)} %collective-permute-done.10.left_ref, f32[112,384]{1,0:T(8,128)S(1)} %collective-permute-done.9.right_ref, f32[2,24,256]{2,1,0:T(8,128)S(1)} %get-tuple-element.38.g_ref, ...), custom_call_target="tpu_custom_call" | custom-call | flops 20000000 | bytes 1000000 | tf_op jit(solution)/shard_map/pallas_call | solution.py:376
  82.4 1.9 %collective-permute-start.12 = (f32[2,16,384]{2,1,0:T(8,128)S(1)}, f32[2,16,384]{2,1,0:T(8,128)S(1)}, u32[]{:S(2)}, u32[]{:S(2)}) collective-permute-start(f32[2,16,384]{2,1,0:T(8,128)S(1)} %shard_map.84), channel_id=1, source_target_pairs={{8,0},{16,8},{24,16},{32,24},{40,32},{48,40},{56,48},{64,56},{72,6... | collective-permute-start | bytes 147464 | tf_op jit(solution)/shard_map/ppermute | solution.py:56
  84.3 3.9 %collective-permute-start.11 = (f32[2,16,384]{2,1,0:T(8,128)S(1)}, f32[2,16,384]{2,1,0:T(8,128)S(1)}, u32[]{:S(2)}, u32[]{:S(2)}) collective-permute-start(f32[2,16,384]{2,1,0:T(8,128)S(1)} %shard_map.84), channel_id=1, source_target_pairs={{120,0},{0,8},{8,16},{16,24},{24,32},{32,40},{40,48},{48,56},{56,6... | collective-permute-start | bytes 147464 | tf_op jit(solution)/shard_map/ppermute | solution.py:56
  88.4 7.9 %collective-permute-done.11 = f32[2,16,384]{2,1,0:T(8,128)S(1)} collective-permute-done((f32[2,16,384]{2,1,0:T(8,128)S(1)}, f32[2,16,384]{2,1,0:T(8,128)S(1)}, u32[]{:S(2)}, u32[]{:S(2)}) %collective-permute-start.11) | collective-permute-done | bytes 49184 | tf_op jit(solution)/shard_map/ppermute | solution.py:56
  96.3 1.9 %collective-permute-start.14 = (f32[96,384]{1,0:T(8,128)S(1)}, f32[96,384]{1,0:T(8,128)S(1)}, u32[]{:S(2)}, u32[]{:S(2)}) collective-permute-start(f32[96,384]{1,0:T(8,128)S(1)} %bitcast.38), channel_id=1, source_target_pairs={{1,0},{2,1},{3,2},{4,3},{5,4},{6,5},{7,6},{0,7},{9,8},{10,9},{11,1... | collective-permute-start | bytes 442376 | tf_op jit(solution)/shard_map/ppermute | solution.py:56
  98.3 2.4 %collective-permute-start.13 = (f32[48,384]{1,0:T(8,128)S(1)}, f32[48,384]{1,0:T(8,128)S(1)}, u32[]{:S(2)}, u32[]{:S(2)}) collective-permute-start(f32[48,384]{1,0:T(8,128)S(1)} %slice_bitcast_fusion), channel_id=1, source_target_pairs={{7,0},{0,1},{1,2},{2,3},{3,4},{4,5},{5,6},{6,7},{15,8},{8,9},{9,10... | collective-permute-start | bytes 221192 | tf_op jit(solution)/shard_map/ppermute | solution.py:56
  100.7 5.1 %collective-permute-done.13.left_ref = f32[48,384]{1,0:T(8,128)S(1)} collective-permute-done((f32[48,384]{1,0:T(8,128)S(1)}, f32[48,384]{1,0:T(8,128)S(1)}, u32[]{:S(2)}, u32[]{:S(2)}) %collective-permute-start.13) | collective-permute-done | bytes 73760 | tf_op jit(solution)/shard_map/ppermute | solution.py:56
  105.7 1.9 %shard_map.85 = f32[2,16,256]{2,1,0:T(8,128)S(1)} custom-call(f32[2,48,384]{2,1,0:T(8,128)S(1)} %pad_maximum_fusion.1.own_ref, f32[48,384]{1,0:T(8,128)S(1)} %collective-permute-done.13.left_ref, f32[96,384]{1,0:T(8,128)S(1)} %collective-permute-done.14.right_ref, f32[2,24,256]{2,1,0:T(8,128)S(1)} %get-tuple-element.38.g_ref, ...), custom_call_target="tpu_custom_call" | custom-call | flops 20000000 | bytes 1000000 | tf_op jit(solution)/shard_map/pallas_call | solution.py:376
  107.7 1.9 %collective-permute-start.16 = (f32[2,16,256]{2,1,0:T(8,128)S(1)}, f32[2,16,256]{2,1,0:T(8,128)S(1)}, u32[]{:S(2)}, u32[]{:S(2)}) collective-permute-start(f32[2,16,256]{2,1,0:T(8,128)S(1)} %shard_map.85), channel_id=1, source_target_pairs={{8,0},{16,8},{24,16},{32,24},{40,32},{48,40},{56,48},{64,56},{72,6... | collective-permute-start | bytes 98312 | tf_op jit(solution)/shard_map/ppermute | solution.py:56
  109.6 3.9 %collective-permute-start.15 = (f32[2,16,256]{2,1,0:T(8,128)S(1)}, f32[2,16,256]{2,1,0:T(8,128)S(1)}, u32[]{:S(2)}, u32[]{:S(2)}) collective-permute-start(f32[2,16,256]{2,1,0:T(8,128)S(1)} %shard_map.85), channel_id=1, source_target_pairs={{120,0},{0,8},{8,16},{16,24},{24,32},{32,40},{40,48},{48,56},{56,6... | collective-permute-start | bytes 98312 | tf_op jit(solution)/shard_map/ppermute | solution.py:56
  113.6 7.9 %collective-permute-done.15 = f32[2,16,256]{2,1,0:T(8,128)S(1)} collective-permute-done((f32[2,16,256]{2,1,0:T(8,128)S(1)}, f32[2,16,256]{2,1,0:T(8,128)S(1)}, u32[]{:S(2)}, u32[]{:S(2)}) %collective-permute-start.15) | collective-permute-done | bytes 32800 | tf_op jit(solution)/shard_map/ppermute | solution.py:56
  121.5 1.9 %collective-permute-start.18 = (f32[96,256]{1,0:T(8,128)S(1)}, f32[96,256]{1,0:T(8,128)S(1)}, u32[]{:S(2)}, u32[]{:S(2)}) collective-permute-start(f32[96,256]{1,0:T(8,128)S(1)} %bitcast.40), channel_id=1, source_target_pairs={{1,0},{2,1},{3,2},{4,3},{5,4},{6,5},{7,6},{0,7},{9,8},{10,9},{11,1... | collective-permute-start | bytes 294920 | tf_op jit(solution)/shard_map/ppermute | solution.py:56
  123.4 2.4 %collective-permute-start.17 = (f32[48,256]{1,0:T(8,128)S(1)}, f32[48,256]{1,0:T(8,128)S(1)}, u32[]{:S(2)}, u32[]{:S(2)}) collective-permute-start(f32[48,256]{1,0:T(8,128)S(1)} %slice_bitcast_fusion.2), channel_id=1, source_target_pairs={{7,0},{0,1},{1,2},{2,3},{3,4},{4,5},{5,6},{6,7},{15,8},{8,9},{9,10... | collective-permute-start | bytes 147464 | tf_op jit(solution)/shard_map/ppermute | solution.py:56
  126.7 3.9 %collective-permute-done.17.left_ref = f32[48,256]{1,0:T(8,128)S(1)} collective-permute-done((f32[48,256]{1,0:T(8,128)S(1)}, f32[48,256]{1,0:T(8,128)S(1)}, u32[]{:S(2)}, u32[]{:S(2)}) %collective-permute-start.17) | collective-permute-done | bytes 49184 | tf_op jit(solution)/shard_map/ppermute | solution.py:56
  (40 shorter events, 5.4 us)
Async XLA Ops:
  0.6 13.0 %copy-start.4 = (bf16[128,128]{1,0:T(8,128)(2,1)S(1)}, bf16[128,128]{1,0:T(8,128)(2,1)}, u32[]{:S(2)}) copy-start(bf16[128,128]{1,0:T(8,128)(2,1)} %constant.5.clone.choice_ref) | copy-start | bytes 98308
  1.4 1.7 %copy-start.1 = (bf16[4,1,2,12,3,32,128]{6,5,4,3,2,1,0:T(8,128)(2,1)S(1)}, bf16[4,1,2,12,3,32,128]{6,5,4,3,2,1,0:T(8,128)(2,1)}, u32[]{:S(2)}) copy-start(bf16[4,1,2,12,3,32,128]{6,5,4,3,2,1,0:T(8,128)(2,1)} %param.6) | copy-start | bytes 7077892
  3.1 10.6 %copy-start.2 = (bf16[1024,768]{1,0:T(8,128)(2,1)S(1)}, bf16[1024,768]{1,0:T(8,128)(2,1)}, u32[]{:S(2)}) copy-start(bf16[1024,768]{1,0:T(8,128)(2,1)} %constant.4.clone.place_ref) | copy-start | bytes 4718596
  3.1 10.6 %copy-start.3 = (f32[4,1,2,36,36]{4,2,3,1,0:T(2,128)S(1)}, f32[4,1,2,36,36]{4,2,3,1,0:T(2,128)}, u32[]{:S(2)}) copy-start(f32[4,1,2,36,36]{4,2,3,1,0:T(2,128)} %param.9) | copy-start | bytes 124420
  4.0 15.3 %collective-permute-start.1 = (f32[2,48,128]{2,1,0:T(8,128)S(1)}, f32[2,48,128]{2,1,0:T(8,128)S(1)}, u32[]{:S(2)}, u32[]{:S(2)}) collective-permute-start(f32[2,48,128]{2,1,0:T(8,128)S(1)} %shard_map.77.sums_ref), channel_id=1, source_target_pairs={{128,0},{256,128},{384,256},{0,384},{129,1},{257,129},{385,257},{1... | collective-permute-start | bytes 147464 | tf_op jit(solution)/shard_map/ppermute | solution.py:56
  6.8 12.5 %collective-permute-start = (f32[2,48,128]{2,1,0:T(8,128)S(1)}, f32[2,48,128]{2,1,0:T(8,128)S(1)}, u32[]{:S(2)}, u32[]{:S(2)}) collective-permute-start(f32[2,48,128]{2,1,0:T(8,128)S(1)} %shard_map.77.sums_ref), channel_id=1, source_target_pairs={{384,0},{0,128},{128,256},{256,384},{385,1},{1,129},{129,257},{257... | collective-permute-start | bytes 147464 | tf_op jit(solution)/shard_map/ppermute | solution.py:56
  13.7 2.1 %copy-start = (f32[4,1,2,27,36,36]{5,2,4,3,1,0:T(2,128)S(1)}, f32[4,1,2,27,36,36]{5,2,4,3,1,0:T(2,128)}, u32[]{:S(2)}) copy-start(f32[4,1,2,27,36,36]{5,2,4,3,1,0:T(2,128)} %param.8) | copy-start | bytes 3359236
  19.4 27.4 %collective-permute-start.6 = (f32[2,2,24,1024]{3,2,1,0:T(8,128)S(1)}, f32[2,2,24,1024]{3,2,1,0:T(8,128)S(1)}, u32[]{:S(2)}, u32[]{:S(2)}) collective-permute-start(f32[2,2,24,1024]{3,2,1,0:T(8,128)S(1)} %get-tuple-element.50), channel_id=1, source_target_pairs={{128,0},{256,128},{384,256},{0,384},{129,1},{257,129},{385,257},{1... | collective-permute-start | bytes 1179656 | tf_op jit(solution)/shard_map/ppermute | solution.py:56
  21.3 25.5 %collective-permute-start.5 = (f32[2,2,24,1024]{3,2,1,0:T(8,128)S(1)}, f32[2,2,24,1024]{3,2,1,0:T(8,128)S(1)}, u32[]{:S(2)}, u32[]{:S(2)}) collective-permute-start(f32[2,2,24,1024]{3,2,1,0:T(8,128)S(1)} %get-tuple-element.51), channel_id=1, source_target_pairs={{384,0},{0,128},{128,256},{256,384},{385,1},{1,129},{129,257},{257... | collective-permute-start | bytes 1179656 | tf_op jit(solution)/shard_map/ppermute | solution.py:56
  26.5 7.1 %collective-permute-start.2 = (f32[24,384]{1,0:T(8,128)S(1)}, f32[24,384]{1,0:T(8,128)S(1)}, u32[]{:S(2)}, u32[]{:S(2)}) collective-permute-start(f32[24,384]{1,0:T(8,128)S(1)} %get-tuple-element.28), channel_id=1, source_target_pairs={{7,0},{0,1},{1,2},{2,3},{3,4},{4,5},{5,6},{6,7},{15,8},{8,9},{9,10... | collective-permute-start | bytes 110600 | tf_op jit(solution)/shard_map/ppermute | solution.py:56
  33.6 13.4 %collective-permute-start.4 = (f32[2,8,384]{2,1,0:T(8,128)S(1)}, f32[2,8,384]{2,1,0:T(8,128)S(1)}, u32[]{:S(2)}, u32[]{:S(2)}) collective-permute-start(f32[2,8,384]{2,1,0:T(8,128)S(1)} %get-tuple-element.29.lower_ref), channel_id=1, source_target_pairs={{8,0},{16,8},{24,16},{32,24},{40,32},{48,40},{56,48},{64,56},{72,6... | collective-permute-start | bytes 73736 | tf_op jit(solution)/shard_map/ppermute | solution.py:56
  44.9 11.7 %collective-permute-start.3 = (f32[2,8,384]{2,1,0:T(8,128)S(1)}, f32[2,8,384]{2,1,0:T(8,128)S(1)}, u32[]{:S(2)}, u32[]{:S(2)}) collective-permute-start(f32[2,8,384]{2,1,0:T(8,128)S(1)} %get-tuple-element.30.upper_ref), channel_id=1, source_target_pairs={{120,0},{0,8},{8,16},{16,24},{24,32},{32,40},{40,48},{48,56},{56,6... | collective-permute-start | bytes 73736 | tf_op jit(solution)/shard_map/ppermute | solution.py:56
  57.1 13.9 %collective-permute-start.8 = (f32[2,16,384]{2,1,0:T(8,128)S(1)}, f32[2,16,384]{2,1,0:T(8,128)S(1)}, u32[]{:S(2)}, u32[]{:S(2)}) collective-permute-start(f32[2,16,384]{2,1,0:T(8,128)S(1)} %get-tuple-element.36), channel_id=1, source_target_pairs={{8,0},{16,8},{24,16},{32,24},{40,32},{48,40},{56,48},{64,56},{72,6... | collective-permute-start | bytes 147464 | tf_op jit(solution)/shard_map/ppermute | solution.py:56
  59.0 12.0 %collective-permute-start.7 = (f32[2,16,384]{2,1,0:T(8,128)S(1)}, f32[2,16,384]{2,1,0:T(8,128)S(1)}, u32[]{:S(2)}, u32[]{:S(2)}) collective-permute-start(f32[2,16,384]{2,1,0:T(8,128)S(1)} %get-tuple-element.36), channel_id=1, source_target_pairs={{120,0},{0,8},{8,16},{16,24},{24,32},{32,40},{40,48},{48,56},{56,6... | collective-permute-start | bytes 147464 | tf_op jit(solution)/shard_map/ppermute | solution.py:56
  71.1 9.4 %collective-permute-start.9 = (f32[112,384]{1,0:T(8,128)S(1)}, f32[112,384]{1,0:T(8,128)S(1)}, u32[]{:S(2)}, u32[]{:S(2)}) collective-permute-start(f32[112,384]{1,0:T(8,128)S(1)} %pad_maximum_fusion), channel_id=1, source_target_pairs={{1,0},{2,1},{3,2},{4,3},{5,4},{6,5},{7,6},{0,7},{9,8},{10,9},{11,1... | collective-permute-start | bytes 516104 | tf_op jit(solution)/shard_map/ppermute | solution.py:56
  73.0 7.5 %collective-permute-start.10 = (f32[48,384]{1,0:T(8,128)S(1)}, f32[48,384]{1,0:T(8,128)S(1)}, u32[]{:S(2)}, u32[]{:S(2)}) collective-permute-start(f32[48,384]{1,0:T(8,128)S(1)} %slice_bitcast_fusion.1), channel_id=1, source_target_pairs={{7,0},{0,1},{1,2},{2,3},{3,4},{4,5},{5,6},{6,7},{15,8},{8,9},{9,10... | collective-permute-start | bytes 221192 | tf_op jit(solution)/shard_map/ppermute | solution.py:56
  82.4 6.0 %collective-permute-start.12 = (f32[2,16,384]{2,1,0:T(8,128)S(1)}, f32[2,16,384]{2,1,0:T(8,128)S(1)}, u32[]{:S(2)}, u32[]{:S(2)}) collective-permute-start(f32[2,16,384]{2,1,0:T(8,128)S(1)} %shard_map.84), channel_id=1, source_target_pairs={{8,0},{16,8},{24,16},{32,24},{40,32},{48,40},{56,48},{64,56},{72,6... | collective-permute-start | bytes 147464 | tf_op jit(solution)/shard_map/ppermute | solution.py:56
  84.3 12.0 %collective-permute-start.11 = (f32[2,16,384]{2,1,0:T(8,128)S(1)}, f32[2,16,384]{2,1,0:T(8,128)S(1)}, u32[]{:S(2)}, u32[]{:S(2)}) collective-permute-start(f32[2,16,384]{2,1,0:T(8,128)S(1)} %shard_map.84), channel_id=1, source_target_pairs={{120,0},{0,8},{8,16},{16,24},{24,32},{32,40},{40,48},{48,56},{56,6... | collective-permute-start | bytes 147464 | tf_op jit(solution)/shard_map/ppermute | solution.py:56
  96.3 9.4 %collective-permute-start.14 = (f32[96,384]{1,0:T(8,128)S(1)}, f32[96,384]{1,0:T(8,128)S(1)}, u32[]{:S(2)}, u32[]{:S(2)}) collective-permute-start(f32[96,384]{1,0:T(8,128)S(1)} %bitcast.38), channel_id=1, source_target_pairs={{1,0},{2,1},{3,2},{4,3},{5,4},{6,5},{7,6},{0,7},{9,8},{10,9},{11,1... | collective-permute-start | bytes 442376 | tf_op jit(solution)/shard_map/ppermute | solution.py:56
  98.3 7.5 %collective-permute-start.13 = (f32[48,384]{1,0:T(8,128)S(1)}, f32[48,384]{1,0:T(8,128)S(1)}, u32[]{:S(2)}, u32[]{:S(2)}) collective-permute-start(f32[48,384]{1,0:T(8,128)S(1)} %slice_bitcast_fusion), channel_id=1, source_target_pairs={{7,0},{0,1},{1,2},{2,3},{3,4},{4,5},{5,6},{6,7},{15,8},{8,9},{9,10... | collective-permute-start | bytes 221192 | tf_op jit(solution)/shard_map/ppermute | solution.py:56
  107.7 5.9 %collective-permute-start.16 = (f32[2,16,256]{2,1,0:T(8,128)S(1)}, f32[2,16,256]{2,1,0:T(8,128)S(1)}, u32[]{:S(2)}, u32[]{:S(2)}) collective-permute-start(f32[2,16,256]{2,1,0:T(8,128)S(1)} %shard_map.85), channel_id=1, source_target_pairs={{8,0},{16,8},{24,16},{32,24},{40,32},{48,40},{56,48},{64,56},{72,6... | collective-permute-start | bytes 98312 | tf_op jit(solution)/shard_map/ppermute | solution.py:56
  109.6 11.8 %collective-permute-start.15 = (f32[2,16,256]{2,1,0:T(8,128)S(1)}, f32[2,16,256]{2,1,0:T(8,128)S(1)}, u32[]{:S(2)}, u32[]{:S(2)}) collective-permute-start(f32[2,16,256]{2,1,0:T(8,128)S(1)} %shard_map.85), channel_id=1, source_target_pairs={{120,0},{0,8},{8,16},{16,24},{24,32},{32,40},{40,48},{48,56},{56,6... | collective-permute-start | bytes 98312 | tf_op jit(solution)/shard_map/ppermute | solution.py:56
  121.5 9.2 %collective-permute-start.18 = (f32[96,256]{1,0:T(8,128)S(1)}, f32[96,256]{1,0:T(8,128)S(1)}, u32[]{:S(2)}, u32[]{:S(2)}) collective-permute-start(f32[96,256]{1,0:T(8,128)S(1)} %bitcast.40), channel_id=1, source_target_pairs={{1,0},{2,1},{3,2},{4,3},{5,4},{6,5},{7,6},{0,7},{9,8},{10,9},{11,1... | collective-permute-start | bytes 294920 | tf_op jit(solution)/shard_map/ppermute | solution.py:56
  123.4 7.2 %collective-permute-start.17 = (f32[48,256]{1,0:T(8,128)S(1)}, f32[48,256]{1,0:T(8,128)S(1)}, u32[]{:S(2)}, u32[]{:S(2)}) collective-permute-start(f32[48,256]{1,0:T(8,128)S(1)} %slice_bitcast_fusion.2), channel_id=1, source_target_pairs={{7,0},{0,1},{1,2},{2,3},{3,4},{4,5},{5,6},{6,7},{15,8},{8,9},{9,10... | collective-permute-start | bytes 147464 | tf_op jit(solution)/shard_map/ppermute | solution.py:56

commit v3 on v2

--- a/solution.py
+++ b/solution.py
@@ -8,6 +8,7 @@
 from jax.experimental.pallas import tpu as pltpu
 from jax.sharding import PartitionSpec as P
 
+
 F32 = jnp.float32
 BF16 = jnp.bfloat16
 OFFSETS = (
@@ -15,7 +16,6 @@
     (0, 0, 0), (0, 0, 1), (1, 0, 0), (1, 0, 1),
     (0, 0, 0), (0, 1, 0), (1, 0, 0), (1, 1, 0),
 )
-SLOT_EDGES = (0, 2, 4, 8, 9)
 WIDE_EDGES = (0, 2, 4, 8, 9, 6, 10, 11)
 
 
@@ -44,10 +44,11 @@
 
 
 def choice():
-    table = np.zeros((128, 128), np.float32)
-    for place, edge in enumerate(WIDE_EDGES):
-        for comp in range(3):
-            table[3 * edge + comp, 3 * place + comp] = 1.0
+    table = np.zeros((512, 128), np.float32)
+    for x in range(4):
+        for place, edge in enumerate(WIDE_EDGES):
+            for comp in range(3):
+                table[128 * x + 3 * edge + comp, 32 * x + 3 * place + comp] = 1.0
     return table
 
 
@@ -92,24 +93,41 @@
     return jax.ShapeDtypeStruct(dims, dtype)
 
 
-def numer_kernel(disp_ref, weight_ref, sums_ref):
+def numer_kernel(disp_ref, weight_ref, block_ref, choice_ref, sums_ref, weights, packed, rows):
+    step = pl.program_id(0)
+
+    @pl.when(step == 0)
+    def _():
+        weights[...] = weight_ref[...].astype(F32)
+        packed[...] = jnp.zeros((4, 72, 128), F32)
+        for x in range(4):
+            packed[x, :, 0:36] = block_ref[x]
+        for z in range(2):
+            value = jnp.concatenate([packed[x, pl.ds(z, 36, stride=2), :] for x in range(4)], axis=1)
+            high, low = split(value)
+            rows[0:36] = dot(high, choice_ref[...]) + dot(low, choice_ref[...])
+            for place, edge in enumerate(WIDE_EDGES):
+                sums_ref[z, 48 + 3 * place : 51 + 3 * place] = rows[3 * edge : 3 * edge + 3]
+
     ones = jnp.ones((128, 128), BF16)
     group = (lanes((4, 512)) % 128) // 32
     keep = group == lax.broadcasted_iota(jnp.int32, (4, 512), 0)
-    for edge in range(12):
-        for z in range(2):
+    for z in range(2):
+        pieces = []
+        for edge in range(2):
             parts = [disp_ref[x, z, edge, c] for c in range(3) for x in range(4)]
             right = jnp.concatenate(parts + [ones], axis=0)
-            left = weight_ref[edge, z]
+            at = 4 * step + 2 * edge + z
+            left = jnp.concatenate([weights[x, pl.ds(at, 1), :] for x in range(4)], axis=0).astype(BF16)
             found = lax.dot_general(left, right, (((1,), (1,)), ((), ())), preferred_element_type=F32)
             row = jnp.sum(jnp.where(keep, found, 0.0), axis=0, keepdims=True)
-            for c in range(4):
-                sums_ref[z, 4 * edge + c : 4 * edge + c + 1, :] = row[:, 128 * c : 128 * c + 128]
+            pieces = pieces + [row[:, 128 * c : 128 * c + 128] for c in range(4)]
+        sums_ref[z, pl.ds(pl.multiple_of(8 * step, 8), 8), :] = jnp.concatenate(pieces, axis=0)
 
 
 def sum_x_kernel(sums_ref, left_ref, right_ref, out_ref, up_ref):
     for z in range(2):
-        all_x = jnp.concatenate([left_ref[z], sums_ref[z], right_ref[z]], axis=1)
+        all_x = jnp.concatenate([left_ref[z, 0:48], sums_ref[z, 0:48], right_ref[z, 0:48]], axis=1)
         below = pltpu.roll(all_x, 32, 1)
         out_ref[z, 0:16] = all_x[0:16]
         out_ref[z, 16:24] = all_x[16:24] + below[24:32]
@@ -145,7 +163,10 @@
     return own_lanes(three(block_high, block_low, rows_ref[...]))
 
 
-def first_kernel(lower_ref, upper_ref, middle_ref, below_ref, above_ref, bh_ref, bl_ref, g_ref, wide_ref, x_ref, rows):
+def first_kernel(
+    lower_ref, upper_ref, middle_ref, below_ref, above_ref, own_ref, left_ref, right_ref,
+    g_ref, wide_ref, x_ref, bh_ref, bl_ref, rows,
+):
     for z in range(2):
         rows[...] = jnp.zeros((32, 384), F32)
         node = lower_ref[z] + below_ref[z]
@@ -153,7 +174,10 @@
         middle = middle_ref[z]
         for slot, (source, at) in enumerate(((node, 0), (top, 0), (middle, 0), (node, 4), (top, 4))):
             rows[3 * slot : 3 * slot + 3] = source[at : at + 3] / source[at + 3 : at + 4]
-        found = by_x(three(bh_ref[z, :, 0:32], bl_ref[z, :, 0:32], rows[...]), 12, 24)
+        parts = [ref[z, 48:72, 32 * x : 32 * x + 32] for ref in (left_ref, own_ref, right_ref) for x in range(4)]
+        high, low = split(jnp.concatenate(parts, axis=0))
+        bh_ref[z], bl_ref[z] = high[48:240], low[48:240]
+        found = by_x(three(high, low, rows[...]), 12, 24)
         x_ref[z] = jnp.where(lax.broadcasted_iota(jnp.int32, (16, 384), 0) < 15, found[0:16], 0.0)
         g_ref[z] = rows[0:16]
         wide_ref[z, 0:16] = pltpu.roll(rows[0:16], 320, 1)[:, 0:256]
@@ -166,9 +190,8 @@
 
 
 def prepare_kernel(
-    matrix_ref, block_ref, place_ref, choice_ref, ah_ref, al_ref, bh_ref, bl_ref, out_ref, packed, stacked, full, small
+    matrix_ref, block_ref, place_ref, ah_ref, al_ref, bh_ref, bl_ref, out_ref, packed, stacked, full
 ):
-    step = pl.program_id(0)
     packed[7] = jnp.zeros((72, 128), F32)
     for offset in range(27):
         start, tile = 36 * offset % 128, 36 * offset // 128
@@ -187,26 +210,19 @@
         ah_ref[z, 0] = high.astype(BF16)
         al_ref[z, 0] = low.astype(BF16)
         for place, value in enumerate(pick(full, high + low)):
-            out_ref[0, z, 3 * place : 3 * place + 3, 0:768] = value
-    for which in range(2):
-        packed[0] = jnp.zeros((72, 128), F32)
-        packed[0, :, 0:36] = block_ref[lax.rem(step + 2 * which, 4)]
-        for z in range(2):
-            high, low = split(packed[0, pl.ds(z, 36, stride=2), :])
-            pad = jnp.zeros((4, 128), BF16)
-            high, low = jnp.concatenate([high, pad], axis=0), jnp.concatenate([low, pad], axis=0)
-            if which == 0:
-                bh_ref[z, 0] = high
-                bl_ref[z, 0] = low
-            value = dot(high, choice_ref[...]) + dot(low, choice_ref[...])
-            at = 768 + 128 * which
-            for place, piece in enumerate(pick(small, value)):
-                out_ref[0, z, 3 * place : 3 * place + 3, at : at + 128] = piece
+            out_ref[0, z, 3 * place : 3 * place + 3] = value
+    packed[0] = jnp.zeros((72, 128), F32)
+    packed[0, :, 0:36] = block_ref[0]
+    for z in range(2):
+        high, low = split(packed[0, pl.ds(z, 36, stride=2), :])
+        pad = jnp.zeros((4, 128), BF16)
+        bh_ref[z, 0] = jnp.concatenate([high, pad], axis=0)
+        bl_ref[z, 0] = jnp.concatenate([low, pad], axis=0)
 
 
 def prepare(matrix, block):
     outs = (shape(2, 4, 40, 768, dtype=BF16),) * 2 + (shape(2, 4, 40, 128, dtype=BF16),) * 2
-    outs = outs + (shape(4, 2, 24, 1024),)
+    outs = outs + (shape(4, 2, 24, 768),)
     wide = pl.BlockSpec((2, 1, 40, 768), lambda i: (0, i, 0, 0))
     slim = pl.BlockSpec((2, 1, 40, 128), lambda i: (0, i, 0, 0))
     ah, al, bh, bl, sent = call(
@@ -216,32 +232,27 @@
             pltpu.VMEM((8, 72, 128), F32),
             pltpu.VMEM((160, 1024), BF16),
             pltpu.VMEM((40, 768), F32),
-            pltpu.VMEM((40, 128), F32),
         ),
         flops=20_000_000,
         grid=(4,),
         in_specs=[
             pl.BlockSpec((1, 27, 72, 36), lambda i: (i, 0, 0, 0)),
-            pl.BlockSpec((4, 72, 36), lambda i: (0, 0, 0)),
+            pl.BlockSpec((1, 72, 36), lambda i: (i, 0, 0)),
             pl.BlockSpec((1024, 768), lambda i: (0, 0)),
-            pl.BlockSpec((128, 128), lambda i: (0, 0)),
         ],
-        out_specs=(wide, wide, slim, slim, pl.BlockSpec((1, 2, 24, 1024), lambda i: (i, 0, 0, 0))),
-    )(matrix, block, jnp.asarray(placement(), BF16), jnp.asarray(choice(), BF16))
+        out_specs=(wide, wide, slim, slim, pl.BlockSpec((1, 2, 24, 768), lambda i: (i, 0, 0, 0))),
+    )(matrix, block, jnp.asarray(placement(), BF16))
     return (
         ah.reshape(2, 160, 768), al.reshape(2, 160, 768),
         bh.reshape(2, 160, 128), bl.reshape(2, 160, 128), sent,
     )
 
 
-def merge_kernel(own_ref, left_ref, right_ref, ah_ref, al_ref, bh_ref, bl_ref):
-    for z in range(2):
-        cells = [left_ref.at[0, z], left_ref.at[1, z]] + [own_ref.at[x, z] for x in range(4)]
-        cells = cells + [right_ref.at[0, z], right_ref.at[1, z]]
-        ah_ref[z], al_ref[z] = split(jnp.concatenate([c[:, 0:768] for c in cells], axis=0))
-        first, second = slice(768, 896), slice(896, 1024)
-        parts = [c[:, second] for c in cells[0:2]] + [c[:, first] for c in cells] + [c[:, second] for c in cells[6:8]]
-        bh_ref[z], bl_ref[z] = split(jnp.concatenate(parts, axis=0))
+def merge_kernel(own_ref, left_ref, right_ref, ah_ref, al_ref):
+    for z in range(2):
+        cells = [left_ref[0, z], left_ref[1, z]] + [own_ref[x, z] for x in range(4)]
+        cells = cells + [right_ref[0, z], right_ref[1, z]]
+        ah_ref[z], al_ref[z] = split(jnp.concatenate(cells, axis=0))
 
 
 def views(near, far):
@@ -282,7 +293,7 @@
         both = dot(ah_ref[z], jnp.concatenate([kept, rest], axis=1))
         found = by_x(both[:, 0:256] + both[:, 256:512] + dot(al_ref[z], kept), 8, 24)
         rows[0:24] = g_ref[z] - found
-        found = by_x(three(bh_ref[z, 48:240, 0:32], bl_ref[z, 48:240, 0:32], rows[...]), 8, 24)
+        found = by_x(three(bh_ref[z], bl_ref[z], rows[...]), 8, 24)
         rows[0:24] = found
         at = 48 * z + 48
         body_rows = look[1][at : at + 16] + rows[0:16]
@@ -327,6 +338,7 @@
     seen = gathered(own_ref, left_ref, right_ref)
     pairs = [split(view) for view in seen]
     high, low = [p[0] for p in pairs], [p[1] for p in pairs]
+    state[...] = jnp.zeros((40, 128), F32)
     for z in range(3):
         ahead[z, 0:16] = seen[1][48 * z + 48 : 48 * z + 64]
         ahead[z, 16:32] = seen[2][48 * z + 48 : 48 * z + 64]
@@ -337,31 +349,57 @@
             state[3 * edge : 3 * edge + 3] = ahead[z + oz, start : start + 3]
         rows[...] = jnp.zeros((48, 128), F32)
         rows[0:36] = wide_ref[z, 0:36] - product(high, low, ah_ref, al_ref, z)[0:36]
-        write(out_ref, z, state[0:36] + solve(bh_ref[z, :, 0:48], bl_ref[z, :, 0:48], rows)[0:36])
-
-
-def body(displacement, dof_weight, coarse_matrix, block_inverse):
-    weights = jnp.transpose(dof_weight[:, 0], (2, 1, 0, 3))
-    sums = call(numer_kernel, shape(2, 48, 128), flops=20_000_000)(displacement[:, 0], weights)
-    left, right = shifted(sums, "gx", 1), shifted(sums, "gx", -1)
+        state[...] = state[...] + solve(bh_ref[z, :, 0:48], bl_ref[z, :, 0:48], rows)
+        turned = state[...].T
+        for x in range(4):
+            out_ref[x, z] = turned[32 * x : 32 * x + 32, 0:36]
+
+
+def after(value, *others):
+    return lax.optimization_barrier((value, *others))[0]
+
+
+def steps(displacement, dof_weight, coarse_matrix, block_inverse):
+    weights = jnp.transpose(dof_weight[:, 0], (0, 2, 1, 3)).reshape(4, 24, 128)
     matrix = jnp.transpose(coarse_matrix[:, 0], (0, 2, 3, 1, 4)).reshape(4, 27, 72, 36)
     block = jnp.transpose(block_inverse[:, 0], (0, 2, 1, 3)).reshape(4, 72, 36)
-    ah, al, bh, bl, sent = prepare(matrix, block)
-    left, right, sent = lax.optimization_barrier((left, right, sent))
-    sums, up = call(sum_x_kernel, (shape(2, 32, 384), shape(24, 384)))(sums, left, right)
+    inputs = (displacement[:, 0], weights, block, jnp.asarray(choice(), BF16))
+    sums = call(
+        numer_kernel,
+        shape(2, 72, 128),
+        (pltpu.VMEM((4, 24, 128), F32), pltpu.VMEM((4, 72, 128), F32), pltpu.VMEM((40, 128), F32)),
+        flops=20_000_000,
+        grid=(6,),
+        in_specs=[
+            pl.BlockSpec((4, 2, 2, 3, 32, 128), lambda i: (0, 0, i, 0, 0, 0)),
+            pl.BlockSpec((4, 24, 128), lambda i: (0, 0, 0)),
+            pl.BlockSpec((4, 72, 36), lambda i: (0, 0, 0)),
+            pl.BlockSpec((512, 128), lambda i: (0, 0)),
+        ],
+        out_specs=pl.BlockSpec((2, 72, 128), lambda i: (0, 0, 0)),
+    )(*(pltpu.with_memory_space_constraint(a, pltpu.HBM) for a in inputs))
+    mine, left, right = sums, shifted(sums, "gx", 1), shifted(sums, "gx", -1)
+    sides = (mine, left, right)
+    sums, up = call(sum_x_kernel, (shape(2, 32, 384), shape(24, 384)))(*sides)
     left = shifted(up, "gz", 1)
-    rows_left, rows_right = shifted(sent[2:4], "gx", 1), shifted(sent[0:2], "gx", -1)
+    ah, al, bh, bl, sent = prepare(after(matrix, up), block)
     lower, upper, middle = call(sum_z_kernel, (shape(2, 8, 384),) * 3)(sums, left)
     below, above = shifted(upper, "gy", 1), shifted(lower, "gy", -1)
-    wide = (shape(2, 192, 768, dtype=BF16),) * 2 + (shape(2, 288, 128, dtype=BF16),) * 2
-    operator = call(merge_kernel, wide, flops=10_000_000)(sent, rows_left, rows_right)
-    g, near, x = call(
+    g, near, x, near_high, near_low = call(
         first_kernel,
-        (shape(2, 16, 384), shape(2, 24, 256), shape(2, 16, 384)),
+        (shape(2, 16, 384), shape(2, 24, 256), shape(2, 16, 384)) + (shape(2, 192, 32, dtype=BF16),) * 2,
         (pltpu.VMEM((32, 384), F32),),
-    )(lower, upper, middle, below, above, operator[2], operator[3])
+    )(lower, upper, middle, below, above, *sides)
+    sent = after(sent, x)
+    rows_left = shifted(sent[2:4], "gx", 1)
+    rows_right = shifted(sent[0:2], "gx", -1)
     for sweep in range(3):
-        below, above = shifted(x, "gy", 1), shifted(x, "gy", -1)
+        below = shifted(x, "gy", 1)
+        above = shifted(x, "gy", -1)
+        if sweep == 0:
+            rows_left = after(rows_left, below, above)
+            wide = (shape(2, 192, 768, dtype=BF16),) * 2
+            operator = call(merge_kernel, wide, flops=10_000_000)(sent, rows_left, rows_right)
         own = jnp.concatenate([x, below, above], axis=1)
         left = shifted(own[1], "gz", 1)
         moving = own.reshape(96, own.shape[2])
@@ -378,14 +416,14 @@
                 shape(2, 16, 384 if sweep == 0 else 256),
                 (pltpu.VMEM((32, 256), F32), pltpu.VMEM((16, 256), F32)),
                 flops=20_000_000,
-            )(own, left, right, near, *operator)
+            )(own, left, right, near, *operator, near_high, near_low)
     x = call(
         last_kernel,
-        shape(4, 2, 36, 32),
+        shape(4, 2, 32, 36),
         (pltpu.VMEM((48, 128), F32), pltpu.VMEM((3, 32, 128), F32), pltpu.VMEM((40, 128), F32)),
         flops=10_000_000,
     )(own, left, right, every, ah, al, bh, bl)
-    return average.reshape(4, 1, 2, 12, 3, 32), x.reshape(4, 1, 2, 36, 32)
+    return average.reshape(4, 1, 2, 12, 3, 32), jnp.swapaxes(x, 2, 3)[:, None]
 
 
 def solution(mesh):
@@ -396,7 +434,7 @@
         P("gx", "gy", "gz", None, None),
     )
     return jax.shard_map(
-        body,
+        steps,
         mesh=mesh,
         in_specs=placed,
         out_specs=(P("gx", "gy", "gz", None, None, None), P("gx", "gy", "gz", None, None)),

time: 133 us -> 129 us (0.970)
  the two profiles are of different devices: /device:TPU:6 before, /device:TPU:56 now
where the time goes in v3:
time: 129 us
  starting transfers between devices  63.1 us (49%)
  waiting for transfers between devices  47.1 us (37%)
  Pallas kernels  14.5 us (11%)
  local copies, waits for them, and re-layouts  2.95 us (2%)
    ppermute x19, starting transfers between devices, shifted(): lax.ppermute(block, axis, [((i - distance) % count, i) for i in range(cou...  63.1 us
    ppermute x19, waiting for transfers between devices, shifted(): lax.ppermute(block, axis, [((i - distance) % count, i) for i in range(cou...  47.1 us
    pallas_call x1, Pallas kernels, steps(): call(numer_kernel, shape(2, 72, 128), (pltpu.VMEM((4, 24, 128), F32), plt...  4.66 us
    pallas_call x2, Pallas kernels, steps(): call(functools.partial(sweep_kernel, 5 - sweep), shape(2, 16, 384 if swee...  3.83 us
    pallas_call x1, Pallas kernels, prepare(): call(prepare_kernel, outs, (pltpu.VMEM((8, 72, 128), F32), pltpu.VMEM((16...  3.41 us
  transfers between devices with their start and end apart: 19, of which 10 were waited for; matrix products, arithmetic and copies ran while one was open for 1% of the time, Pallas kernels for 3%

profile of v3, /device:TPU:56, one launch (start us, length us, event | category | flops | bytes accessed | tf_op | source)
XLA Modules:
  0.0 128.6 jit_solution(9532661639025789793)
XLA Ops:
  0.7 4.7 %shard_map.77.sums_ref.own_ref = f32[2,72,128]{2,1,0:T(8,128)S(1)} custom-call(bf16[4,2,12,3,32,128]{5,4,3,2,1,0:T(8,128)(2,1)} %bitcast.49, bf16[4,24,128]{2,1,0:T(8,128)(2,1)} %bitcast.52, f32[4,72,36]{2,1,0:T(8,128)} %bitcast.43, bf16[512,128]{1,0:T(8,128)(2,1)} %constant.4.clone.choice_ref), custom_call_target="tpu_custom_call" | custom-call | flops 20000000 | bytes 1000000 | tf_op jit(solution)/shard_map/pallas_call | solution.py:367
  5.3 3.4 %collective-permute-start = (f32[2,72,128]{2,1,0:T(8,128)S(1)}, f32[2,72,128]{2,1,0:T(8,128)S(1)}, u32[]{:S(2)}, u32[]{:S(2)}) collective-permute-start(f32[2,72,128]{2,1,0:T(8,128)S(1)} %shard_map.77.sums_ref.own_ref), channel_id=1, source_target_pairs={{384,0},{0,128},{128,256},{256,384},{385,1},{1,129},{129,257},{257... | collective-permute-start | bytes 221192 | tf_op jit(solution)/shard_map/ppermute | solution.py:57
  8.7 3.7 %collective-permute-start.1 = (f32[2,72,128]{2,1,0:T(8,128)S(1)}, f32[2,72,128]{2,1,0:T(8,128)S(1)}, u32[]{:S(2)}, u32[]{:S(2)}) collective-permute-start(f32[2,72,128]{2,1,0:T(8,128)S(1)} %shard_map.77.sums_ref.own_ref), channel_id=1, source_target_pairs={{128,0},{256,128},{384,256},{0,384},{129,1},{257,129},{385,257},{1... | collective-permute-start | bytes 221192 | tf_op jit(solution)/shard_map/ppermute | solution.py:57
  12.8 2.2 %collective-permute-done.1.right_ref = f32[2,72,128]{2,1,0:T(8,128)S(1)} collective-permute-done((f32[2,72,128]{2,1,0:T(8,128)S(1)}, f32[2,72,128]{2,1,0:T(8,128)S(1)}, u32[]{:S(2)}, u32[]{:S(2)}) %collective-permute-start.1) | collective-permute-done | bytes 73760 | tf_op jit(solution)/shard_map/ppermute | solution.py:57
  15.1 1.9 %collective-permute-start.2 = (f32[24,384]{1,0:T(8,128)S(1)}, f32[24,384]{1,0:T(8,128)S(1)}, u32[]{:S(2)}, u32[]{:S(2)}) collective-permute-start(f32[24,384]{1,0:T(8,128)S(1)} %get-tuple-element.25), channel_id=1, source_target_pairs={{7,0},{0,1},{1,2},{2,3},{3,4},{4,5},{5,6},{6,7},{15,8},{8,9},{9,10... | collective-permute-start | bytes 110600 | tf_op jit(solution)/shard_map/ppermute | solution.py:57
  17.0 5.6 %collective-permute-done.2.left_ref = f32[24,384]{1,0:T(8,128)S(1)} collective-permute-done((f32[24,384]{1,0:T(8,128)S(1)}, f32[24,384]{1,0:T(8,128)S(1)}, u32[]{:S(2)}, u32[]{:S(2)}) %collective-permute-start.2) | collective-permute-done | bytes 36896 | tf_op jit(solution)/shard_map/ppermute | solution.py:57
  22.6 9.7 %collective-permute-start.3 = (f32[2,8,384]{2,1,0:T(8,128)S(1)}, f32[2,8,384]{2,1,0:T(8,128)S(1)}, u32[]{:S(2)}, u32[]{:S(2)}) collective-permute-start(f32[2,8,384]{2,1,0:T(8,128)S(1)} %get-tuple-element.27.upper_ref), channel_id=1, source_target_pairs={{120,0},{0,8},{8,16},{16,24},{24,32},{32,40},{40,48},{48,56},{56,6... | collective-permute-start | bytes 73736 | tf_op jit(solution)/shard_map/ppermute | solution.py:57
  32.3 1.9 %collective-permute-start.4 = (f32[2,8,384]{2,1,0:T(8,128)S(1)}, f32[2,8,384]{2,1,0:T(8,128)S(1)}, u32[]{:S(2)}, u32[]{:S(2)}) collective-permute-start(f32[2,8,384]{2,1,0:T(8,128)S(1)} %get-tuple-element.26.lower_ref), channel_id=1, source_target_pairs={{8,0},{16,8},{24,16},{32,24},{40,32},{48,40},{56,48},{64,56},{72,6... | collective-permute-start | bytes 73736 | tf_op jit(solution)/shard_map/ppermute | solution.py:57
  34.3 2.1 %copy-done = f32[4,1,2,27,36,36]{5,2,4,3,1,0:T(2,128)S(1)} copy-done((f32[4,1,2,27,36,36]{5,2,4,3,1,0:T(2,128)S(1)}, f32[4,1,2,27,36,36]{5,2,4,3,1,0:T(2,128)}, u32[]{:S(2)}) %copy-start) | copy-done | bytes 1119768
  36.4 3.4 %shard_map.82 = (bf16[2,4,40,768]{3,2,1,0:T(8,128)(2,1)S(1)}, bf16[2,4,40,768]{3,2,1,0:T(8,128)(2,1)S(1)}, bf16[2,4,40,128]{3,2,1,0:T(8,128)(2,1)S(1)}, bf16[2,4...) custom-call(f32[4,27,72,36]{3,2,1,0:T(8,128)S(1)} %bitcast.39, f32[4,72,36]{2,1,0:T(8,128)S(1)} %bitcast.44, ...), custom_call_target="tpu_custom_call" | custom-call | flops 20000000 | bytes 1000000 | tf_op jit(solution)/shard_map/pallas_call | solution.py:228
  39.8 4.2 %collective-permute-done.4.above_ref = f32[2,8,384]{2,1,0:T(8,128)S(1)} collective-permute-done((f32[2,8,384]{2,1,0:T(8,128)S(1)}, f32[2,8,384]{2,1,0:T(8,128)S(1)}, u32[]{:S(2)}, u32[]{:S(2)}) %collective-permute-start.4) | collective-permute-done | bytes 24608 | tf_op jit(solution)/shard_map/ppermute | solution.py:57
  44.6 5.7 %collective-permute-start.5 = (f32[2,16,384]{2,1,0:T(8,128)S(1)}, f32[2,16,384]{2,1,0:T(8,128)S(1)}, u32[]{:S(2)}, u32[]{:S(2)}) collective-permute-start(f32[2,16,384]{2,1,0:T(8,128)S(1)} %get-tuple-element.30), channel_id=1, source_target_pairs={{120,0},{0,8},{8,16},{16,24},{24,32},{32,40},{40,48},{48,56},{56,6... | collective-permute-start | bytes 147464 | tf_op jit(solution)/shard_map/ppermute | solution.py:57
  50.3 1.9 %collective-permute-start.6 = (f32[2,16,384]{2,1,0:T(8,128)S(1)}, f32[2,16,384]{2,1,0:T(8,128)S(1)}, u32[]{:S(2)}, u32[]{:S(2)}) collective-permute-start(f32[2,16,384]{2,1,0:T(8,128)S(1)} %get-tuple-element.30), channel_id=1, source_target_pairs={{8,0},{16,8},{24,16},{32,24},{40,32},{48,40},{56,48},{64,56},{72,6... | collective-permute-start | bytes 147464 | tf_op jit(solution)/shard_map/ppermute | solution.py:57
  52.3 3.4 %collective-permute-start.9 = (f32[2,2,24,768]{3,2,1,0:T(8,128)S(1)}, f32[2,2,24,768]{3,2,1,0:T(8,128)S(1)}, u32[]{:S(2)}, u32[]{:S(2)}) collective-permute-start(f32[2,2,24,768]{3,2,1,0:T(8,128)S(1)} %get-tuple-element.51), channel_id=1, source_target_pairs={{384,0},{0,128},{128,256},{256,384},{385,1},{1,129},{129,257},{257... | collective-permute-start | bytes 884744 | tf_op jit(solution)/shard_map/ppermute | solution.py:57
  55.7 3.6 %collective-permute-start.10 = (f32[2,2,24,768]{3,2,1,0:T(8,128)S(1)}, f32[2,2,24,768]{3,2,1,0:T(8,128)S(1)}, u32[]{:S(2)}, u32[]{:S(2)}) collective-permute-start(f32[2,2,24,768]{3,2,1,0:T(8,128)S(1)} %get-tuple-element.50), channel_id=1, source_target_pairs={{128,0},{256,128},{384,256},{0,384},{129,1},{257,129},{385,257},{1... | collective-permute-start | bytes 884744 | tf_op jit(solution)/shard_map/ppermute | solution.py:57
  59.4 2.9 %collective-permute-done.6 = f32[2,16,384]{2,1,0:T(8,128)S(1)} collective-permute-done((f32[2,16,384]{2,1,0:T(8,128)S(1)}, f32[2,16,384]{2,1,0:T(8,128)S(1)}, u32[]{:S(2)}, u32[]{:S(2)}) %collective-permute-start.6) | collective-permute-done | bytes 49184 | tf_op jit(solution)/shard_map/ppermute | solution.py:57
  62.3 1.9 %collective-permute-start.7 = (f32[112,384]{1,0:T(8,128)S(1)}, f32[112,384]{1,0:T(8,128)S(1)}, u32[]{:S(2)}, u32[]{:S(2)}) collective-permute-start(f32[112,384]{1,0:T(8,128)S(1)} %pad_maximum_fusion), channel_id=1, source_target_pairs={{1,0},{2,1},{3,2},{4,3},{5,4},{6,5},{7,6},{0,7},{9,8},{10,9},{11,1... | collective-permute-start | bytes 516104 | tf_op jit(solution)/shard_map/ppermute | solution.py:57
  64.3 2.4 %collective-permute-start.8 = (f32[48,384]{1,0:T(8,128)S(1)}, f32[48,384]{1,0:T(8,128)S(1)}, u32[]{:S(2)}, u32[]{:S(2)}) collective-permute-start(f32[48,384]{1,0:T(8,128)S(1)} %slice_bitcast_fusion.1), channel_id=1, source_target_pairs={{7,0},{0,1},{1,2},{2,3},{3,4},{4,5},{5,6},{6,7},{15,8},{8,9},{9,10... | collective-permute-start | bytes 221192 | tf_op jit(solution)/shard_map/ppermute | solution.py:57
  66.9 4.8 %collective-permute-done.8.left_ref = f32[48,384]{1,0:T(8,128)S(1)} collective-permute-done((f32[48,384]{1,0:T(8,128)S(1)}, f32[48,384]{1,0:T(8,128)S(1)}, u32[]{:S(2)}, u32[]{:S(2)}) %collective-permute-start.8) | collective-permute-done | bytes 73760 | tf_op jit(solution)/shard_map/ppermute | solution.py:57
  73.7 7.1 %collective-permute-start.11 = (f32[2,16,384]{2,1,0:T(8,128)S(1)}, f32[2,16,384]{2,1,0:T(8,128)S(1)}, u32[]{:S(2)}, u32[]{:S(2)}) collective-permute-start(f32[2,16,384]{2,1,0:T(8,128)S(1)} %shard_map.84), channel_id=1, source_target_pairs={{120,0},{0,8},{8,16},{16,24},{24,32},{32,40},{40,48},{48,56},{56,6... | collective-permute-start | bytes 147464 | tf_op jit(solution)/shard_map/ppermute | solution.py:57
  80.7 1.9 %collective-permute-start.12 = (f32[2,16,384]{2,1,0:T(8,128)S(1)}, f32[2,16,384]{2,1,0:T(8,128)S(1)}, u32[]{:S(2)}, u32[]{:S(2)}) collective-permute-start(f32[2,16,384]{2,1,0:T(8,128)S(1)} %shard_map.84), channel_id=1, source_target_pairs={{8,0},{16,8},{24,16},{32,24},{40,32},{48,40},{56,48},{64,56},{72,6... | collective-permute-start | bytes 147464 | tf_op jit(solution)/shard_map/ppermute | solution.py:57
  82.7 10.1 %collective-permute-done.12 = f32[2,16,384]{2,1,0:T(8,128)S(1)} collective-permute-done((f32[2,16,384]{2,1,0:T(8,128)S(1)}, f32[2,16,384]{2,1,0:T(8,128)S(1)}, u32[]{:S(2)}, u32[]{:S(2)}) %collective-permute-start.12) | collective-permute-done | bytes 49184 | tf_op jit(solution)/shard_map/ppermute | solution.py:57
  92.7 1.9 %collective-permute-start.14 = (f32[96,384]{1,0:T(8,128)S(1)}, f32[96,384]{1,0:T(8,128)S(1)}, u32[]{:S(2)}, u32[]{:S(2)}) collective-permute-start(f32[96,384]{1,0:T(8,128)S(1)} %bitcast.41), channel_id=1, source_target_pairs={{1,0},{2,1},{3,2},{4,3},{5,4},{6,5},{7,6},{0,7},{9,8},{10,9},{11,1... | collective-permute-start | bytes 442376 | tf_op jit(solution)/shard_map/ppermute | solution.py:57
  94.7 2.4 %collective-permute-start.13 = (f32[48,384]{1,0:T(8,128)S(1)}, f32[48,384]{1,0:T(8,128)S(1)}, u32[]{:S(2)}, u32[]{:S(2)}) collective-permute-start(f32[48,384]{1,0:T(8,128)S(1)} %slice_bitcast_fusion), channel_id=1, source_target_pairs={{7,0},{0,1},{1,2},{2,3},{3,4},{4,5},{5,6},{6,7},{15,8},{8,9},{9,10... | collective-permute-start | bytes 221192 | tf_op jit(solution)/shard_map/ppermute | solution.py:57
  97.1 5.1 %collective-permute-done.13.left_ref = f32[48,384]{1,0:T(8,128)S(1)} collective-permute-done((f32[48,384]{1,0:T(8,128)S(1)}, f32[48,384]{1,0:T(8,128)S(1)}, u32[]{:S(2)}, u32[]{:S(2)}) %collective-permute-start.13) | collective-permute-done | bytes 73760 | tf_op jit(solution)/shard_map/ppermute | solution.py:57
  102.2 1.9 %shard_map.85 = f32[2,16,256]{2,1,0:T(8,128)S(1)} custom-call(f32[2,48,384]{2,1,0:T(8,128)S(1)} %pad_maximum_fusion.1.own_ref, f32[48,384]{1,0:T(8,128)S(1)} %collective-permute-done.13.left_ref, f32[96,384]{1,0:T(8,128)S(1)} %collective-permute-done.14.right_ref, f32[2,24,256]{2,1,0:T(8,128)S(1)} %get-tuple-element.32.g_ref, ...), custom_call_target="tpu_custom_call" | custom-call | flops 20000000 | bytes 1000000 | tf_op jit(solution)/shard_map/pallas_call | solution.py:414
  104.1 1.9 %collective-permute-start.15 = (f32[2,16,256]{2,1,0:T(8,128)S(1)}, f32[2,16,256]{2,1,0:T(8,128)S(1)}, u32[]{:S(2)}, u32[]{:S(2)}) collective-permute-start(f32[2,16,256]{2,1,0:T(8,128)S(1)} %shard_map.85), channel_id=1, source_target_pairs={{120,0},{0,8},{8,16},{16,24},{24,32},{32,40},{40,48},{48,56},{56,6... | collective-permute-start | bytes 98312 | tf_op jit(solution)/shard_map/ppermute | solution.py:57
  106.0 3.9 %collective-permute-start.16 = (f32[2,16,256]{2,1,0:T(8,128)S(1)}, f32[2,16,256]{2,1,0:T(8,128)S(1)}, u32[]{:S(2)}, u32[]{:S(2)}) collective-permute-start(f32[2,16,256]{2,1,0:T(8,128)S(1)} %shard_map.85), channel_id=1, source_target_pairs={{8,0},{16,8},{24,16},{32,24},{40,32},{48,40},{56,48},{64,56},{72,6... | collective-permute-start | bytes 98312 | tf_op jit(solution)/shard_map/ppermute | solution.py:57
  110.0 7.9 %collective-permute-done.16 = f32[2,16,256]{2,1,0:T(8,128)S(1)} collective-permute-done((f32[2,16,256]{2,1,0:T(8,128)S(1)}, f32[2,16,256]{2,1,0:T(8,128)S(1)}, u32[]{:S(2)}, u32[]{:S(2)}) %collective-permute-start.16) | collective-permute-done | bytes 32800 | tf_op jit(solution)/shard_map/ppermute | solution.py:57
  117.9 1.9 %collective-permute-start.18 = (f32[96,256]{1,0:T(8,128)S(1)}, f32[96,256]{1,0:T(8,128)S(1)}, u32[]{:S(2)}, u32[]{:S(2)}) collective-permute-start(f32[96,256]{1,0:T(8,128)S(1)} %bitcast.42), channel_id=1, source_target_pairs={{1,0},{2,1},{3,2},{4,3},{5,4},{6,5},{7,6},{0,7},{9,8},{10,9},{11,1... | collective-permute-start | bytes 294920 | tf_op jit(solution)/shard_map/ppermute | solution.py:57
  119.8 2.4 %collective-permute-start.17 = (f32[48,256]{1,0:T(8,128)S(1)}, f32[48,256]{1,0:T(8,128)S(1)}, u32[]{:S(2)}, u32[]{:S(2)}) collective-permute-start(f32[48,256]{1,0:T(8,128)S(1)} %slice_bitcast_fusion.2), channel_id=1, source_target_pairs={{7,0},{0,1},{1,2},{2,3},{3,4},{4,5},{5,6},{6,7},{15,8},{8,9},{9,10... | collective-permute-start | bytes 147464 | tf_op jit(solution)/shard_map/ppermute | solution.py:57
  123.1 3.9 %collective-permute-done.17.left_ref = f32[48,256]{1,0:T(8,128)S(1)} collective-permute-done((f32[48,256]{1,0:T(8,128)S(1)}, f32[48,256]{1,0:T(8,128)S(1)}, u32[]{:S(2)}, u32[]{:S(2)}) %collective-permute-start.17) | collective-permute-done | bytes 49184 | tf_op jit(solution)/shard_map/ppermute | solution.py:57
  (34 shorter events, 5.8 us)
Async XLA Ops:
  0.6 33.6 %copy-start.1 = (bf16[1024,768]{1,0:T(8,128)(2,1)S(1)}, bf16[1024,768]{1,0:T(8,128)(2,1)}, u32[]{:S(2)}) copy-start(bf16[1024,768]{1,0:T(8,128)(2,1)} %constant.5.clone.place_ref) | copy-start | bytes 4718596
  0.6 33.6 %copy-start.2 = (f32[4,1,2,36,36]{4,2,3,1,0:T(2,128)S(1)}, f32[4,1,2,36,36]{4,2,3,1,0:T(2,128)}, u32[]{:S(2)}) copy-start(f32[4,1,2,36,36]{4,2,3,1,0:T(2,128)} %param.9) | copy-start | bytes 124420
  5.3 7.5 %collective-permute-start = (f32[2,72,128]{2,1,0:T(8,128)S(1)}, f32[2,72,128]{2,1,0:T(8,128)S(1)}, u32[]{:S(2)}, u32[]{:S(2)}) collective-permute-start(f32[2,72,128]{2,1,0:T(8,128)S(1)} %shard_map.77.sums_ref.own_ref), channel_id=1, source_target_pairs={{384,0},{0,128},{128,256},{256,384},{385,1},{1,129},{129,257},{257... | collective-permute-start | bytes 221192 | tf_op jit(solution)/shard_map/ppermute | solution.py:57
  8.7 6.2 %collective-permute-start.1 = (f32[2,72,128]{2,1,0:T(8,128)S(1)}, f32[2,72,128]{2,1,0:T(8,128)S(1)}, u32[]{:S(2)}, u32[]{:S(2)}) collective-permute-start(f32[2,72,128]{2,1,0:T(8,128)S(1)} %shard_map.77.sums_ref.own_ref), channel_id=1, source_target_pairs={{128,0},{256,128},{384,256},{0,384},{129,1},{257,129},{385,257},{1... | collective-permute-start | bytes 221192 | tf_op jit(solution)/shard_map/ppermute | solution.py:57
  15.1 7.5 %collective-permute-start.2 = (f32[24,384]{1,0:T(8,128)S(1)}, f32[24,384]{1,0:T(8,128)S(1)}, u32[]{:S(2)}, u32[]{:S(2)}) collective-permute-start(f32[24,384]{1,0:T(8,128)S(1)} %get-tuple-element.25), channel_id=1, source_target_pairs={{7,0},{0,1},{1,2},{2,3},{3,4},{4,5},{5,6},{6,7},{15,8},{8,9},{9,10... | collective-permute-start | bytes 110600 | tf_op jit(solution)/shard_map/ppermute | solution.py:57
  22.6 17.2 %collective-permute-start.3 = (f32[2,8,384]{2,1,0:T(8,128)S(1)}, f32[2,8,384]{2,1,0:T(8,128)S(1)}, u32[]{:S(2)}, u32[]{:S(2)}) collective-permute-start(f32[2,8,384]{2,1,0:T(8,128)S(1)} %get-tuple-element.27.upper_ref), channel_id=1, source_target_pairs={{120,0},{0,8},{8,16},{16,24},{24,32},{32,40},{40,48},{48,56},{56,6... | collective-permute-start | bytes 73736 | tf_op jit(solution)/shard_map/ppermute | solution.py:57
  32.3 11.7 %collective-permute-start.4 = (f32[2,8,384]{2,1,0:T(8,128)S(1)}, f32[2,8,384]{2,1,0:T(8,128)S(1)}, u32[]{:S(2)}, u32[]{:S(2)}) collective-permute-start(f32[2,8,384]{2,1,0:T(8,128)S(1)} %get-tuple-element.26.lower_ref), channel_id=1, source_target_pairs={{8,0},{16,8},{24,16},{32,24},{40,32},{48,40},{56,48},{64,56},{72,6... | collective-permute-start | bytes 73736 | tf_op jit(solution)/shard_map/ppermute | solution.py:57
  34.2 2.1 %copy-start = (f32[4,1,2,27,36,36]{5,2,4,3,1,0:T(2,128)S(1)}, f32[4,1,2,27,36,36]{5,2,4,3,1,0:T(2,128)}, u32[]{:S(2)}) copy-start(f32[4,1,2,27,36,36]{5,2,4,3,1,0:T(2,128)} %param.8) | copy-start | bytes 3359236
  44.6 14.8 %collective-permute-start.5 = (f32[2,16,384]{2,1,0:T(8,128)S(1)}, f32[2,16,384]{2,1,0:T(8,128)S(1)}, u32[]{:S(2)}, u32[]{:S(2)}) collective-permute-start(f32[2,16,384]{2,1,0:T(8,128)S(1)} %get-tuple-element.30), channel_id=1, source_target_pairs={{120,0},{0,8},{8,16},{16,24},{24,32},{32,40},{40,48},{48,56},{56,6... | collective-permute-start | bytes 147464 | tf_op jit(solution)/shard_map/ppermute | solution.py:57
  50.3 12.0 %collective-permute-start.6 = (f32[2,16,384]{2,1,0:T(8,128)S(1)}, f32[2,16,384]{2,1,0:T(8,128)S(1)}, u32[]{:S(2)}, u32[]{:S(2)}) collective-permute-start(f32[2,16,384]{2,1,0:T(8,128)S(1)} %get-tuple-element.30), channel_id=1, source_target_pairs={{8,0},{16,8},{24,16},{32,24},{40,32},{48,40},{56,48},{64,56},{72,6... | collective-permute-start | bytes 147464 | tf_op jit(solution)/shard_map/ppermute | solution.py:57
  52.3 14.4 %collective-permute-start.9 = (f32[2,2,24,768]{3,2,1,0:T(8,128)S(1)}, f32[2,2,24,768]{3,2,1,0:T(8,128)S(1)}, u32[]{:S(2)}, u32[]{:S(2)}) collective-permute-start(f32[2,2,24,768]{3,2,1,0:T(8,128)S(1)} %get-tuple-element.51), channel_id=1, source_target_pairs={{384,0},{0,128},{128,256},{256,384},{385,1},{1,129},{129,257},{257... | collective-permute-start | bytes 884744 | tf_op jit(solution)/shard_map/ppermute | solution.py:57
  55.7 11.0 %collective-permute-start.10 = (f32[2,2,24,768]{3,2,1,0:T(8,128)S(1)}, f32[2,2,24,768]{3,2,1,0:T(8,128)S(1)}, u32[]{:S(2)}, u32[]{:S(2)}) collective-permute-start(f32[2,2,24,768]{3,2,1,0:T(8,128)S(1)} %get-tuple-element.50), channel_id=1, source_target_pairs={{128,0},{256,128},{384,256},{0,384},{129,1},{257,129},{385,257},{1... | collective-permute-start | bytes 884744 | tf_op jit(solution)/shard_map/ppermute | solution.py:57
  62.3 9.4 %collective-permute-start.7 = (f32[112,384]{1,0:T(8,128)S(1)}, f32[112,384]{1,0:T(8,128)S(1)}, u32[]{:S(2)}, u32[]{:S(2)}) collective-permute-start(f32[112,384]{1,0:T(8,128)S(1)} %pad_maximum_fusion), channel_id=1, source_target_pairs={{1,0},{2,1},{3,2},{4,3},{5,4},{6,5},{7,6},{0,7},{9,8},{10,9},{11,1... | collective-permute-start | bytes 516104 | tf_op jit(solution)/shard_map/ppermute | solution.py:57
  64.3 7.5 %collective-permute-start.8 = (f32[48,384]{1,0:T(8,128)S(1)}, f32[48,384]{1,0:T(8,128)S(1)}, u32[]{:S(2)}, u32[]{:S(2)}) collective-permute-start(f32[48,384]{1,0:T(8,128)S(1)} %slice_bitcast_fusion.1), channel_id=1, source_target_pairs={{7,0},{0,1},{1,2},{2,3},{3,4},{4,5},{5,6},{6,7},{15,8},{8,9},{9,10... | collective-permute-start | bytes 221192 | tf_op jit(solution)/shard_map/ppermute | solution.py:57
  73.7 9.0 %collective-permute-start.11 = (f32[2,16,384]{2,1,0:T(8,128)S(1)}, f32[2,16,384]{2,1,0:T(8,128)S(1)}, u32[]{:S(2)}, u32[]{:S(2)}) collective-permute-start(f32[2,16,384]{2,1,0:T(8,128)S(1)} %shard_map.84), channel_id=1, source_target_pairs={{120,0},{0,8},{8,16},{16,24},{24,32},{32,40},{40,48},{48,56},{56,6... | collective-permute-start | bytes 147464 | tf_op jit(solution)/shard_map/ppermute | solution.py:57
  80.7 12.0 %collective-permute-start.12 = (f32[2,16,384]{2,1,0:T(8,128)S(1)}, f32[2,16,384]{2,1,0:T(8,128)S(1)}, u32[]{:S(2)}, u32[]{:S(2)}) collective-permute-start(f32[2,16,384]{2,1,0:T(8,128)S(1)} %shard_map.84), channel_id=1, source_target_pairs={{8,0},{16,8},{24,16},{32,24},{40,32},{48,40},{56,48},{64,56},{72,6... | collective-permute-start | bytes 147464 | tf_op jit(solution)/shard_map/ppermute | solution.py:57
  92.7 9.4 %collective-permute-start.14 = (f32[96,384]{1,0:T(8,128)S(1)}, f32[96,384]{1,0:T(8,128)S(1)}, u32[]{:S(2)}, u32[]{:S(2)}) collective-permute-start(f32[96,384]{1,0:T(8,128)S(1)} %bitcast.41), channel_id=1, source_target_pairs={{1,0},{2,1},{3,2},{4,3},{5,4},{6,5},{7,6},{0,7},{9,8},{10,9},{11,1... | collective-permute-start | bytes 442376 | tf_op jit(solution)/shard_map/ppermute | solution.py:57
  94.7 7.5 %collective-permute-start.13 = (f32[48,384]{1,0:T(8,128)S(1)}, f32[48,384]{1,0:T(8,128)S(1)}, u32[]{:S(2)}, u32[]{:S(2)}) collective-permute-start(f32[48,384]{1,0:T(8,128)S(1)} %slice_bitcast_fusion), channel_id=1, source_target_pairs={{7,0},{0,1},{1,2},{2,3},{3,4},{4,5},{5,6},{6,7},{15,8},{8,9},{9,10... | collective-permute-start | bytes 221192 | tf_op jit(solution)/shard_map/ppermute | solution.py:57
  104.1 5.9 %collective-permute-start.15 = (f32[2,16,256]{2,1,0:T(8,128)S(1)}, f32[2,16,256]{2,1,0:T(8,128)S(1)}, u32[]{:S(2)}, u32[]{:S(2)}) collective-permute-start(f32[2,16,256]{2,1,0:T(8,128)S(1)} %shard_map.85), channel_id=1, source_target_pairs={{120,0},{0,8},{8,16},{16,24},{24,32},{32,40},{40,48},{48,56},{56,6... | collective-permute-start | bytes 98312 | tf_op jit(solution)/shard_map/ppermute | solution.py:57
  106.0 11.8 %collective-permute-start.16 = (f32[2,16,256]{2,1,0:T(8,128)S(1)}, f32[2,16,256]{2,1,0:T(8,128)S(1)}, u32[]{:S(2)}, u32[]{:S(2)}) collective-permute-start(f32[2,16,256]{2,1,0:T(8,128)S(1)} %shard_map.85), channel_id=1, source_target_pairs={{8,0},{16,8},{24,16},{32,24},{40,32},{48,40},{56,48},{64,56},{72,6... | collective-permute-start | bytes 98312 | tf_op jit(solution)/shard_map/ppermute | solution.py:57
  117.9 9.2 %collective-permute-start.18 = (f32[96,256]{1,0:T(8,128)S(1)}, f32[96,256]{1,0:T(8,128)S(1)}, u32[]{:S(2)}, u32[]{:S(2)}) collective-permute-start(f32[96,256]{1,0:T(8,128)S(1)} %bitcast.42), channel_id=1, source_target_pairs={{1,0},{2,1},{3,2},{4,3},{5,4},{6,5},{7,6},{0,7},{9,8},{10,9},{11,1... | collective-permute-start | bytes 294920 | tf_op jit(solution)/shard_map/ppermute | solution.py:57
  119.8 7.2 %collective-permute-start.17 = (f32[48,256]{1,0:T(8,128)S(1)}, f32[48,256]{1,0:T(8,128)S(1)}, u32[]{:S(2)}, u32[]{:S(2)}) collective-permute-start(f32[48,256]{1,0:T(8,128)S(1)} %slice_bitcast_fusion.2), channel_id=1, source_target_pairs={{7,0},{0,1},{1,2},{2,3},{3,4},{4,5},{5,6},{6,7},{15,8},{8,9},{9,10... | collective-permute-start | bytes 147464 | tf_op jit(solution)/shard_map/ppermute | solution.py:57

commit v4 on v3

--- a/solution.py
+++ b/solution.py
@@ -87,6 +87,10 @@
         compiler_params=pltpu.CompilerParams(vmem_limit_bytes=40 * 1024 * 1024),
         **options,
     )
+
+
+def streamed(*arrays):
+    return [pltpu.with_memory_space_constraint(a, pltpu.HBM) for a in arrays]
 
 
 def shape(*dims, dtype=F32):
@@ -241,7 +245,7 @@
             pl.BlockSpec((1024, 768), lambda i: (0, 0)),
         ],
         out_specs=(wide, wide, slim, slim, pl.BlockSpec((1, 2, 24, 768), lambda i: (i, 0, 0, 0))),
-    )(matrix, block, jnp.asarray(placement(), BF16))
+    )(*streamed(matrix, block, jnp.asarray(placement(), BF16)))
     return (
         ah.reshape(2, 160, 768), al.reshape(2, 160, 768),
         bh.reshape(2, 160, 128), bl.reshape(2, 160, 128), sent,
@@ -363,7 +367,6 @@
     weights = jnp.transpose(dof_weight[:, 0], (0, 2, 1, 3)).reshape(4, 24, 128)
     matrix = jnp.transpose(coarse_matrix[:, 0], (0, 2, 3, 1, 4)).reshape(4, 27, 72, 36)
     block = jnp.transpose(block_inverse[:, 0], (0, 2, 1, 3)).reshape(4, 72, 36)
-    inputs = (displacement[:, 0], weights, block, jnp.asarray(choice(), BF16))
     sums = call(
         numer_kernel,
         shape(2, 72, 128),
@@ -377,14 +380,15 @@
             pl.BlockSpec((512, 128), lambda i: (0, 0)),
         ],
         out_specs=pl.BlockSpec((2, 72, 128), lambda i: (0, 0, 0)),
-    )(*(pltpu.with_memory_space_constraint(a, pltpu.HBM) for a in inputs))
+    )(*streamed(displacement[:, 0], weights, block, jnp.asarray(choice(), BF16)))
     mine, left, right = sums, shifted(sums, "gx", 1), shifted(sums, "gx", -1)
     sides = (mine, left, right)
     sums, up = call(sum_x_kernel, (shape(2, 32, 384), shape(24, 384)))(*sides)
     left = shifted(up, "gz", 1)
     ah, al, bh, bl, sent = prepare(after(matrix, up), block)
     lower, upper, middle = call(sum_z_kernel, (shape(2, 8, 384),) * 3)(sums, left)
-    below, above = shifted(upper, "gy", 1), shifted(lower, "gy", -1)
+    below = shifted(upper, "gy", 1)
+    above = shifted(lower, "gy", -1)
     g, near, x, near_high, near_low = call(
         first_kernel,
         (shape(2, 16, 384), shape(2, 24, 256), shape(2, 16, 384)) + (shape(2, 192, 32, dtype=BF16),) * 2,

time: 129 us -> 129 us (level)
  local copies, waits for them, and re-layouts: 2.95 us -> 0.82 us
  Pallas kernels: 14.5 us -> 16.6 us
    pallas_call x1, Pallas kernels: 3.41 us -> 5.63 us  [prepare(): call(prepare_kernel, outs, (pltpu.VMEM((8, 72, 128), F32), pltpu.VMEM((16...]
    unnamed x8 -> x2, local copies, waits for them, and re-layouts: 2.15 us -> 0.01 us
  transfers between devices with their start and end apart: 19 -> 19, of which waited for: 10 -> 10; matrix products, arithmetic and copies ran while one was open for 1% -> 1% of each run, Pallas kernels for 3% -> 5%
where the time goes in v4:
time: 129 us
  starting transfers between devices  63.1 us (49%)
  waiting for transfers between devices  47 us (36%)
  Pallas kernels  16.6 us (13%)
    ppermute x19, starting transfers between devices, shifted(): lax.ppermute(block, axis, [((i - distance) % count, i) for i in range(cou...  63.1 us
    ppermute x19, waiting for transfers between devices, shifted(): lax.ppermute(block, axis, [((i - distance) % count, i) for i in range(cou...  47 us
    pallas_call x1, Pallas kernels, prepare(): call(prepare_kernel, outs, (pltpu.VMEM((8, 72, 128), F32), pltpu.VMEM((16...  5.63 us
    pallas_call x1, Pallas kernels, steps(): call(numer_kernel, shape(2, 72, 128), (pltpu.VMEM((4, 24, 128), F32), plt...  4.55 us
    pallas_call x2, Pallas kernels, steps(): call(functools.partial(sweep_kernel, 5 - sweep), shape(2, 16, 384 if swee...  3.83 us
  transfers between devices with their start and end apart: 19, of which 10 were waited for; matrix products, arithmetic and copies ran while one was open for 1% of the time, Pallas kernels for 5%

profile of v4, /device:TPU:56, one launch (start us, length us, event | category | flops | bytes accessed | tf_op | source)
XLA Modules:
  0.0 128.5 jit_solution(9166642551575584140)
XLA Ops:
  0.6 4.5 %shard_map.77.sums_ref.own_ref = f32[2,72,128]{2,1,0:T(8,128)S(1)} custom-call(bf16[4,2,12,3,32,128]{5,4,3,2,1,0:T(8,128)(2,1)} %bitcast.47, bf16[4,24,128]{2,1,0:T(8,128)(2,1)} %bitcast.52, f32[4,72,36]{2,1,0:T(8,128)} %bitcast.48, bf16[512,128]{1,0:T(8,128)(2,1)} %constant.4.clone.choice_ref), custom_call_target="tpu_custom_call" | custom-call | flops 20000000 | bytes 1000000 | tf_op jit(solution)/shard_map/pallas_call | solution.py:370
  5.2 3.4 %collective-permute-start = (f32[2,72,128]{2,1,0:T(8,128)S(1)}, f32[2,72,128]{2,1,0:T(8,128)S(1)}, u32[]{:S(2)}, u32[]{:S(2)}) collective-permute-start(f32[2,72,128]{2,1,0:T(8,128)S(1)} %shard_map.77.sums_ref.own_ref), channel_id=1, source_target_pairs={{384,0},{0,128},{128,256},{256,384},{385,1},{1,129},{129,257},{257... | collective-permute-start | bytes 221192 | tf_op jit(solution)/shard_map/ppermute | solution.py:57
  8.6 3.7 %collective-permute-start.1 = (f32[2,72,128]{2,1,0:T(8,128)S(1)}, f32[2,72,128]{2,1,0:T(8,128)S(1)}, u32[]{:S(2)}, u32[]{:S(2)}) collective-permute-start(f32[2,72,128]{2,1,0:T(8,128)S(1)} %shard_map.77.sums_ref.own_ref), channel_id=1, source_target_pairs={{128,0},{256,128},{384,256},{0,384},{129,1},{257,129},{385,257},{1... | collective-permute-start | bytes 221192 | tf_op jit(solution)/shard_map/ppermute | solution.py:57
  12.6 2.2 %collective-permute-done.1.right_ref = f32[2,72,128]{2,1,0:T(8,128)S(1)} collective-permute-done((f32[2,72,128]{2,1,0:T(8,128)S(1)}, f32[2,72,128]{2,1,0:T(8,128)S(1)}, u32[]{:S(2)}, u32[]{:S(2)}) %collective-permute-start.1) | collective-permute-done | bytes 73760 | tf_op jit(solution)/shard_map/ppermute | solution.py:57
  14.9 1.9 %collective-permute-start.2 = (f32[24,384]{1,0:T(8,128)S(1)}, f32[24,384]{1,0:T(8,128)S(1)}, u32[]{:S(2)}, u32[]{:S(2)}) collective-permute-start(f32[24,384]{1,0:T(8,128)S(1)} %get-tuple-element.25), channel_id=1, source_target_pairs={{7,0},{0,1},{1,2},{2,3},{3,4},{4,5},{5,6},{6,7},{15,8},{8,9},{9,10... | collective-permute-start | bytes 110600 | tf_op jit(solution)/shard_map/ppermute | solution.py:57
  16.9 5.6 %collective-permute-done.2.left_ref = f32[24,384]{1,0:T(8,128)S(1)} collective-permute-done((f32[24,384]{1,0:T(8,128)S(1)}, f32[24,384]{1,0:T(8,128)S(1)}, u32[]{:S(2)}, u32[]{:S(2)}) %collective-permute-start.2) | collective-permute-done | bytes 36896 | tf_op jit(solution)/shard_map/ppermute | solution.py:57
  22.5 9.7 %collective-permute-start.3 = (f32[2,8,384]{2,1,0:T(8,128)S(1)}, f32[2,8,384]{2,1,0:T(8,128)S(1)}, u32[]{:S(2)}, u32[]{:S(2)}) collective-permute-start(f32[2,8,384]{2,1,0:T(8,128)S(1)} %get-tuple-element.27.upper_ref), channel_id=1, source_target_pairs={{120,0},{0,8},{8,16},{16,24},{24,32},{32,40},{40,48},{48,56},{56,6... | collective-permute-start | bytes 73736 | tf_op jit(solution)/shard_map/ppermute | solution.py:57
  32.1 1.9 %collective-permute-start.4 = (f32[2,8,384]{2,1,0:T(8,128)S(1)}, f32[2,8,384]{2,1,0:T(8,128)S(1)}, u32[]{:S(2)}, u32[]{:S(2)}) collective-permute-start(f32[2,8,384]{2,1,0:T(8,128)S(1)} %get-tuple-element.26.lower_ref), channel_id=1, source_target_pairs={{8,0},{16,8},{24,16},{32,24},{40,32},{48,40},{56,48},{64,56},{72,6... | collective-permute-start | bytes 73736 | tf_op jit(solution)/shard_map/ppermute | solution.py:57
  34.1 5.6 %shard_map.82 = (bf16[2,4,40,768]{3,2,1,0:T(8,128)(2,1)S(1)}, bf16[2,4,40,768]{3,2,1,0:T(8,128)(2,1)S(1)}, bf16[2,4,40,128]{3,2,1,0:T(8,128)(2,1)S(1)}, bf16[2,4...) custom-call(f32[4,27,72,36]{3,2,1,0:T(8,128)} %bitcast.46, f32[4,72,36]{2,1,0:T(8,128)} %bitcast.49, ...), custom_call_target="tpu_custom_call" | custom-call | flops 20000000 | bytes 1000000 | tf_op jit(solution)/shard_map/pallas_call | solution.py:232
  39.7 4.2 %collective-permute-done.4.above_ref = f32[2,8,384]{2,1,0:T(8,128)S(1)} collective-permute-done((f32[2,8,384]{2,1,0:T(8,128)S(1)}, f32[2,8,384]{2,1,0:T(8,128)S(1)}, u32[]{:S(2)}, u32[]{:S(2)}) %collective-permute-start.4) | collective-permute-done | bytes 24608 | tf_op jit(solution)/shard_map/ppermute | solution.py:57
  44.5 5.8 %collective-permute-start.5 = (f32[2,16,384]{2,1,0:T(8,128)S(1)}, f32[2,16,384]{2,1,0:T(8,128)S(1)}, u32[]{:S(2)}, u32[]{:S(2)}) collective-permute-start(f32[2,16,384]{2,1,0:T(8,128)S(1)} %get-tuple-element.30), channel_id=1, source_target_pairs={{120,0},{0,8},{8,16},{16,24},{24,32},{32,40},{40,48},{48,56},{56,6... | collective-permute-start | bytes 147464 | tf_op jit(solution)/shard_map/ppermute | solution.py:57
  50.2 1.9 %collective-permute-start.6 = (f32[2,16,384]{2,1,0:T(8,128)S(1)}, f32[2,16,384]{2,1,0:T(8,128)S(1)}, u32[]{:S(2)}, u32[]{:S(2)}) collective-permute-start(f32[2,16,384]{2,1,0:T(8,128)S(1)} %get-tuple-element.30), channel_id=1, source_target_pairs={{8,0},{16,8},{24,16},{32,24},{40,32},{48,40},{56,48},{64,56},{72,6... | collective-permute-start | bytes 147464 | tf_op jit(solution)/shard_map/ppermute | solution.py:57
  52.2 3.4 %collective-permute-start.9 = (f32[2,2,24,768]{3,2,1,0:T(8,128)S(1)}, f32[2,2,24,768]{3,2,1,0:T(8,128)S(1)}, u32[]{:S(2)}, u32[]{:S(2)}) collective-permute-start(f32[2,2,24,768]{3,2,1,0:T(8,128)S(1)} %get-tuple-element.51), channel_id=1, source_target_pairs={{384,0},{0,128},{128,256},{256,384},{385,1},{1,129},{129,257},{257... | collective-permute-start | bytes 884744 | tf_op jit(solution)/shard_map/ppermute | solution.py:57
  55.6 3.7 %collective-permute-start.10 = (f32[2,2,24,768]{3,2,1,0:T(8,128)S(1)}, f32[2,2,24,768]{3,2,1,0:T(8,128)S(1)}, u32[]{:S(2)}, u32[]{:S(2)}) collective-permute-start(f32[2,2,24,768]{3,2,1,0:T(8,128)S(1)} %get-tuple-element.50), channel_id=1, source_target_pairs={{128,0},{256,128},{384,256},{0,384},{129,1},{257,129},{385,257},{1... | collective-permute-start | bytes 884744 | tf_op jit(solution)/shard_map/ppermute | solution.py:57
  59.3 2.9 %collective-permute-done.6 = f32[2,16,384]{2,1,0:T(8,128)S(1)} collective-permute-done((f32[2,16,384]{2,1,0:T(8,128)S(1)}, f32[2,16,384]{2,1,0:T(8,128)S(1)}, u32[]{:S(2)}, u32[]{:S(2)}) %collective-permute-start.6) | collective-permute-done | bytes 49184 | tf_op jit(solution)/shard_map/ppermute | solution.py:57
  62.3 1.9 %collective-permute-start.7 = (f32[112,384]{1,0:T(8,128)S(1)}, f32[112,384]{1,0:T(8,128)S(1)}, u32[]{:S(2)}, u32[]{:S(2)}) collective-permute-start(f32[112,384]{1,0:T(8,128)S(1)} %pad_maximum_fusion), channel_id=1, source_target_pairs={{1,0},{2,1},{3,2},{4,3},{5,4},{6,5},{7,6},{0,7},{9,8},{10,9},{11,1... | collective-permute-start | bytes 516104 | tf_op jit(solution)/shard_map/ppermute | solution.py:57
  64.2 2.4 %collective-permute-start.8 = (f32[48,384]{1,0:T(8,128)S(1)}, f32[48,384]{1,0:T(8,128)S(1)}, u32[]{:S(2)}, u32[]{:S(2)}) collective-permute-start(f32[48,384]{1,0:T(8,128)S(1)} %slice_bitcast_fusion.1), channel_id=1, source_target_pairs={{7,0},{0,1},{1,2},{2,3},{3,4},{4,5},{5,6},{6,7},{15,8},{8,9},{9,10... | collective-permute-start | bytes 221192 | tf_op jit(solution)/shard_map/ppermute | solution.py:57
  66.9 4.8 %collective-permute-done.8.left_ref = f32[48,384]{1,0:T(8,128)S(1)} collective-permute-done((f32[48,384]{1,0:T(8,128)S(1)}, f32[48,384]{1,0:T(8,128)S(1)}, u32[]{:S(2)}, u32[]{:S(2)}) %collective-permute-start.8) | collective-permute-done | bytes 73760 | tf_op jit(solution)/shard_map/ppermute | solution.py:57
  71.7 1.9 %shard_map.84 = f32[2,16,384]{2,1,0:T(8,128)S(1)} custom-call(f32[2,48,384]{2,1,0:T(8,128)S(1)} %constant_dynamic-update-slice_fusion.own_ref, f32[48,384]{1,0:T(8,128)S(1)} %collective-permute-done.8.left_ref, f32[112,384]{1,0:T(8,128)S(1)} %collective-permute-done.7.right_ref, f32[2,24,256]{2,1,0:T(8,128)S(1)} %get-tuple-element.32.g_ref, ...), custom_call_target="tpu_custom_call" | custom-call | flops 20000000 | bytes 1000000 | tf_op jit(solution)/shard_map/pallas_call | solution.py:418
  73.6 7.1 %collective-permute-start.11 = (f32[2,16,384]{2,1,0:T(8,128)S(1)}, f32[2,16,384]{2,1,0:T(8,128)S(1)}, u32[]{:S(2)}, u32[]{:S(2)}) collective-permute-start(f32[2,16,384]{2,1,0:T(8,128)S(1)} %shard_map.84), channel_id=1, source_target_pairs={{120,0},{0,8},{8,16},{16,24},{24,32},{32,40},{40,48},{48,56},{56,6... | collective-permute-start | bytes 147464 | tf_op jit(solution)/shard_map/ppermute | solution.py:57
  80.6 1.9 %collective-permute-start.12 = (f32[2,16,384]{2,1,0:T(8,128)S(1)}, f32[2,16,384]{2,1,0:T(8,128)S(1)}, u32[]{:S(2)}, u32[]{:S(2)}) collective-permute-start(f32[2,16,384]{2,1,0:T(8,128)S(1)} %shard_map.84), channel_id=1, source_target_pairs={{8,0},{16,8},{24,16},{32,24},{40,32},{48,40},{56,48},{64,56},{72,6... | collective-permute-start | bytes 147464 | tf_op jit(solution)/shard_map/ppermute | solution.py:57
  82.6 10.1 %collective-permute-done.12 = f32[2,16,384]{2,1,0:T(8,128)S(1)} collective-permute-done((f32[2,16,384]{2,1,0:T(8,128)S(1)}, f32[2,16,384]{2,1,0:T(8,128)S(1)}, u32[]{:S(2)}, u32[]{:S(2)}) %collective-permute-start.12) | collective-permute-done | bytes 49184 | tf_op jit(solution)/shard_map/ppermute | solution.py:57
  92.7 1.9 %collective-permute-start.14 = (f32[96,384]{1,0:T(8,128)S(1)}, f32[96,384]{1,0:T(8,128)S(1)}, u32[]{:S(2)}, u32[]{:S(2)}) collective-permute-start(f32[96,384]{1,0:T(8,128)S(1)} %bitcast.40), channel_id=1, source_target_pairs={{1,0},{2,1},{3,2},{4,3},{5,4},{6,5},{7,6},{0,7},{9,8},{10,9},{11,1... | collective-permute-start | bytes 442376 | tf_op jit(solution)/shard_map/ppermute | solution.py:57
  94.6 2.4 %collective-permute-start.13 = (f32[48,384]{1,0:T(8,128)S(1)}, f32[48,384]{1,0:T(8,128)S(1)}, u32[]{:S(2)}, u32[]{:S(2)}) collective-permute-start(f32[48,384]{1,0:T(8,128)S(1)} %slice_bitcast_fusion), channel_id=1, source_target_pairs={{7,0},{0,1},{1,2},{2,3},{3,4},{4,5},{5,6},{6,7},{15,8},{8,9},{9,10... | collective-permute-start | bytes 221192 | tf_op jit(solution)/shard_map/ppermute | solution.py:57
  97.0 5.1 %collective-permute-done.13.left_ref = f32[48,384]{1,0:T(8,128)S(1)} collective-permute-done((f32[48,384]{1,0:T(8,128)S(1)}, f32[48,384]{1,0:T(8,128)S(1)}, u32[]{:S(2)}, u32[]{:S(2)}) %collective-permute-start.13) | collective-permute-done | bytes 73760 | tf_op jit(solution)/shard_map/ppermute | solution.py:57
  102.1 1.9 %shard_map.85 = f32[2,16,256]{2,1,0:T(8,128)S(1)} custom-call(f32[2,48,384]{2,1,0:T(8,128)S(1)} %pad_maximum_fusion.1.own_ref, f32[48,384]{1,0:T(8,128)S(1)} %collective-permute-done.13.left_ref, f32[96,384]{1,0:T(8,128)S(1)} %collective-permute-done.14.right_ref, f32[2,24,256]{2,1,0:T(8,128)S(1)} %get-tuple-element.32.g_ref, ...), custom_call_target="tpu_custom_call" | custom-call | flops 20000000 | bytes 1000000 | tf_op jit(solution)/shard_map/pallas_call | solution.py:418
  104.0 1.9 %collective-permute-start.15 = (f32[2,16,256]{2,1,0:T(8,128)S(1)}, f32[2,16,256]{2,1,0:T(8,128)S(1)}, u32[]{:S(2)}, u32[]{:S(2)}) collective-permute-start(f32[2,16,256]{2,1,0:T(8,128)S(1)} %shard_map.85), channel_id=1, source_target_pairs={{120,0},{0,8},{8,16},{16,24},{24,32},{32,40},{40,48},{48,56},{56,6... | collective-permute-start | bytes 98312 | tf_op jit(solution)/shard_map/ppermute | solution.py:57
  106.0 3.9 %collective-permute-start.16 = (f32[2,16,256]{2,1,0:T(8,128)S(1)}, f32[2,16,256]{2,1,0:T(8,128)S(1)}, u32[]{:S(2)}, u32[]{:S(2)}) collective-permute-start(f32[2,16,256]{2,1,0:T(8,128)S(1)} %shard_map.85), channel_id=1, source_target_pairs={{8,0},{16,8},{24,16},{32,24},{40,32},{48,40},{56,48},{64,56},{72,6... | collective-permute-start | bytes 98312 | tf_op jit(solution)/shard_map/ppermute | solution.py:57
  109.9 7.9 %collective-permute-done.16 = f32[2,16,256]{2,1,0:T(8,128)S(1)} collective-permute-done((f32[2,16,256]{2,1,0:T(8,128)S(1)}, f32[2,16,256]{2,1,0:T(8,128)S(1)}, u32[]{:S(2)}, u32[]{:S(2)}) %collective-permute-start.16) | collective-permute-done | bytes 32800 | tf_op jit(solution)/shard_map/ppermute | solution.py:57
  117.8 1.9 %collective-permute-start.18 = (f32[96,256]{1,0:T(8,128)S(1)}, f32[96,256]{1,0:T(8,128)S(1)}, u32[]{:S(2)}, u32[]{:S(2)}) collective-permute-start(f32[96,256]{1,0:T(8,128)S(1)} %bitcast.41), channel_id=1, source_target_pairs={{1,0},{2,1},{3,2},{4,3},{5,4},{6,5},{7,6},{0,7},{9,8},{10,9},{11,1... | collective-permute-start | bytes 294920 | tf_op jit(solution)/shard_map/ppermute | solution.py:57
  119.7 2.4 %collective-permute-start.17 = (f32[48,256]{1,0:T(8,128)S(1)}, f32[48,256]{1,0:T(8,128)S(1)}, u32[]{:S(2)}, u32[]{:S(2)}) collective-permute-start(f32[48,256]{1,0:T(8,128)S(1)} %slice_bitcast_fusion.2), channel_id=1, source_target_pairs={{7,0},{0,1},{1,2},{2,3},{3,4},{4,5},{5,6},{6,7},{15,8},{8,9},{9,10... | collective-permute-start | bytes 147464 | tf_op jit(solution)/shard_map/ppermute | solution.py:57
  123.1 3.9 %collective-permute-done.17.left_ref = f32[48,256]{1,0:T(8,128)S(1)} collective-permute-done((f32[48,256]{1,0:T(8,128)S(1)}, f32[48,256]{1,0:T(8,128)S(1)}, u32[]{:S(2)}, u32[]{:S(2)}) %collective-permute-start.17) | collective-permute-done | bytes 49184 | tf_op jit(solution)/shard_map/ppermute | solution.py:57
  (28 shorter events, 3.9 us)
Async XLA Ops:
  5.2 7.5 %collective-permute-start = (f32[2,72,128]{2,1,0:T(8,128)S(1)}, f32[2,72,128]{2,1,0:T(8,128)S(1)}, u32[]{:S(2)}, u32[]{:S(2)}) collective-permute-start(f32[2,72,128]{2,1,0:T(8,128)S(1)} %shard_map.77.sums_ref.own_ref), channel_id=1, source_target_pairs={{384,0},{0,128},{128,256},{256,384},{385,1},{1,129},{129,257},{257... | collective-permute-start | bytes 221192 | tf_op jit(solution)/shard_map/ppermute | solution.py:57
  8.6 6.2 %collective-permute-start.1 = (f32[2,72,128]{2,1,0:T(8,128)S(1)}, f32[2,72,128]{2,1,0:T(8,128)S(1)}, u32[]{:S(2)}, u32[]{:S(2)}) collective-permute-start(f32[2,72,128]{2,1,0:T(8,128)S(1)} %shard_map.77.sums_ref.own_ref), channel_id=1, source_target_pairs={{128,0},{256,128},{384,256},{0,384},{129,1},{257,129},{385,257},{1... | collective-permute-start | bytes 221192 | tf_op jit(solution)/shard_map/ppermute | solution.py:57
  14.9 7.5 %collective-permute-start.2 = (f32[24,384]{1,0:T(8,128)S(1)}, f32[24,384]{1,0:T(8,128)S(1)}, u32[]{:S(2)}, u32[]{:S(2)}) collective-permute-start(f32[24,384]{1,0:T(8,128)S(1)} %get-tuple-element.25), channel_id=1, source_target_pairs={{7,0},{0,1},{1,2},{2,3},{3,4},{4,5},{5,6},{6,7},{15,8},{8,9},{9,10... | collective-permute-start | bytes 110600 | tf_op jit(solution)/shard_map/ppermute | solution.py:57
  22.5 17.2 %collective-permute-start.3 = (f32[2,8,384]{2,1,0:T(8,128)S(1)}, f32[2,8,384]{2,1,0:T(8,128)S(1)}, u32[]{:S(2)}, u32[]{:S(2)}) collective-permute-start(f32[2,8,384]{2,1,0:T(8,128)S(1)} %get-tuple-element.27.upper_ref), channel_id=1, source_target_pairs={{120,0},{0,8},{8,16},{16,24},{24,32},{32,40},{40,48},{48,56},{56,6... | collective-permute-start | bytes 73736 | tf_op jit(solution)/shard_map/ppermute | solution.py:57
  32.1 11.7 %collective-permute-start.4 = (f32[2,8,384]{2,1,0:T(8,128)S(1)}, f32[2,8,384]{2,1,0:T(8,128)S(1)}, u32[]{:S(2)}, u32[]{:S(2)}) collective-permute-start(f32[2,8,384]{2,1,0:T(8,128)S(1)} %get-tuple-element.26.lower_ref), channel_id=1, source_target_pairs={{8,0},{16,8},{24,16},{32,24},{40,32},{48,40},{56,48},{64,56},{72,6... | collective-permute-start | bytes 73736 | tf_op jit(solution)/shard_map/ppermute | solution.py:57
  44.5 14.9 %collective-permute-start.5 = (f32[2,16,384]{2,1,0:T(8,128)S(1)}, f32[2,16,384]{2,1,0:T(8,128)S(1)}, u32[]{:S(2)}, u32[]{:S(2)}) collective-permute-start(f32[2,16,384]{2,1,0:T(8,128)S(1)} %get-tuple-element.30), channel_id=1, source_target_pairs={{120,0},{0,8},{8,16},{16,24},{24,32},{32,40},{40,48},{48,56},{56,6... | collective-permute-start | bytes 147464 | tf_op jit(solution)/shard_map/ppermute | solution.py:57
  50.2 12.0 %collective-permute-start.6 = (f32[2,16,384]{2,1,0:T(8,128)S(1)}, f32[2,16,384]{2,1,0:T(8,128)S(1)}, u32[]{:S(2)}, u32[]{:S(2)}) collective-permute-start(f32[2,16,384]{2,1,0:T(8,128)S(1)} %get-tuple-element.30), channel_id=1, source_target_pairs={{8,0},{16,8},{24,16},{32,24},{40,32},{48,40},{56,48},{64,56},{72,6... | collective-permute-start | bytes 147464 | tf_op jit(solution)/shard_map/ppermute | solution.py:57
  52.2 14.4 %collective-permute-start.9 = (f32[2,2,24,768]{3,2,1,0:T(8,128)S(1)}, f32[2,2,24,768]{3,2,1,0:T(8,128)S(1)}, u32[]{:S(2)}, u32[]{:S(2)}) collective-permute-start(f32[2,2,24,768]{3,2,1,0:T(8,128)S(1)} %get-tuple-element.51), channel_id=1, source_target_pairs={{384,0},{0,128},{128,256},{256,384},{385,1},{1,129},{129,257},{257... | collective-permute-start | bytes 884744 | tf_op jit(solution)/shard_map/ppermute | solution.py:57
  55.6 11.0 %collective-permute-start.10 = (f32[2,2,24,768]{3,2,1,0:T(8,128)S(1)}, f32[2,2,24,768]{3,2,1,0:T(8,128)S(1)}, u32[]{:S(2)}, u32[]{:S(2)}) collective-permute-start(f32[2,2,24,768]{3,2,1,0:T(8,128)S(1)} %get-tuple-element.50), channel_id=1, source_target_pairs={{128,0},{256,128},{384,256},{0,384},{129,1},{257,129},{385,257},{1... | collective-permute-start | bytes 884744 | tf_op jit(solution)/shard_map/ppermute | solution.py:57
  62.3 9.4 %collective-permute-start.7 = (f32[112,384]{1,0:T(8,128)S(1)}, f32[112,384]{1,0:T(8,128)S(1)}, u32[]{:S(2)}, u32[]{:S(2)}) collective-permute-start(f32[112,384]{1,0:T(8,128)S(1)} %pad_maximum_fusion), channel_id=1, source_target_pairs={{1,0},{2,1},{3,2},{4,3},{5,4},{6,5},{7,6},{0,7},{9,8},{10,9},{11,1... | collective-permute-start | bytes 516104 | tf_op jit(solution)/shard_map/ppermute | solution.py:57
  64.2 7.5 %collective-permute-start.8 = (f32[48,384]{1,0:T(8,128)S(1)}, f32[48,384]{1,0:T(8,128)S(1)}, u32[]{:S(2)}, u32[]{:S(2)}) collective-permute-start(f32[48,384]{1,0:T(8,128)S(1)} %slice_bitcast_fusion.1), channel_id=1, source_target_pairs={{7,0},{0,1},{1,2},{2,3},{3,4},{4,5},{5,6},{6,7},{15,8},{8,9},{9,10... | collective-permute-start | bytes 221192 | tf_op jit(solution)/shard_map/ppermute | solution.py:57
  73.6 9.0 %collective-permute-start.11 = (f32[2,16,384]{2,1,0:T(8,128)S(1)}, f32[2,16,384]{2,1,0:T(8,128)S(1)}, u32[]{:S(2)}, u32[]{:S(2)}) collective-permute-start(f32[2,16,384]{2,1,0:T(8,128)S(1)} %shard_map.84), channel_id=1, source_target_pairs={{120,0},{0,8},{8,16},{16,24},{24,32},{32,40},{40,48},{48,56},{56,6... | collective-permute-start | bytes 147464 | tf_op jit(solution)/shard_map/ppermute | solution.py:57
  80.6 12.0 %collective-permute-start.12 = (f32[2,16,384]{2,1,0:T(8,128)S(1)}, f32[2,16,384]{2,1,0:T(8,128)S(1)}, u32[]{:S(2)}, u32[]{:S(2)}) collective-permute-start(f32[2,16,384]{2,1,0:T(8,128)S(1)} %shard_map.84), channel_id=1, source_target_pairs={{8,0},{16,8},{24,16},{32,24},{40,32},{48,40},{56,48},{64,56},{72,6... | collective-permute-start | bytes 147464 | tf_op jit(solution)/shard_map/ppermute | solution.py:57
  92.7 9.4 %collective-permute-start.14 = (f32[96,384]{1,0:T(8,128)S(1)}, f32[96,384]{1,0:T(8,128)S(1)}, u32[]{:S(2)}, u32[]{:S(2)}) collective-permute-start(f32[96,384]{1,0:T(8,128)S(1)} %bitcast.40), channel_id=1, source_target_pairs={{1,0},{2,1},{3,2},{4,3},{5,4},{6,5},{7,6},{0,7},{9,8},{10,9},{11,1... | collective-permute-start | bytes 442376 | tf_op jit(solution)/shard_map/ppermute | solution.py:57
  94.6 7.5 %collective-permute-start.13 = (f32[48,384]{1,0:T(8,128)S(1)}, f32[48,384]{1,0:T(8,128)S(1)}, u32[]{:S(2)}, u32[]{:S(2)}) collective-permute-start(f32[48,384]{1,0:T(8,128)S(1)} %slice_bitcast_fusion), channel_id=1, source_target_pairs={{7,0},{0,1},{1,2},{2,3},{3,4},{4,5},{5,6},{6,7},{15,8},{8,9},{9,10... | collective-permute-start | bytes 221192 | tf_op jit(solution)/shard_map/ppermute | solution.py:57
  104.0 5.9 %collective-permute-start.15 = (f32[2,16,256]{2,1,0:T(8,128)S(1)}, f32[2,16,256]{2,1,0:T(8,128)S(1)}, u32[]{:S(2)}, u32[]{:S(2)}) collective-permute-start(f32[2,16,256]{2,1,0:T(8,128)S(1)} %shard_map.85), channel_id=1, source_target_pairs={{120,0},{0,8},{8,16},{16,24},{24,32},{32,40},{40,48},{48,56},{56,6... | collective-permute-start | bytes 98312 | tf_op jit(solution)/shard_map/ppermute | solution.py:57
  106.0 11.8 %collective-permute-start.16 = (f32[2,16,256]{2,1,0:T(8,128)S(1)}, f32[2,16,256]{2,1,0:T(8,128)S(1)}, u32[]{:S(2)}, u32[]{:S(2)}) collective-permute-start(f32[2,16,256]{2,1,0:T(8,128)S(1)} %shard_map.85), channel_id=1, source_target_pairs={{8,0},{16,8},{24,16},{32,24},{40,32},{48,40},{56,48},{64,56},{72,6... | collective-permute-start | bytes 98312 | tf_op jit(solution)/shard_map/ppermute | solution.py:57
  117.8 9.2 %collective-permute-start.18 = (f32[96,256]{1,0:T(8,128)S(1)}, f32[96,256]{1,0:T(8,128)S(1)}, u32[]{:S(2)}, u32[]{:S(2)}) collective-permute-start(f32[96,256]{1,0:T(8,128)S(1)} %bitcast.41), channel_id=1, source_target_pairs={{1,0},{2,1},{3,2},{4,3},{5,4},{6,5},{7,6},{0,7},{9,8},{10,9},{11,1... | collective-permute-start | bytes 294920 | tf_op jit(solution)/shard_map/ppermute | solution.py:57
  119.7 7.2 %collective-permute-start.17 = (f32[48,256]{1,0:T(8,128)S(1)}, f32[48,256]{1,0:T(8,128)S(1)}, u32[]{:S(2)}, u32[]{:S(2)}) collective-permute-start(f32[48,256]{1,0:T(8,128)S(1)} %slice_bitcast_fusion.2), channel_id=1, source_target_pairs={{7,0},{0,1},{1,2},{2,3},{3,4},{4,5},{5,6},{6,7},{15,8},{8,9},{9,10... | collective-permute-start | bytes 147464 | tf_op jit(solution)/shard_map/ppermute | solution.py:57

commit v5 on v4

--- a/solution.py
+++ b/solution.py
@@ -26,9 +26,9 @@
 
 
 def placement():
-    table = np.zeros((1024, 768), np.float32)
-    for offset in range(27):
-        dx, dy, dz = offset // 9 - 1, offset // 3 % 3 - 1, offset % 3 - 1
+    table = np.zeros((384, 384), np.float32)
+    for offset in range(9):
+        dy, dz = offset // 3 - 1, offset % 3 - 1
         for edge in range(12):
             ox, oy, oz = OFFSETS[edge]
             direction = edge // 4
@@ -39,7 +39,7 @@
                 group, slot = {-1: (1, base), 0: (0, base), 1: (0, base + 1), 2: (2, base + 1)}[dy + oy]
             for comp in range(3):
                 row = 16 * group + 3 * slot + comp
-                table[36 * offset + 3 * edge + comp, 192 * (dx + ox + 1) + 48 * (dz + oz + 1) + row] = 1.0
+                table[36 * offset + 3 * edge + comp, 192 * ox + 48 * (dz + oz + 1) + row] = 1.0
     return table
 
 
@@ -97,36 +97,133 @@
     return jax.ShapeDtypeStruct(dims, dtype)
 
 
-def numer_kernel(disp_ref, weight_ref, block_ref, choice_ref, sums_ref, weights, packed, rows):
+def pick(rows_ref, value):
+    rows_ref[...] = value
+    return [rows_ref[3 * edge : 3 * edge + 3] for edge in WIDE_EDGES]
+
+
+def take_sums(step, disp_ref, weights, held):
+    ones = jnp.ones((128, 128), BF16)
+    group = (lanes((4, 512)) % 128) // 32
+    keep = group == lax.broadcasted_iota(jnp.int32, (4, 512), 0)
+    for z in range(2):
+        pieces = []
+        for edge in range(3):
+            parts = [disp_ref[x, z, edge, c] for c in range(3) for x in range(4)]
+            right = jnp.concatenate(parts + [ones], axis=0)
+            at = 6 * step + 2 * edge + z
+            left = jnp.concatenate([weights[x, pl.ds(at, 1), :] for x in range(4)], axis=0).astype(BF16)
+            found = lax.dot_general(left, right, (((1,), (1,)), ((), ())), preferred_element_type=F32)
+            row = jnp.sum(jnp.where(keep, found, 0.0), axis=0, keepdims=True)
+            pieces = pieces + [row[:, 128 * c : 128 * c + 128] for c in range(4)]
+        held[step, z, 0:12] = jnp.concatenate(pieces, axis=0)
+
+
+def take_operator(matrix_ref, place_ref, ah_ref, al_ref, sent_ref, packed, stacked, full):
+    for offset in range(27):
+        start, tile = 36 * (offset % 9) % 128, 3 * (offset // 9) + 36 * (offset % 9) // 128
+        size = min(36, 128 - start)
+        packed[tile, :, start : start + size] = matrix_ref[0, offset, :, 0:size]
+        if size < 36:
+            packed[tile + 1, :, 0 : 36 - size] = matrix_ref[0, offset, :, size:36]
+    pad = jnp.zeros((4, 384), BF16)
+    found = []
+    for dx in range(3):
+        for z in range(2):
+            high, low = split(
+                jnp.concatenate([packed[3 * dx + k, pl.ds(z, 36, stride=2), :] for k in range(3)], axis=1)
+            )
+            stacked[40 * z : 40 * z + 40] = jnp.concatenate([high, pad], axis=0)
+            stacked[80 + 40 * z : 120 + 40 * z] = jnp.concatenate([low, pad], axis=0)
+        found.append(dot(stacked[...], place_ref[...]))
+    none = jnp.zeros((160, 384), F32)
+    total = jnp.concatenate([found[0], found[2]], axis=1)
+    total = total + pltpu.roll(jnp.concatenate([found[1], none], axis=1), 192, 1)
+    for z in range(2):
+        high, low = total[40 * z : 40 * z + 40], total[80 + 40 * z : 120 + 40 * z]
+        ah_ref[z, 0] = high.astype(BF16)
+        al_ref[z, 0] = low.astype(BF16)
+        for place, value in enumerate(pick(full, high + low)):
+            sent_ref[0, z, 3 * place : 3 * place + 3] = value
+
+
+def start_kernel(
+    disp_ref, weight_ref, block_ref, choice_ref, matrix_ref, place_ref,
+    sums_ref, ah_ref, al_ref, bh_ref, bl_ref, sent_ref,
+    weights, inner, rows, held, packed, stacked, full,
+):
     step = pl.program_id(0)
 
     @pl.when(step == 0)
     def _():
         weights[...] = weight_ref[...].astype(F32)
-        packed[...] = jnp.zeros((4, 72, 128), F32)
+        inner[...] = jnp.zeros((4, 72, 128), F32)
+        for tile in range(9):
+            packed[tile] = jnp.zeros((72, 128), F32)
         for x in range(4):
-            packed[x, :, 0:36] = block_ref[x]
+            inner[x, :, 0:36] = block_ref[x]
         for z in range(2):
-            value = jnp.concatenate([packed[x, pl.ds(z, 36, stride=2), :] for x in range(4)], axis=1)
+            value = jnp.concatenate([inner[x, pl.ds(z, 36, stride=2), :] for x in range(4)], axis=1)
             high, low = split(value)
             rows[0:36] = dot(high, choice_ref[...]) + dot(low, choice_ref[...])
             for place, edge in enumerate(WIDE_EDGES):
                 sums_ref[z, 48 + 3 * place : 51 + 3 * place] = rows[3 * edge : 3 * edge + 3]
 
-    ones = jnp.ones((128, 128), BF16)
-    group = (lanes((4, 512)) % 128) // 32
-    keep = group == lax.broadcasted_iota(jnp.int32, (4, 512), 0)
-    for z in range(2):
-        pieces = []
-        for edge in range(2):
-            parts = [disp_ref[x, z, edge, c] for c in range(3) for x in range(4)]
-            right = jnp.concatenate(parts + [ones], axis=0)
-            at = 4 * step + 2 * edge + z
-            left = jnp.concatenate([weights[x, pl.ds(at, 1), :] for x in range(4)], axis=0).astype(BF16)
-            found = lax.dot_general(left, right, (((1,), (1,)), ((), ())), preferred_element_type=F32)
-            row = jnp.sum(jnp.where(keep, found, 0.0), axis=0, keepdims=True)
-            pieces = pieces + [row[:, 128 * c : 128 * c + 128] for c in range(4)]
-        sums_ref[z, pl.ds(pl.multiple_of(8 * step, 8), 8), :] = jnp.concatenate(pieces, axis=0)
+    take_sums(step, disp_ref, weights, held)
+    take_operator(matrix_ref, place_ref, ah_ref, al_ref, sent_ref, packed, stacked, full)
+    for z in range(2):
+        high, low = split(inner[step, pl.ds(z, 36, stride=2), :])
+        pad = jnp.zeros((4, 128), BF16)
+        bh_ref[z, 0] = jnp.concatenate([high, pad], axis=0)
+        bl_ref[z, 0] = jnp.concatenate([low, pad], axis=0)
+
+    @pl.when(step == 3)
+    def _():
+        for z in range(2):
+            for part in range(4):
+                sums_ref[z, 12 * part : 12 * part + 12] = held[part, z, 0:12]
+
+
+def start(displacement, weights, block, matrix):
+    outs = (shape(2, 72, 128),) + (shape(2, 4, 40, 768, dtype=BF16),) * 2
+    outs = outs + (shape(2, 4, 40, 128, dtype=BF16),) * 2 + (shape(4, 2, 24, 768),)
+    wide = pl.BlockSpec((2, 1, 40, 768), lambda i: (0, i, 0, 0))
+    slim = pl.BlockSpec((2, 1, 40, 128), lambda i: (0, i, 0, 0))
+    sums, ah, al, bh, bl, sent = call(
+        start_kernel,
+        outs,
+        (
+            pltpu.VMEM((4, 24, 128), F32),
+            pltpu.VMEM((4, 72, 128), F32),
+            pltpu.VMEM((40, 128), F32),
+            pltpu.VMEM((4, 2, 16, 128), F32),
+            pltpu.VMEM((9, 72, 128), F32),
+            pltpu.VMEM((160, 384), BF16),
+            pltpu.VMEM((40, 768), F32),
+        ),
+        flops=40_000_000,
+        grid=(4,),
+        in_specs=[
+            pl.BlockSpec((4, 2, 3, 3, 32, 128), lambda i: (0, 0, i, 0, 0, 0)),
+            pl.BlockSpec((4, 24, 128), lambda i: (0, 0, 0)),
+            pl.BlockSpec((4, 72, 36), lambda i: (0, 0, 0)),
+            pl.BlockSpec((512, 128), lambda i: (0, 0)),
+            pl.BlockSpec((1, 27, 72, 36), lambda i: (i, 0, 0, 0)),
+            pl.BlockSpec((384, 384), lambda i: (0, 0)),
+        ],
+        out_specs=(
+            pl.BlockSpec((2, 72, 128), lambda i: (0, 0, 0)),
+            wide,
+            wide,
+            slim,
+            slim,
+            pl.BlockSpec((1, 2, 24, 768), lambda i: (i, 0, 0, 0)),
+        ),
+    )(*streamed(displacement, weights, block, jnp.asarray(choice(), BF16), matrix, jnp.asarray(placement(), BF16)))
+    return (
+        sums, ah.reshape(2, 160, 768), al.reshape(2, 160, 768),
+        bh.reshape(2, 160, 128), bl.reshape(2, 160, 128), sent,
+    )
 
 
 def sum_x_kernel(sums_ref, left_ref, right_ref, out_ref, up_ref):
@@ -186,70 +283,6 @@
         g_ref[z] = rows[0:16]
         wide_ref[z, 0:16] = pltpu.roll(rows[0:16], 320, 1)[:, 0:256]
         wide_ref[z, 15:24] = pltpu.roll(rows[0:16], 288, 1)[6:15, 0:256]
-
-
-def pick(rows_ref, value):
-    rows_ref[...] = value
-    return [rows_ref[3 * edge : 3 * edge + 3] for edge in WIDE_EDGES]
-
-
-def prepare_kernel(
-    matrix_ref, block_ref, place_ref, ah_ref, al_ref, bh_ref, bl_ref, out_ref, packed, stacked, full
-):
-    packed[7] = jnp.zeros((72, 128), F32)
-    for offset in range(27):
-        start, tile = 36 * offset % 128, 36 * offset // 128
-        size = min(36, 128 - start)
-        packed[tile, :, start : start + size] = matrix_ref[0, offset, :, 0:size]
-        if size < 36:
-            packed[tile + 1, :, 0 : 36 - size] = matrix_ref[0, offset, :, size:36]
-    for z in range(2):
-        high, low = split(jnp.concatenate([packed[k, pl.ds(z, 36, stride=2), :] for k in range(8)], axis=1))
-        pad = jnp.zeros((4, 1024), BF16)
-        stacked[40 * z : 40 * z + 40] = jnp.concatenate([high, pad], axis=0)
-        stacked[80 + 40 * z : 120 + 40 * z] = jnp.concatenate([low, pad], axis=0)
-    found = dot(stacked[...], place_ref[...])
-    for z in range(2):
-        high, low = found[40 * z : 40 * z + 40], found[80 + 40 * z : 120 + 40 * z]
-        ah_ref[z, 0] = high.astype(BF16)
-        al_ref[z, 0] = low.astype(BF16)
-        for place, value in enumerate(pick(full, high + low)):
-            out_ref[0, z, 3 * place : 3 * place + 3] = value
-    packed[0] = jnp.zeros((72, 128), F32)
-    packed[0, :, 0:36] = block_ref[0]
-    for z in range(2):
-        high, low = split(packed[0, pl.ds(z, 36, stride=2), :])
-        pad = jnp.zeros((4, 128), BF16)
-        bh_ref[z, 0] = jnp.concatenate([high, pad], axis=0)
-        bl_ref[z, 0] = jnp.concatenate([low, pad], axis=0)
-
-
-def prepare(matrix, block):
-    outs = (shape(2, 4, 40, 768, dtype=BF16),) * 2 + (shape(2, 4, 40, 128, dtype=BF16),) * 2
-    outs = outs + (shape(4, 2, 24, 768),)
-    wide = pl.BlockSpec((2, 1, 40, 768), lambda i: (0, i, 0, 0))
-    slim = pl.BlockSpec((2, 1, 40, 128), lambda i: (0, i, 0, 0))
-    ah, al, bh, bl, sent = call(
-        prepare_kernel,
-        outs,
-        (
-            pltpu.VMEM((8, 72, 128), F32),
-            pltpu.VMEM((160, 1024), BF16),
-            pltpu.VMEM((40, 768), F32),
-        ),
-        flops=20_000_000,
-        grid=(4,),
-        in_specs=[
-            pl.BlockSpec((1, 27, 72, 36), lambda i: (i, 0, 0, 0)),
-            pl.BlockSpec((1, 72, 36), lambda i: (i, 0, 0)),
-            pl.BlockSpec((1024, 768), lambda i: (0, 0)),
-        ],
-        out_specs=(wide, wide, slim, slim, pl.BlockSpec((1, 2, 24, 768), lambda i: (i, 0, 0, 0))),
-    )(*streamed(matrix, block, jnp.asarray(placement(), BF16)))
-    return (
-        ah.reshape(2, 160, 768), al.reshape(2, 160, 768),
-        bh.reshape(2, 160, 128), bl.reshape(2, 160, 128), sent,
-    )
 
 
 def merge_kernel(own_ref, left_ref, right_ref, ah_ref, al_ref):
@@ -367,25 +400,14 @@
     weights = jnp.transpose(dof_weight[:, 0], (0, 2, 1, 3)).reshape(4, 24, 128)
     matrix = jnp.transpose(coarse_matrix[:, 0], (0, 2, 3, 1, 4)).reshape(4, 27, 72, 36)
     block = jnp.transpose(block_inverse[:, 0], (0, 2, 1, 3)).reshape(4, 72, 36)
-    sums = call(
-        numer_kernel,
-        shape(2, 72, 128),
-        (pltpu.VMEM((4, 24, 128), F32), pltpu.VMEM((4, 72, 128), F32), pltpu.VMEM((40, 128), F32)),
-        flops=20_000_000,
-        grid=(6,),
-        in_specs=[
-            pl.BlockSpec((4, 2, 2, 3, 32, 128), lambda i: (0, 0, i, 0, 0, 0)),
-            pl.BlockSpec((4, 24, 128), lambda i: (0, 0, 0)),
-            pl.BlockSpec((4, 72, 36), lambda i: (0, 0, 0)),
-            pl.BlockSpec((512, 128), lambda i: (0, 0)),
-        ],
-        out_specs=pl.BlockSpec((2, 72, 128), lambda i: (0, 0, 0)),
-    )(*streamed(displacement[:, 0], weights, block, jnp.asarray(choice(), BF16)))
-    mine, left, right = sums, shifted(sums, "gx", 1), shifted(sums, "gx", -1)
+    mine, ah, al, bh, bl, sent = start(displacement[:, 0], weights, block, matrix)
+    left = shifted(mine, "gx", 1)
+    right = shifted(mine, "gx", -1)
+    rows_left = shifted(sent[2:4], "gx", 1)
+    rows_right = shifted(sent[0:2], "gx", -1)
     sides = (mine, left, right)
     sums, up = call(sum_x_kernel, (shape(2, 32, 384), shape(24, 384)))(*sides)
     left = shifted(up, "gz", 1)
-    ah, al, bh, bl, sent = prepare(after(matrix, up), block)
     lower, upper, middle = call(sum_z_kernel, (shape(2, 8, 384),) * 3)(sums, left)
     below = shifted(upper, "gy", 1)
     above = shifted(lower, "gy", -1)
@@ -394,9 +416,6 @@
         (shape(2, 16, 384), shape(2, 24, 256), shape(2, 16, 384)) + (shape(2, 192, 32, dtype=BF16),) * 2,
         (pltpu.VMEM((32, 384), F32),),
     )(lower, upper, middle, below, above, *sides)
-    sent = after(sent, x)
-    rows_left = shifted(sent[2:4], "gx", 1)
-    rows_right = shifted(sent[0:2], "gx", -1)
     for sweep in range(3):
         below = shifted(x, "gy", 1)
         above = shifted(x, "gy", -1)

time: 129 us -> 127 us (0.984)
  Pallas kernels: 16.6 us -> 12 us
  waiting for transfers between devices: 47 us -> 50.6 us
  starting transfers between devices: 63.1 us -> 61.5 us
    pallas_call x2 -> x1, Pallas kernels: 10.2 us -> 5.58 us  [start(): call(start_kernel, outs, (pltpu.VMEM((4, 24, 128), F32), pltpu.VMEM((4, 7...]
    ppermute x19, waiting for transfers between devices: 47 us -> 50.6 us  [shifted(): lax.ppermute(block, axis, [((i - distance) % count, i) for i in range(cou...]
    ppermute x19, starting transfers between devices: 63.1 us -> 61.5 us  [shifted(): lax.ppermute(block, axis, [((i - distance) % count, i) for i in range(cou...]
  transfers between devices with their start and end apart: 19 -> 19, of which waited for: 10 -> 11; matrix products, arithmetic and copies ran while one was open for 1% -> 1% of each run, Pallas kernels for 5% -> 1%
where the time goes in v5:
time: 127 us; the launch traced here: 126 us
  starting transfers between devices  61.5 us (48%)
  waiting for transfers between devices  50.6 us (40%)
  Pallas kernels  12 us (9%)
    ppermute x19, starting transfers between devices, shifted(): lax.ppermute(block, axis, [((i - distance) % count, i) for i in range(cou...  61.5 us
    ppermute x19, waiting for transfers between devices, shifted(): lax.ppermute(block, axis, [((i - distance) % count, i) for i in range(cou...  50.6 us
    pallas_call x1, Pallas kernels, start(): call(start_kernel, outs, (pltpu.VMEM((4, 24, 128), F32), pltpu.VMEM((4, 7...  5.58 us
    pallas_call x2, Pallas kernels, steps(): call(functools.partial(sweep_kernel, 5 - sweep), shape(2, 16, 384 if swee...  3.83 us
  transfers between devices with their start and end apart: 19, of which 11 were waited for; matrix products, arithmetic and copies ran while one was open for 1% of the time, Pallas kernels for 1%

profile of v5, /device:TPU:56, one launch (start us, length us, event | category | flops | bytes accessed | tf_op | source)
XLA Modules:
  0.0 125.9 jit_solution(5365573903549200087)
XLA Ops:
  0.6 5.6 %shard_map.77 = (f32[2,72,128]{2,1,0:T(8,128)S(1)}, bf16[2,4,40,768]{3,2,1,0:T(8,128)(2,1)S(1)}, bf16[2,4,40,768]{3,2,1,0:T(8,128)(2,1)S(1)}, bf16[2,4,40,128]{3...) custom-call(bf16[4,2,12,3,32,128]{5,4,3,2,1,0:T(8,128)(2,1)} %bitcast.47, ...), custom_call_target="tpu_custom_call" | custom-call | flops 40000000 | bytes 1000000 | tf_op jit(solution)/shard_map/pallas_call | solution.py:192
  6.2 3.4 %collective-permute-start = (f32[2,72,128]{2,1,0:T(8,128)S(1)}, f32[2,72,128]{2,1,0:T(8,128)S(1)}, u32[]{:S(2)}, u32[]{:S(2)}) collective-permute-start(f32[2,72,128]{2,1,0:T(8,128)S(1)} %get-tuple-element.23.sums_ref.own_ref), channel_id=1, source_target_pairs={{384,0},{0,128},{128,256},{256,384},{385,1},{1,129},{129,257},{257... | collective-permute-start | bytes 221192 | tf_op jit(solution)/shard_map/ppermute | solution.py:57
  9.6 3.7 %collective-permute-start.1 = (f32[2,72,128]{2,1,0:T(8,128)S(1)}, f32[2,72,128]{2,1,0:T(8,128)S(1)}, u32[]{:S(2)}, u32[]{:S(2)}) collective-permute-start(f32[2,72,128]{2,1,0:T(8,128)S(1)} %get-tuple-element.23.sums_ref.own_ref), channel_id=1, source_target_pairs={{128,0},{256,128},{384,256},{0,384},{129,1},{257,129},{385,257},{1... | collective-permute-start | bytes 221192 | tf_op jit(solution)/shard_map/ppermute | solution.py:57
  13.7 2.2 %collective-permute-done.1.right_ref = f32[2,72,128]{2,1,0:T(8,128)S(1)} collective-permute-done((f32[2,72,128]{2,1,0:T(8,128)S(1)}, f32[2,72,128]{2,1,0:T(8,128)S(1)}, u32[]{:S(2)}, u32[]{:S(2)}) %collective-permute-start.1) | collective-permute-done | bytes 73760 | tf_op jit(solution)/shard_map/ppermute | solution.py:57
  16.0 1.9 %collective-permute-start.2 = (f32[24,384]{1,0:T(8,128)S(1)}, f32[24,384]{1,0:T(8,128)S(1)}, u32[]{:S(2)}, u32[]{:S(2)}) collective-permute-start(f32[24,384]{1,0:T(8,128)S(1)} %get-tuple-element.25), channel_id=1, source_target_pairs={{7,0},{0,1},{1,2},{2,3},{3,4},{4,5},{5,6},{6,7},{15,8},{8,9},{9,10... | collective-permute-start | bytes 110600 | tf_op jit(solution)/shard_map/ppermute | solution.py:57
  17.9 5.6 %collective-permute-done.2.left_ref = f32[24,384]{1,0:T(8,128)S(1)} collective-permute-done((f32[24,384]{1,0:T(8,128)S(1)}, f32[24,384]{1,0:T(8,128)S(1)}, u32[]{:S(2)}, u32[]{:S(2)}) %collective-permute-start.2) | collective-permute-done | bytes 36896 | tf_op jit(solution)/shard_map/ppermute | solution.py:57
  23.5 9.7 %collective-permute-start.3 = (f32[2,8,384]{2,1,0:T(8,128)S(1)}, f32[2,8,384]{2,1,0:T(8,128)S(1)}, u32[]{:S(2)}, u32[]{:S(2)}) collective-permute-start(f32[2,8,384]{2,1,0:T(8,128)S(1)} %get-tuple-element.27.upper_ref), channel_id=1, source_target_pairs={{120,0},{0,8},{8,16},{16,24},{24,32},{32,40},{40,48},{48,56},{56,6... | collective-permute-start | bytes 73736 | tf_op jit(solution)/shard_map/ppermute | solution.py:57
  33.2 1.9 %collective-permute-start.4 = (f32[2,8,384]{2,1,0:T(8,128)S(1)}, f32[2,8,384]{2,1,0:T(8,128)S(1)}, u32[]{:S(2)}, u32[]{:S(2)}) collective-permute-start(f32[2,8,384]{2,1,0:T(8,128)S(1)} %get-tuple-element.26.lower_ref), channel_id=1, source_target_pairs={{8,0},{16,8},{24,16},{32,24},{40,32},{48,40},{56,48},{64,56},{72,6... | collective-permute-start | bytes 73736 | tf_op jit(solution)/shard_map/ppermute | solution.py:57
  35.2 3.4 %collective-permute-start.9 = (f32[2,2,24,768]{3,2,1,0:T(8,128)S(1)}, f32[2,2,24,768]{3,2,1,0:T(8,128)S(1)}, u32[]{:S(2)}, u32[]{:S(2)}) collective-permute-start(f32[2,2,24,768]{3,2,1,0:T(8,128)S(1)} %get-tuple-element.49), channel_id=1, source_target_pairs={{384,0},{0,128},{128,256},{256,384},{385,1},{1,129},{129,257},{257... | collective-permute-start | bytes 884744 | tf_op jit(solution)/shard_map/ppermute | solution.py:57
  38.6 3.7 %collective-permute-start.10 = (f32[2,2,24,768]{3,2,1,0:T(8,128)S(1)}, f32[2,2,24,768]{3,2,1,0:T(8,128)S(1)}, u32[]{:S(2)}, u32[]{:S(2)}) collective-permute-start(f32[2,2,24,768]{3,2,1,0:T(8,128)S(1)} %get-tuple-element.48), channel_id=1, source_target_pairs={{128,0},{256,128},{384,256},{0,384},{129,1},{257,129},{385,257},{1... | collective-permute-start | bytes 884744 | tf_op jit(solution)/shard_map/ppermute | solution.py:57
  42.2 2.7 %collective-permute-done.4.above_ref = f32[2,8,384]{2,1,0:T(8,128)S(1)} collective-permute-done((f32[2,8,384]{2,1,0:T(8,128)S(1)}, f32[2,8,384]{2,1,0:T(8,128)S(1)}, u32[]{:S(2)}, u32[]{:S(2)}) %collective-permute-start.4) | collective-permute-done | bytes 24608 | tf_op jit(solution)/shard_map/ppermute | solution.py:57
  45.5 7.3 %collective-permute-start.5 = (f32[2,16,384]{2,1,0:T(8,128)S(1)}, f32[2,16,384]{2,1,0:T(8,128)S(1)}, u32[]{:S(2)}, u32[]{:S(2)}) collective-permute-start(f32[2,16,384]{2,1,0:T(8,128)S(1)} %get-tuple-element.30), channel_id=1, source_target_pairs={{120,0},{0,8},{8,16},{16,24},{24,32},{32,40},{40,48},{48,56},{56,6... | collective-permute-start | bytes 147464 | tf_op jit(solution)/shard_map/ppermute | solution.py:57
  52.8 1.9 %collective-permute-start.6 = (f32[2,16,384]{2,1,0:T(8,128)S(1)}, f32[2,16,384]{2,1,0:T(8,128)S(1)}, u32[]{:S(2)}, u32[]{:S(2)}) collective-permute-start(f32[2,16,384]{2,1,0:T(8,128)S(1)} %get-tuple-element.30), channel_id=1, source_target_pairs={{8,0},{16,8},{24,16},{32,24},{40,32},{48,40},{56,48},{64,56},{72,6... | collective-permute-start | bytes 147464 | tf_op jit(solution)/shard_map/ppermute | solution.py:57
  54.7 10.0 %collective-permute-done.6 = f32[2,16,384]{2,1,0:T(8,128)S(1)} collective-permute-done((f32[2,16,384]{2,1,0:T(8,128)S(1)}, f32[2,16,384]{2,1,0:T(8,128)S(1)}, u32[]{:S(2)}, u32[]{:S(2)}) %collective-permute-start.6) | collective-permute-done | bytes 49184 | tf_op jit(solution)/shard_map/ppermute | solution.py:57
  64.8 1.9 %collective-permute-start.7 = (f32[112,384]{1,0:T(8,128)S(1)}, f32[112,384]{1,0:T(8,128)S(1)}, u32[]{:S(2)}, u32[]{:S(2)}) collective-permute-start(f32[112,384]{1,0:T(8,128)S(1)} %pad_maximum_fusion), channel_id=1, source_target_pairs={{1,0},{2,1},{3,2},{4,3},{5,4},{6,5},{7,6},{0,7},{9,8},{10,9},{11,1... | collective-permute-start | bytes 516104 | tf_op jit(solution)/shard_map/ppermute | solution.py:57
  66.7 2.4 %collective-permute-start.8 = (f32[48,384]{1,0:T(8,128)S(1)}, f32[48,384]{1,0:T(8,128)S(1)}, u32[]{:S(2)}, u32[]{:S(2)}) collective-permute-start(f32[48,384]{1,0:T(8,128)S(1)} %slice_bitcast_fusion.1), channel_id=1, source_target_pairs={{7,0},{0,1},{1,2},{2,3},{3,4},{4,5},{5,6},{6,7},{15,8},{8,9},{9,10... | collective-permute-start | bytes 221192 | tf_op jit(solution)/shard_map/ppermute | solution.py:57
  69.4 4.8 %collective-permute-done.8.left_ref = f32[48,384]{1,0:T(8,128)S(1)} collective-permute-done((f32[48,384]{1,0:T(8,128)S(1)}, f32[48,384]{1,0:T(8,128)S(1)}, u32[]{:S(2)}, u32[]{:S(2)}) %collective-permute-start.8) | collective-permute-done | bytes 73760 | tf_op jit(solution)/shard_map/ppermute | solution.py:57
  74.2 1.9 %shard_map.83 = f32[2,16,384]{2,1,0:T(8,128)S(1)} custom-call(f32[2,48,384]{2,1,0:T(8,128)S(1)} %constant_dynamic-update-slice_fusion.own_ref, f32[48,384]{1,0:T(8,128)S(1)} %collective-permute-done.8.left_ref, f32[112,384]{1,0:T(8,128)S(1)} %collective-permute-done.7.right_ref, f32[2,24,256]{2,1,0:T(8,128)S(1)} %get-tuple-element.32.g_ref, ...), custom_call_target="tpu_custom_call" | custom-call | flops 20000000 | bytes 1000000 | tf_op jit(solution)/shard_map/pallas_call | solution.py:437
  76.1 1.9 %collective-permute-start.11 = (f32[2,16,384]{2,1,0:T(8,128)S(1)}, f32[2,16,384]{2,1,0:T(8,128)S(1)}, u32[]{:S(2)}, u32[]{:S(2)}) collective-permute-start(f32[2,16,384]{2,1,0:T(8,128)S(1)} %shard_map.83), channel_id=1, source_target_pairs={{120,0},{0,8},{8,16},{16,24},{24,32},{32,40},{40,48},{48,56},{56,6... | collective-permute-start | bytes 147464 | tf_op jit(solution)/shard_map/ppermute | solution.py:57
  78.0 3.9 %collective-permute-start.12 = (f32[2,16,384]{2,1,0:T(8,128)S(1)}, f32[2,16,384]{2,1,0:T(8,128)S(1)}, u32[]{:S(2)}, u32[]{:S(2)}) collective-permute-start(f32[2,16,384]{2,1,0:T(8,128)S(1)} %shard_map.83), channel_id=1, source_target_pairs={{8,0},{16,8},{24,16},{32,24},{40,32},{48,40},{56,48},{64,56},{72,6... | collective-permute-start | bytes 147464 | tf_op jit(solution)/shard_map/ppermute | solution.py:57
  82.1 7.9 %collective-permute-done.12 = f32[2,16,384]{2,1,0:T(8,128)S(1)} collective-permute-done((f32[2,16,384]{2,1,0:T(8,128)S(1)}, f32[2,16,384]{2,1,0:T(8,128)S(1)}, u32[]{:S(2)}, u32[]{:S(2)}) %collective-permute-start.12) | collective-permute-done | bytes 49184 | tf_op jit(solution)/shard_map/ppermute | solution.py:57
  90.0 1.9 %collective-permute-start.14 = (f32[96,384]{1,0:T(8,128)S(1)}, f32[96,384]{1,0:T(8,128)S(1)}, u32[]{:S(2)}, u32[]{:S(2)}) collective-permute-start(f32[96,384]{1,0:T(8,128)S(1)} %bitcast.40), channel_id=1, source_target_pairs={{1,0},{2,1},{3,2},{4,3},{5,4},{6,5},{7,6},{0,7},{9,8},{10,9},{11,1... | collective-permute-start | bytes 442376 | tf_op jit(solution)/shard_map/ppermute | solution.py:57
  92.0 2.4 %collective-permute-start.13 = (f32[48,384]{1,0:T(8,128)S(1)}, f32[48,384]{1,0:T(8,128)S(1)}, u32[]{:S(2)}, u32[]{:S(2)}) collective-permute-start(f32[48,384]{1,0:T(8,128)S(1)} %slice_bitcast_fusion), channel_id=1, source_target_pairs={{7,0},{0,1},{1,2},{2,3},{3,4},{4,5},{5,6},{6,7},{15,8},{8,9},{9,10... | collective-permute-start | bytes 221192 | tf_op jit(solution)/shard_map/ppermute | solution.py:57
  94.4 5.1 %collective-permute-done.13.left_ref = f32[48,384]{1,0:T(8,128)S(1)} collective-permute-done((f32[48,384]{1,0:T(8,128)S(1)}, f32[48,384]{1,0:T(8,128)S(1)}, u32[]{:S(2)}, u32[]{:S(2)}) %collective-permute-start.13) | collective-permute-done | bytes 73760 | tf_op jit(solution)/shard_map/ppermute | solution.py:57
  99.5 1.9 %shard_map.84 = f32[2,16,256]{2,1,0:T(8,128)S(1)} custom-call(f32[2,48,384]{2,1,0:T(8,128)S(1)} %pad_maximum_fusion.1.own_ref, f32[48,384]{1,0:T(8,128)S(1)} %collective-permute-done.13.left_ref, f32[96,384]{1,0:T(8,128)S(1)} %collective-permute-done.14.right_ref, f32[2,24,256]{2,1,0:T(8,128)S(1)} %get-tuple-element.32.g_ref, ...), custom_call_target="tpu_custom_call" | custom-call | flops 20000000 | bytes 1000000 | tf_op jit(solution)/shard_map/pallas_call | solution.py:437
  101.4 1.9 %collective-permute-start.15 = (f32[2,16,256]{2,1,0:T(8,128)S(1)}, f32[2,16,256]{2,1,0:T(8,128)S(1)}, u32[]{:S(2)}, u32[]{:S(2)}) collective-permute-start(f32[2,16,256]{2,1,0:T(8,128)S(1)} %shard_map.84), channel_id=1, source_target_pairs={{120,0},{0,8},{8,16},{16,24},{24,32},{32,40},{40,48},{48,56},{56,6... | collective-permute-start | bytes 98312 | tf_op jit(solution)/shard_map/ppermute | solution.py:57
  103.3 3.9 %collective-permute-start.16 = (f32[2,16,256]{2,1,0:T(8,128)S(1)}, f32[2,16,256]{2,1,0:T(8,128)S(1)}, u32[]{:S(2)}, u32[]{:S(2)}) collective-permute-start(f32[2,16,256]{2,1,0:T(8,128)S(1)} %shard_map.84), channel_id=1, source_target_pairs={{8,0},{16,8},{24,16},{32,24},{40,32},{48,40},{56,48},{64,56},{72,6... | collective-permute-start | bytes 98312 | tf_op jit(solution)/shard_map/ppermute | solution.py:57
  107.3 7.9 %collective-permute-done.16 = f32[2,16,256]{2,1,0:T(8,128)S(1)} collective-permute-done((f32[2,16,256]{2,1,0:T(8,128)S(1)}, f32[2,16,256]{2,1,0:T(8,128)S(1)}, u32[]{:S(2)}, u32[]{:S(2)}) %collective-permute-start.16) | collective-permute-done | bytes 32800 | tf_op jit(solution)/shard_map/ppermute | solution.py:57
  115.2 1.9 %collective-permute-start.18 = (f32[96,256]{1,0:T(8,128)S(1)}, f32[96,256]{1,0:T(8,128)S(1)}, u32[]{:S(2)}, u32[]{:S(2)}) collective-permute-start(f32[96,256]{1,0:T(8,128)S(1)} %bitcast.41), channel_id=1, source_target_pairs={{1,0},{2,1},{3,2},{4,3},{5,4},{6,5},{7,6},{0,7},{9,8},{10,9},{11,1... | collective-permute-start | bytes 294920 | tf_op jit(solution)/shard_map/ppermute | solution.py:57
  117.1 2.4 %collective-permute-start.17 = (f32[48,256]{1,0:T(8,128)S(1)}, f32[48,256]{1,0:T(8,128)S(1)}, u32[]{:S(2)}, u32[]{:S(2)}) collective-permute-start(f32[48,256]{1,0:T(8,128)S(1)} %slice_bitcast_fusion.2), channel_id=1, source_target_pairs={{7,0},{0,1},{1,2},{2,3},{3,4},{4,5},{5,6},{6,7},{15,8},{8,9},{9,10... | collective-permute-start | bytes 147464 | tf_op jit(solution)/shard_map/ppermute | solution.py:57
  120.4 3.9 %collective-permute-done.17.left_ref = f32[48,256]{1,0:T(8,128)S(1)} collective-permute-done((f32[48,256]{1,0:T(8,128)S(1)}, f32[48,256]{1,0:T(8,128)S(1)}, u32[]{:S(2)}, u32[]{:S(2)}) %collective-permute-start.17) | collective-permute-done | bytes 49184 | tf_op jit(solution)/shard_map/ppermute | solution.py:57
  124.3 1.6 %shard_map.85 = f32[4,2,32,36]{3,2,1,0:T(8,128)} custom-call(f32[2,48,256]{2,1,0:T(8,128)S(1)} %pad_maximum_fusion.2.own_ref, f32[48,256]{1,0:T(8,128)S(1)} %collective-permute-done.17.left_ref, f32[96,256]{1,0:T(8,128)S(1)} %collective-permute-done.18.right_ref, f32[2,48,128]{2,1,0:T(8,128)S(1)} %get-tuple-element.39.wide_ref, ...), custom_call_target="tpu_custom_call" | custom-call | flops 10000000 | bytes 1000000 | tf_op jit(solution)/shard_map/pallas_call | solution.py:443
  (27 shorter events, 2.4 us)
Async XLA Ops:
  6.2 7.5 %collective-permute-start = (f32[2,72,128]{2,1,0:T(8,128)S(1)}, f32[2,72,128]{2,1,0:T(8,128)S(1)}, u32[]{:S(2)}, u32[]{:S(2)}) collective-permute-start(f32[2,72,128]{2,1,0:T(8,128)S(1)} %get-tuple-element.23.sums_ref.own_ref), channel_id=1, source_target_pairs={{384,0},{0,128},{128,256},{256,384},{385,1},{1,129},{129,257},{257... | collective-permute-start | bytes 221192 | tf_op jit(solution)/shard_map/ppermute | solution.py:57
  9.6 6.2 %collective-permute-start.1 = (f32[2,72,128]{2,1,0:T(8,128)S(1)}, f32[2,72,128]{2,1,0:T(8,128)S(1)}, u32[]{:S(2)}, u32[]{:S(2)}) collective-permute-start(f32[2,72,128]{2,1,0:T(8,128)S(1)} %get-tuple-element.23.sums_ref.own_ref), channel_id=1, source_target_pairs={{128,0},{256,128},{384,256},{0,384},{129,1},{257,129},{385,257},{1... | collective-permute-start | bytes 221192 | tf_op jit(solution)/shard_map/ppermute | solution.py:57
  16.0 7.5 %collective-permute-start.2 = (f32[24,384]{1,0:T(8,128)S(1)}, f32[24,384]{1,0:T(8,128)S(1)}, u32[]{:S(2)}, u32[]{:S(2)}) collective-permute-start(f32[24,384]{1,0:T(8,128)S(1)} %get-tuple-element.25), channel_id=1, source_target_pairs={{7,0},{0,1},{1,2},{2,3},{3,4},{4,5},{5,6},{6,7},{15,8},{8,9},{9,10... | collective-permute-start | bytes 110600 | tf_op jit(solution)/shard_map/ppermute | solution.py:57
  23.5 18.7 %collective-permute-start.3 = (f32[2,8,384]{2,1,0:T(8,128)S(1)}, f32[2,8,384]{2,1,0:T(8,128)S(1)}, u32[]{:S(2)}, u32[]{:S(2)}) collective-permute-start(f32[2,8,384]{2,1,0:T(8,128)S(1)} %get-tuple-element.27.upper_ref), channel_id=1, source_target_pairs={{120,0},{0,8},{8,16},{16,24},{24,32},{32,40},{40,48},{48,56},{56,6... | collective-permute-start | bytes 73736 | tf_op jit(solution)/shard_map/ppermute | solution.py:57
  33.2 11.7 %collective-permute-start.4 = (f32[2,8,384]{2,1,0:T(8,128)S(1)}, f32[2,8,384]{2,1,0:T(8,128)S(1)}, u32[]{:S(2)}, u32[]{:S(2)}) collective-permute-start(f32[2,8,384]{2,1,0:T(8,128)S(1)} %get-tuple-element.26.lower_ref), channel_id=1, source_target_pairs={{8,0},{16,8},{24,16},{32,24},{40,32},{48,40},{56,48},{64,56},{72,6... | collective-permute-start | bytes 73736 | tf_op jit(solution)/shard_map/ppermute | solution.py:57
  35.2 34.0 %collective-permute-start.9 = (f32[2,2,24,768]{3,2,1,0:T(8,128)S(1)}, f32[2,2,24,768]{3,2,1,0:T(8,128)S(1)}, u32[]{:S(2)}, u32[]{:S(2)}) collective-permute-start(f32[2,2,24,768]{3,2,1,0:T(8,128)S(1)} %get-tuple-element.49), channel_id=1, source_target_pairs={{384,0},{0,128},{128,256},{256,384},{385,1},{1,129},{129,257},{257... | collective-permute-start | bytes 884744 | tf_op jit(solution)/shard_map/ppermute | solution.py:57
  38.6 30.6 %collective-permute-start.10 = (f32[2,2,24,768]{3,2,1,0:T(8,128)S(1)}, f32[2,2,24,768]{3,2,1,0:T(8,128)S(1)}, u32[]{:S(2)}, u32[]{:S(2)}) collective-permute-start(f32[2,2,24,768]{3,2,1,0:T(8,128)S(1)} %get-tuple-element.48), channel_id=1, source_target_pairs={{128,0},{256,128},{384,256},{0,384},{129,1},{257,129},{385,257},{1... | collective-permute-start | bytes 884744 | tf_op jit(solution)/shard_map/ppermute | solution.py:57
  45.5 9.2 %collective-permute-start.5 = (f32[2,16,384]{2,1,0:T(8,128)S(1)}, f32[2,16,384]{2,1,0:T(8,128)S(1)}, u32[]{:S(2)}, u32[]{:S(2)}) collective-permute-start(f32[2,16,384]{2,1,0:T(8,128)S(1)} %get-tuple-element.30), channel_id=1, source_target_pairs={{120,0},{0,8},{8,16},{16,24},{24,32},{32,40},{40,48},{48,56},{56,6... | collective-permute-start | bytes 147464 | tf_op jit(solution)/shard_map/ppermute | solution.py:57
  52.8 12.0 %collective-permute-start.6 = (f32[2,16,384]{2,1,0:T(8,128)S(1)}, f32[2,16,384]{2,1,0:T(8,128)S(1)}, u32[]{:S(2)}, u32[]{:S(2)}) collective-permute-start(f32[2,16,384]{2,1,0:T(8,128)S(1)} %get-tuple-element.30), channel_id=1, source_target_pairs={{8,0},{16,8},{24,16},{32,24},{40,32},{48,40},{56,48},{64,56},{72,6... | collective-permute-start | bytes 147464 | tf_op jit(solution)/shard_map/ppermute | solution.py:57
  64.8 9.4 %collective-permute-start.7 = (f32[112,384]{1,0:T(8,128)S(1)}, f32[112,384]{1,0:T(8,128)S(1)}, u32[]{:S(2)}, u32[]{:S(2)}) collective-permute-start(f32[112,384]{1,0:T(8,128)S(1)} %pad_maximum_fusion), channel_id=1, source_target_pairs={{1,0},{2,1},{3,2},{4,3},{5,4},{6,5},{7,6},{0,7},{9,8},{10,9},{11,1... | collective-permute-start | bytes 516104 | tf_op jit(solution)/shard_map/ppermute | solution.py:57
  66.7 7.5 %collective-permute-start.8 = (f32[48,384]{1,0:T(8,128)S(1)}, f32[48,384]{1,0:T(8,128)S(1)}, u32[]{:S(2)}, u32[]{:S(2)}) collective-permute-start(f32[48,384]{1,0:T(8,128)S(1)} %slice_bitcast_fusion.1), channel_id=1, source_target_pairs={{7,0},{0,1},{1,2},{2,3},{3,4},{4,5},{5,6},{6,7},{15,8},{8,9},{9,10... | collective-permute-start | bytes 221192 | tf_op jit(solution)/shard_map/ppermute | solution.py:57
  76.1 6.0 %collective-permute-start.11 = (f32[2,16,384]{2,1,0:T(8,128)S(1)}, f32[2,16,384]{2,1,0:T(8,128)S(1)}, u32[]{:S(2)}, u32[]{:S(2)}) collective-permute-start(f32[2,16,384]{2,1,0:T(8,128)S(1)} %shard_map.83), channel_id=1, source_target_pairs={{120,0},{0,8},{8,16},{16,24},{24,32},{32,40},{40,48},{48,56},{56,6... | collective-permute-start | bytes 147464 | tf_op jit(solution)/shard_map/ppermute | solution.py:57
  78.0 12.0 %collective-permute-start.12 = (f32[2,16,384]{2,1,0:T(8,128)S(1)}, f32[2,16,384]{2,1,0:T(8,128)S(1)}, u32[]{:S(2)}, u32[]{:S(2)}) collective-permute-start(f32[2,16,384]{2,1,0:T(8,128)S(1)} %shard_map.83), channel_id=1, source_target_pairs={{8,0},{16,8},{24,16},{32,24},{40,32},{48,40},{56,48},{64,56},{72,6... | collective-permute-start | bytes 147464 | tf_op jit(solution)/shard_map/ppermute | solution.py:57
  90.0 9.4 %collective-permute-start.14 = (f32[96,384]{1,0:T(8,128)S(1)}, f32[96,384]{1,0:T(8,128)S(1)}, u32[]{:S(2)}, u32[]{:S(2)}) collective-permute-start(f32[96,384]{1,0:T(8,128)S(1)} %bitcast.40), channel_id=1, source_target_pairs={{1,0},{2,1},{3,2},{4,3},{5,4},{6,5},{7,6},{0,7},{9,8},{10,9},{11,1... | collective-permute-start | bytes 442376 | tf_op jit(solution)/shard_map/ppermute | solution.py:57
  92.0 7.5 %collective-permute-start.13 = (f32[48,384]{1,0:T(8,128)S(1)}, f32[48,384]{1,0:T(8,128)S(1)}, u32[]{:S(2)}, u32[]{:S(2)}) collective-permute-start(f32[48,384]{1,0:T(8,128)S(1)} %slice_bitcast_fusion), channel_id=1, source_target_pairs={{7,0},{0,1},{1,2},{2,3},{3,4},{4,5},{5,6},{6,7},{15,8},{8,9},{9,10... | collective-permute-start | bytes 221192 | tf_op jit(solution)/shard_map/ppermute | solution.py:57
  101.4 5.9 %collective-permute-start.15 = (f32[2,16,256]{2,1,0:T(8,128)S(1)}, f32[2,16,256]{2,1,0:T(8,128)S(1)}, u32[]{:S(2)}, u32[]{:S(2)}) collective-permute-start(f32[2,16,256]{2,1,0:T(8,128)S(1)} %shard_map.84), channel_id=1, source_target_pairs={{120,0},{0,8},{8,16},{16,24},{24,32},{32,40},{40,48},{48,56},{56,6... | collective-permute-start | bytes 98312 | tf_op jit(solution)/shard_map/ppermute | solution.py:57
  103.3 11.8 %collective-permute-start.16 = (f32[2,16,256]{2,1,0:T(8,128)S(1)}, f32[2,16,256]{2,1,0:T(8,128)S(1)}, u32[]{:S(2)}, u32[]{:S(2)}) collective-permute-start(f32[2,16,256]{2,1,0:T(8,128)S(1)} %shard_map.84), channel_id=1, source_target_pairs={{8,0},{16,8},{24,16},{32,24},{40,32},{48,40},{56,48},{64,56},{72,6... | collective-permute-start | bytes 98312 | tf_op jit(solution)/shard_map/ppermute | solution.py:57
  115.2 9.2 %collective-permute-start.18 = (f32[96,256]{1,0:T(8,128)S(1)}, f32[96,256]{1,0:T(8,128)S(1)}, u32[]{:S(2)}, u32[]{:S(2)}) collective-permute-start(f32[96,256]{1,0:T(8,128)S(1)} %bitcast.41), channel_id=1, source_target_pairs={{1,0},{2,1},{3,2},{4,3},{5,4},{6,5},{7,6},{0,7},{9,8},{10,9},{11,1... | collective-permute-start | bytes 294920 | tf_op jit(solution)/shard_map/ppermute | solution.py:57
  117.1 7.2 %collective-permute-start.17 = (f32[48,256]{1,0:T(8,128)S(1)}, f32[48,256]{1,0:T(8,128)S(1)}, u32[]{:S(2)}, u32[]{:S(2)}) collective-permute-start(f32[48,256]{1,0:T(8,128)S(1)} %slice_bitcast_fusion.2), channel_id=1, source_target_pairs={{7,0},{0,1},{1,2},{2,3},{3,4},{4,5},{5,6},{6,7},{15,8},{8,9},{9,10... | collective-permute-start | bytes 147464 | tf_op jit(solution)/shard_map/ppermute | solution.py:57

commit v6 on v5

--- a/solution.py
+++ b/solution.py
@@ -57,6 +57,15 @@
     return lax.ppermute(block, axis, [((i - distance) % count, i) for i in range(count)])
 
 
+def matched(block, axis, which):
+    count = lax.axis_size(axis)
+    return lax.ppermute(block, axis, [(i, (i - 1 if i % 2 == which else i + 1) % count) for i in range(count)])
+
+
+def ordered(even, pair):
+    return jnp.where(even, pair[0], pair[1]), jnp.where(even, pair[1], pair[0])
+
+
 def lanes(shape):
     return lax.broadcasted_iota(jnp.int32, shape, len(shape) - 1)
 
@@ -78,7 +87,10 @@
     return total
 
 
-def call(kernel, outs, scratch=(), flops=1_000_000, **options):
+def call(kernel, outs, scratch=(), flops=1_000_000, scalar=False, count=0, **options):
+    if scalar:
+        places = [pltpu.SMEM] + [pltpu.VMEM] * count
+        options["in_specs"] = [pl.BlockSpec(memory_space=place) for place in places]
     return pl.pallas_call(
         kernel,
         out_shape=outs,
@@ -309,18 +321,20 @@
     return own_lanes(both[:, 0:128] + both[:, 128:256] + dot(kl_ref[z], kept))
 
 
-def gathered(own_ref, left_ref, right_ref):
-    near = jnp.concatenate(
-        [left_ref[:, 0:128], own_ref[0, :, 0:128], own_ref[1, :, 0:128], right_ref[0:96, 0:128]], axis=0
-    )
-    far = jnp.concatenate(
-        [left_ref[:, 128:256], own_ref[0, :, 128:256], own_ref[1, :, 128:256], right_ref[0:96, 128:256]], axis=0
-    )
-    return views(near, far)
-
-
-def sweep_kernel(top, own_ref, left_ref, right_ref, g_ref, ah_ref, al_ref, bh_ref, bl_ref, x_ref, rows, closed):
-    seen = jnp.concatenate([left_ref[...], own_ref[0], own_ref[1], right_ref[0:96]], axis=0)
+def gathered(odd_ref, own_ref, first_ref, second_ref):
+    left, right = sides_of(odd_ref, first_ref, second_ref)
+    all_z = jnp.concatenate([left, own_ref[0], own_ref[1], right], axis=0)
+    return views(all_z[:, 0:128], all_z[:, 128:256])
+
+
+def sides_of(odd_ref, first_ref, second_ref):
+    odd = jnp.full(first_ref.shape, odd_ref[0], jnp.int32) == 1
+    return jnp.where(odd[48:96], second_ref[48:96], first_ref[48:96]), jnp.where(odd, first_ref[...], second_ref[...])
+
+
+def sweep_kernel(top, odd_ref, own_ref, first_ref, second_ref, g_ref, ah_ref, al_ref, bh_ref, bl_ref, x_ref, rows, closed):
+    left, right = sides_of(odd_ref, first_ref, second_ref)
+    seen = jnp.concatenate([left, own_ref[0], own_ref[1], right[0:96]], axis=0)
     look = [pltpu.roll(seen, 384 - 32 * start, 1)[:, 0:256] for start in (1, 2, 3, 4)]
     pairs = [split(view) for view in look]
     rows[24:32] = jnp.zeros((8, 256), F32)
@@ -351,9 +365,9 @@
             x_ref[z] = pltpu.roll(jnp.where(use, after, body_rows), 192, 1)
 
 
-def average_kernel(g_ref, right_ref, wide_ref, out_ref, ahead):
+def average_kernel(odd_ref, g_ref, first_ref, second_ref, wide_ref, out_ref, ahead):
     for z in range(3):
-        source = g_ref.at[z] if z < 2 else right_ref.at[96:112]
+        source = g_ref[z] if z < 2 else sides_of(odd_ref, first_ref, second_ref)[1][96:112]
         ahead[z, 0:16] = source[:, 128:256]
         ahead[z, 16:32] = views(source[:, 128:256], source[:, 256:384])[2]
     for z in range(2):
@@ -371,8 +385,10 @@
         out_ref[x, z] = value[:, 32 * x : 32 * x + 32]
 
 
-def last_kernel(own_ref, left_ref, right_ref, wide_ref, ah_ref, al_ref, bh_ref, bl_ref, out_ref, rows, ahead, state):
-    seen = gathered(own_ref, left_ref, right_ref)
+def last_kernel(
+    odd_ref, own_ref, first_ref, second_ref, wide_ref, ah_ref, al_ref, bh_ref, bl_ref, out_ref, rows, ahead, state
+):
+    seen = gathered(odd_ref, own_ref, first_ref, second_ref)
     pairs = [split(view) for view in seen]
     high, low = [p[0] for p in pairs], [p[1] for p in pairs]
     state[...] = jnp.zeros((40, 128), F32)
@@ -409,43 +425,58 @@
     sums, up = call(sum_x_kernel, (shape(2, 32, 384), shape(24, 384)))(*sides)
     left = shifted(up, "gz", 1)
     lower, upper, middle = call(sum_z_kernel, (shape(2, 8, 384),) * 3)(sums, left)
-    below = shifted(upper, "gy", 1)
-    above = shifted(lower, "gy", -1)
+    even = lax.axis_index("gy") % 2 == 0
+    odd = (lax.axis_index("gz") % 2).astype(jnp.int32).reshape(1)
+    sent_down, sent_up = ordered(even, (lower, upper))
+    pair = []
+    for which, value in enumerate((sent_down, sent_up)):
+        pair.append(matched(value, "gy", which))
+    below, above = ordered(even, pair)
     g, near, x, near_high, near_low = call(
         first_kernel,
         (shape(2, 16, 384), shape(2, 24, 256), shape(2, 16, 384)) + (shape(2, 192, 32, dtype=BF16),) * 2,
         (pltpu.VMEM((32, 384), F32),),
     )(lower, upper, middle, below, above, *sides)
     for sweep in range(3):
-        below = shifted(x, "gy", 1)
-        above = shifted(x, "gy", -1)
+        pair = []
+        for which in range(2):
+            pair.append(matched(x, "gy", which))
         if sweep == 0:
-            rows_left = after(rows_left, below, above)
+            rows_left = after(rows_left, *pair)
             wide = (shape(2, 192, 768, dtype=BF16),) * 2
             operator = call(merge_kernel, wide, flops=10_000_000)(sent, rows_left, rows_right)
-        own = jnp.concatenate([x, below, above], axis=1)
-        left = shifted(own[1], "gz", 1)
+        own = jnp.concatenate([x, *ordered(even, pair)], axis=1)
         moving = own.reshape(96, own.shape[2])
         if sweep == 0:
             moving = jnp.concatenate([moving, g[0]], axis=0)
-        right = shifted(moving, "gz", -1)
+        pair = []
+        for which in range(2):
+            pair.append(matched(moving, "gz", which))
         if sweep == 0:
             every, average = call(
-                average_kernel, (shape(2, 48, 128), shape(4, 2, 36, 32)), (pltpu.VMEM((3, 32, 128), F32),)
-            )(g, right)
+                average_kernel,
+                (shape(2, 48, 128), shape(4, 2, 36, 32)),
+                (pltpu.VMEM((3, 32, 128), F32),),
+                scalar=True,
+                count=3,
+            )(odd, g, *pair)
         if sweep < 2:
             x = call(
                 functools.partial(sweep_kernel, 5 - sweep),
                 shape(2, 16, 384 if sweep == 0 else 256),
                 (pltpu.VMEM((32, 256), F32), pltpu.VMEM((16, 256), F32)),
                 flops=20_000_000,
-            )(own, left, right, near, *operator, near_high, near_low)
+                scalar=True,
+                count=8,
+            )(odd, own, *pair, near, *operator, near_high, near_low)
     x = call(
         last_kernel,
         shape(4, 2, 32, 36),
         (pltpu.VMEM((48, 128), F32), pltpu.VMEM((3, 32, 128), F32), pltpu.VMEM((40, 128), F32)),
         flops=10_000_000,
-    )(own, left, right, every, ah, al, bh, bl)
+        scalar=True,
+        count=8,
+    )(odd, own, *pair, every, ah, al, bh, bl)
     return average.reshape(4, 1, 2, 12, 3, 32), jnp.swapaxes(x, 2, 3)[:, None]
 
 

time: 127 us -> 114 us (0.90)
  the two profiles are of different devices: /device:TPU:56 before, /device:TPU:6 now
where the time goes in v6:
time: 114 us; the launch traced here: 113 us
  starting transfers between devices  61.6 us (54%)
  waiting for transfers between devices  36.2 us (32%)
  Pallas kernels  12 us (11%)
  local copies, waits for them, and re-layouts  1.5 us (1%)
    ppermute x14, starting transfers between devices, matched(): lax.ppermute(block, axis, [(i, (i - 1 if i % 2 == which else i + 1) % cou...  44.2 us
    ppermute x14, waiting for transfers between devices, matched(): lax.ppermute(block, axis, [(i, (i - 1 if i % 2 == which else i + 1) % cou...  25.6 us
    ppermute x5, starting transfers between devices, shifted(): lax.ppermute(block, axis, [((i - distance) % count, i) for i in range(cou...  17.4 us
    ppermute x5, waiting for transfers between devices, shifted(): lax.ppermute(block, axis, [((i - distance) % count, i) for i in range(cou...  10.7 us
    pallas_call x1, Pallas kernels, start(): call(start_kernel, outs, (pltpu.VMEM((4, 24, 128), F32), pltpu.VMEM((4, 7...  5.57 us
    pallas_call x2, Pallas kernels, steps(): call(functools.partial(sweep_kernel, 5 - sweep), shape(2, 16, 384 if swee...  3.83 us
  transfers between devices with their start and end apart: 19, of which 8 were waited for; matrix products, arithmetic and copies ran while one was open for 2% of the time, Pallas kernels for 1%

profile of v6, /device:TPU:6, one launch (start us, length us, event | category | flops | bytes accessed | tf_op | source)
XLA Modules:
  0.0 113.1 jit_solution(11727680184575155461)
XLA Ops:
  0.6 5.6 %shard_map.77 = (f32[2,72,128]{2,1,0:T(8,128)S(1)}, bf16[2,4,40,768]{3,2,1,0:T(8,128)(2,1)S(1)}, bf16[2,4,40,768]{3,2,1,0:T(8,128)(2,1)S(1)}, bf16[2,4,40,128]{3...) custom-call(bf16[4,2,12,3,32,128]{5,4,3,2,1,0:T(8,128)(2,1)} %bitcast.44, ...), custom_call_target="tpu_custom_call" | custom-call | flops 40000000 | bytes 1000000 | tf_op jit(solution)/shard_map/pallas_call | solution.py:204
  6.2 7.7 %collective-permute-start = (f32[2,72,128]{2,1,0:T(8,128)S(1)}, f32[2,72,128]{2,1,0:T(8,128)S(1)}, u32[]{:S(2)}, u32[]{:S(2)}) collective-permute-start(f32[2,72,128]{2,1,0:T(8,128)S(1)} %get-tuple-element.23.sums_ref.own_ref), channel_id=1, source_target_pairs={{384,0},{0,128},{128,256},{256,384},{385,1},{1,129},{129,257},{257... | collective-permute-start | bytes 221192 | tf_op jit(solution)/shard_map/ppermute | solution.py:57
  14.0 1.9 %collective-permute-start.1 = (f32[2,72,128]{2,1,0:T(8,128)S(1)}, f32[2,72,128]{2,1,0:T(8,128)S(1)}, u32[]{:S(2)}, u32[]{:S(2)}) collective-permute-start(f32[2,72,128]{2,1,0:T(8,128)S(1)} %get-tuple-element.23.sums_ref.own_ref), channel_id=1, source_target_pairs={{128,0},{256,128},{384,256},{0,384},{129,1},{257,129},{385,257},{1... | collective-permute-start | bytes 221192 | tf_op jit(solution)/shard_map/ppermute | solution.py:57
  15.9 5.5 %collective-permute-done.1.right_ref = f32[2,72,128]{2,1,0:T(8,128)S(1)} collective-permute-done((f32[2,72,128]{2,1,0:T(8,128)S(1)}, f32[2,72,128]{2,1,0:T(8,128)S(1)}, u32[]{:S(2)}, u32[]{:S(2)}) %collective-permute-start.1) | collective-permute-done | bytes 73760 | tf_op jit(solution)/shard_map/ppermute | solution.py:57
  21.5 1.9 %collective-permute-start.2 = (f32[24,384]{1,0:T(8,128)S(1)}, f32[24,384]{1,0:T(8,128)S(1)}, u32[]{:S(2)}, u32[]{:S(2)}) collective-permute-start(f32[24,384]{1,0:T(8,128)S(1)} %get-tuple-element.25), channel_id=1, source_target_pairs={{7,0},{0,1},{1,2},{2,3},{3,4},{4,5},{5,6},{6,7},{15,8},{8,9},{9,10... | collective-permute-start | bytes 110600 | tf_op jit(solution)/shard_map/ppermute | solution.py:57
  23.4 5.1 %collective-permute-done.2.left_ref = f32[24,384]{1,0:T(8,128)S(1)} collective-permute-done((f32[24,384]{1,0:T(8,128)S(1)}, f32[24,384]{1,0:T(8,128)S(1)}, u32[]{:S(2)}, u32[]{:S(2)}) %collective-permute-start.2) | collective-permute-done | bytes 36896 | tf_op jit(solution)/shard_map/ppermute | solution.py:57
  28.6 8.5 %collective-permute-start.3 = (f32[2,8,384]{2,1,0:T(8,128)S(1)}, f32[2,8,384]{2,1,0:T(8,128)S(1)}, u32[]{:S(2)}, u32[]{:S(2)}) collective-permute-start(f32[2,8,384]{2,1,0:T(8,128)S(1)} %get-tuple-element.59), channel_id=1, source_target_pairs={{0,120},{8,16},{16,8},{24,32},{32,24},{40,48},{48,40},{56,64},{64,... | collective-permute-start | bytes 73736 | tf_op jit(solution)/shard_map/ppermute | solution.py:62
  37.1 1.9 %collective-permute-start.4 = (f32[2,8,384]{2,1,0:T(8,128)S(1)}, f32[2,8,384]{2,1,0:T(8,128)S(1)}, u32[]{:S(2)}, u32[]{:S(2)}) collective-permute-start(f32[2,8,384]{2,1,0:T(8,128)S(1)} %get-tuple-element.58), channel_id=1, source_target_pairs={{0,8},{8,0},{16,24},{24,16},{32,40},{40,32},{48,56},{56,48},{64,72... | collective-permute-start | bytes 73736 | tf_op jit(solution)/shard_map/ppermute | solution.py:62
  39.0 0.8 fusion
  39.8 2.2 %collective-permute-start.9 = (f32[2,2,24,768]{3,2,1,0:T(8,128)}, f32[2,2,24,768]{3,2,1,0:T(8,128)S(1)}, u32[]{:S(2)}, u32[]{:S(2)}) collective-permute-start(f32[2,2,24,768]{3,2,1,0:T(8,128)} %get-tuple-element.49), channel_id=1, source_target_pairs={{384,0},{0,128},{128,256},{256,384},{385,1},{1,129},{129,257},{257... | collective-permute-start | bytes 884744 | tf_op jit(solution)/shard_map/ppermute | solution.py:57
  42.0 3.7 %collective-permute-start.10 = (f32[2,2,24,768]{3,2,1,0:T(8,128)S(1)}, f32[2,2,24,768]{3,2,1,0:T(8,128)S(1)}, u32[]{:S(2)}, u32[]{:S(2)}) collective-permute-start(f32[2,2,24,768]{3,2,1,0:T(8,128)S(1)} %get-tuple-element.48), channel_id=1, source_target_pairs={{128,0},{256,128},{384,256},{0,384},{129,1},{257,129},{385,257},{1... | collective-permute-start | bytes 884744 | tf_op jit(solution)/shard_map/ppermute | solution.py:57
  46.2 4.6 %collective-permute-start.5 = (f32[2,16,384]{2,1,0:T(8,128)S(1)}, f32[2,16,384]{2,1,0:T(8,128)S(1)}, u32[]{:S(2)}, u32[]{:S(2)}) collective-permute-start(f32[2,16,384]{2,1,0:T(8,128)S(1)} %get-tuple-element.30), channel_id=1, source_target_pairs={{0,120},{8,16},{16,8},{24,32},{32,24},{40,48},{48,40},{56,64},{64,... | collective-permute-start | bytes 147464 | tf_op jit(solution)/shard_map/ppermute | solution.py:62
  50.8 1.9 %collective-permute-start.6 = (f32[2,16,384]{2,1,0:T(8,128)S(1)}, f32[2,16,384]{2,1,0:T(8,128)S(1)}, u32[]{:S(2)}, u32[]{:S(2)}) collective-permute-start(f32[2,16,384]{2,1,0:T(8,128)S(1)} %get-tuple-element.30), channel_id=1, source_target_pairs={{0,8},{8,0},{16,24},{24,16},{32,40},{40,32},{48,56},{56,48},{64,72... | collective-permute-start | bytes 147464 | tf_op jit(solution)/shard_map/ppermute | solution.py:62
  52.8 5.5 %collective-permute-done.5 = f32[2,16,384]{2,1,0:T(8,128)S(1)} collective-permute-done((f32[2,16,384]{2,1,0:T(8,128)S(1)}, f32[2,16,384]{2,1,0:T(8,128)S(1)}, u32[]{:S(2)}, u32[]{:S(2)}) %collective-permute-start.5) | collective-permute-done | bytes 49184 | tf_op jit(solution)/shard_map/ppermute | solution.py:62
  58.9 1.9 %collective-permute-start.7 = (f32[112,384]{1,0:T(8,128)}, f32[112,384]{1,0:T(8,128)S(1)}, u32[]{:S(2)}, u32[]{:S(2)}) collective-permute-start(f32[112,384]{1,0:T(8,128)} %pad_maximum_fusion), channel_id=1, source_target_pairs={{0,7},{1,2},{2,1},{3,4},{4,3},{5,6},{6,5},{7,0},{8,15},{9,10},{10,... | collective-permute-start | bytes 516104 | tf_op jit(solution)/shard_map/ppermute | solution.py:62
  60.9 1.9 %collective-permute-start.8 = (f32[112,384]{1,0:T(8,128)}, f32[112,384]{1,0:T(8,128)S(1)}, u32[]{:S(2)}, u32[]{:S(2)}) collective-permute-start(f32[112,384]{1,0:T(8,128)} %pad_maximum_fusion), channel_id=1, source_target_pairs={{0,1},{1,0},{2,3},{3,2},{4,5},{5,4},{6,7},{7,6},{8,9},{9,8},{10,11... | collective-permute-start | bytes 516104 | tf_op jit(solution)/shard_map/ppermute | solution.py:62
  63.0 4.7 %collective-permute-done.7.first_ref = f32[112,384]{1,0:T(8,128)S(1)} collective-permute-done((f32[112,384]{1,0:T(8,128)}, f32[112,384]{1,0:T(8,128)S(1)}, u32[]{:S(2)}, u32[]{:S(2)}) %collective-permute-start.7) | collective-permute-done | bytes 172064 | tf_op jit(solution)/shard_map/ppermute | solution.py:62
  67.8 1.9 %shard_map.83 = f32[2,16,384]{2,1,0:T(8,128)S(1)} custom-call(s32[1]{0:T(128)} %bitcast.odd_ref, f32[2,48,384]{2,1,0:T(8,128)S(1)} %pad_maximum_fusion.1.own_ref, f32[112,384]{1,0:T(8,128)S(1)} %collective-permute-done.7.first_ref, f32[112,384]{1,0:T(8,128)S(1)} %collective-permute-done.8.second_ref, f32[2,24,256]{2,1,0:T(8,128)S(1)} %get-tuple-element.32.g_ref, ...), custom_call_target="tpu_custom_call" | custom-call | flops 20000000 | bytes 1000000 | tf_op jit(solution)/shard_map/pallas_call | solution.py:464
  69.7 5.8 %collective-permute-start.11 = (f32[2,16,384]{2,1,0:T(8,128)S(1)}, f32[2,16,384]{2,1,0:T(8,128)S(1)}, u32[]{:S(2)}, u32[]{:S(2)}) collective-permute-start(f32[2,16,384]{2,1,0:T(8,128)S(1)} %shard_map.83), channel_id=1, source_target_pairs={{0,120},{8,16},{16,8},{24,32},{32,24},{40,48},{48,40},{56,64},{64,... | collective-permute-start | bytes 147464 | tf_op jit(solution)/shard_map/ppermute | solution.py:62
  75.5 1.9 %collective-permute-start.12 = (f32[2,16,384]{2,1,0:T(8,128)S(1)}, f32[2,16,384]{2,1,0:T(8,128)S(1)}, u32[]{:S(2)}, u32[]{:S(2)}) collective-permute-start(f32[2,16,384]{2,1,0:T(8,128)S(1)} %shard_map.83), channel_id=1, source_target_pairs={{0,8},{8,0},{16,24},{24,16},{32,40},{40,32},{48,56},{56,48},{64,72... | collective-permute-start | bytes 147464 | tf_op jit(solution)/shard_map/ppermute | solution.py:62
  77.4 4.2 %collective-permute-done.11 = f32[2,16,384]{2,1,0:T(8,128)S(1)} collective-permute-done((f32[2,16,384]{2,1,0:T(8,128)S(1)}, f32[2,16,384]{2,1,0:T(8,128)S(1)}, u32[]{:S(2)}, u32[]{:S(2)}) %collective-permute-start.11) | collective-permute-done | bytes 49184 | tf_op jit(solution)/shard_map/ppermute | solution.py:62
  81.7 2.2 %collective-permute-start.13 = (f32[96,384]{1,0:T(8,128)S(1)}, f32[96,384]{1,0:T(8,128)S(1)}, u32[]{:S(2)}, u32[]{:S(2)}) collective-permute-start(f32[96,384]{1,0:T(8,128)S(1)} %bitcast.35), channel_id=1, source_target_pairs={{0,7},{1,2},{2,1},{3,4},{4,3},{5,6},{6,5},{7,0},{8,15},{9,10},{10,... | collective-permute-start | bytes 442376 | tf_op jit(solution)/shard_map/ppermute | solution.py:62
  83.9 1.9 %collective-permute-start.14 = (f32[96,384]{1,0:T(8,128)S(1)}, f32[96,384]{1,0:T(8,128)S(1)}, u32[]{:S(2)}, u32[]{:S(2)}) collective-permute-start(f32[96,384]{1,0:T(8,128)S(1)} %bitcast.36), channel_id=1, source_target_pairs={{0,1},{1,0},{2,3},{3,2},{4,5},{5,4},{6,7},{7,6},{8,9},{9,8},{10,11... | collective-permute-start | bytes 442376 | tf_op jit(solution)/shard_map/ppermute | solution.py:62
  85.8 4.1 %collective-permute-done.13.first_ref = f32[96,384]{1,0:T(8,128)S(1)} collective-permute-done((f32[96,384]{1,0:T(8,128)S(1)}, f32[96,384]{1,0:T(8,128)S(1)}, u32[]{:S(2)}, u32[]{:S(2)}) %collective-permute-start.13) | collective-permute-done | bytes 147488 | tf_op jit(solution)/shard_map/ppermute | solution.py:62
  90.0 1.9 %shard_map.84 = f32[2,16,256]{2,1,0:T(8,128)S(1)} custom-call(s32[1]{0:T(128)} %bitcast.odd_ref, f32[2,48,384]{2,1,0:T(8,128)S(1)} %pad_maximum_fusion.2.own_ref, f32[96,384]{1,0:T(8,128)S(1)} %collective-permute-done.13.first_ref, f32[96,384]{1,0:T(8,128)S(1)} %collective-permute-done.14.second_ref, f32[2,24,256]{2,1,0:T(8,128)S(1)} %get-tuple-element.32.g_ref, ...), custom_call_target="tpu_custom_call" | custom-call | flops 20000000 | bytes 1000000 | tf_op jit(solution)/shard_map/pallas_call | solution.py:464
  91.9 5.8 %collective-permute-start.15 = (f32[2,16,256]{2,1,0:T(8,128)S(1)}, f32[2,16,256]{2,1,0:T(8,128)S(1)}, u32[]{:S(2)}, u32[]{:S(2)}) collective-permute-start(f32[2,16,256]{2,1,0:T(8,128)S(1)} %shard_map.84), channel_id=1, source_target_pairs={{0,120},{8,16},{16,8},{24,32},{32,24},{40,48},{48,40},{56,64},{64,... | collective-permute-start | bytes 98312 | tf_op jit(solution)/shard_map/ppermute | solution.py:62
  97.8 1.9 %collective-permute-start.16 = (f32[2,16,256]{2,1,0:T(8,128)S(1)}, f32[2,16,256]{2,1,0:T(8,128)S(1)}, u32[]{:S(2)}, u32[]{:S(2)}) collective-permute-start(f32[2,16,256]{2,1,0:T(8,128)S(1)} %shard_map.84), channel_id=1, source_target_pairs={{0,8},{8,0},{16,24},{24,16},{32,40},{40,32},{48,56},{56,48},{64,72... | collective-permute-start | bytes 98312 | tf_op jit(solution)/shard_map/ppermute | solution.py:62
  99.7 4.0 %collective-permute-done.15 = f32[2,16,256]{2,1,0:T(8,128)S(1)} collective-permute-done((f32[2,16,256]{2,1,0:T(8,128)S(1)}, f32[2,16,256]{2,1,0:T(8,128)S(1)}, u32[]{:S(2)}, u32[]{:S(2)}) %collective-permute-start.15) | collective-permute-done | bytes 32800 | tf_op jit(solution)/shard_map/ppermute | solution.py:62
  103.8 1.9 %collective-permute-start.17 = (f32[96,256]{1,0:T(8,128)S(1)}, f32[96,256]{1,0:T(8,128)S(1)}, u32[]{:S(2)}, u32[]{:S(2)}) collective-permute-start(f32[96,256]{1,0:T(8,128)S(1)} %bitcast.39), channel_id=1, source_target_pairs={{0,7},{1,2},{2,1},{3,4},{4,3},{5,6},{6,5},{7,0},{8,15},{9,10},{10,... | collective-permute-start | bytes 294920 | tf_op jit(solution)/shard_map/ppermute | solution.py:62
  105.7 1.9 %collective-permute-start.18 = (f32[96,256]{1,0:T(8,128)S(1)}, f32[96,256]{1,0:T(8,128)S(1)}, u32[]{:S(2)}, u32[]{:S(2)}) collective-permute-start(f32[96,256]{1,0:T(8,128)S(1)} %bitcast.40), channel_id=1, source_target_pairs={{0,1},{1,0},{2,3},{3,2},{4,5},{5,4},{6,7},{7,6},{8,9},{9,8},{10,11... | collective-permute-start | bytes 294920 | tf_op jit(solution)/shard_map/ppermute | solution.py:62
  108.5 3.0 %collective-permute-done.17.first_ref = f32[96,256]{1,0:T(8,128)S(1)} collective-permute-done((f32[96,256]{1,0:T(8,128)S(1)}, f32[96,256]{1,0:T(8,128)S(1)}, u32[]{:S(2)}, u32[]{:S(2)}) %collective-permute-start.17) | collective-permute-done | bytes 98336 | tf_op jit(solution)/shard_map/ppermute | solution.py:62
  111.5 1.6 %shard_map.85 = f32[4,2,32,36]{3,2,1,0:T(8,128)} custom-call(s32[1]{0:T(128)} %bitcast.odd_ref, f32[2,48,256]{2,1,0:T(8,128)S(1)} %pad_maximum_fusion.3.own_ref, f32[96,256]{1,0:T(8,128)S(1)} %collective-permute-done.17.first_ref, f32[96,256]{1,0:T(8,128)S(1)} %collective-permute-done.18.second_ref, f32[2,48,128]{2,1,0:T(8,128)S(1)} %get-tuple-element.39.wide_ref, ...), custom_call_target="tpu_custom_call" | custom-call | flops 10000000 | bytes 1000000 | tf_op jit(solution)/shard_map/pallas_call | solution.py:472
  (27 shorter events, 2.6 us)
Async XLA Ops:
  6.2 9.7 %collective-permute-start = (f32[2,72,128]{2,1,0:T(8,128)S(1)}, f32[2,72,128]{2,1,0:T(8,128)S(1)}, u32[]{:S(2)}, u32[]{:S(2)}) collective-permute-start(f32[2,72,128]{2,1,0:T(8,128)S(1)} %get-tuple-element.23.sums_ref.own_ref), channel_id=1, source_target_pairs={{384,0},{0,128},{128,256},{256,384},{385,1},{1,129},{129,257},{257... | collective-permute-start | bytes 221192 | tf_op jit(solution)/shard_map/ppermute | solution.py:57
  14.0 7.5 %collective-permute-start.1 = (f32[2,72,128]{2,1,0:T(8,128)S(1)}, f32[2,72,128]{2,1,0:T(8,128)S(1)}, u32[]{:S(2)}, u32[]{:S(2)}) collective-permute-start(f32[2,72,128]{2,1,0:T(8,128)S(1)} %get-tuple-element.23.sums_ref.own_ref), channel_id=1, source_target_pairs={{128,0},{256,128},{384,256},{0,384},{129,1},{257,129},{385,257},{1... | collective-permute-start | bytes 221192 | tf_op jit(solution)/shard_map/ppermute | solution.py:57
  21.5 7.1 %collective-permute-start.2 = (f32[24,384]{1,0:T(8,128)S(1)}, f32[24,384]{1,0:T(8,128)S(1)}, u32[]{:S(2)}, u32[]{:S(2)}) collective-permute-start(f32[24,384]{1,0:T(8,128)S(1)} %get-tuple-element.25), channel_id=1, source_target_pairs={{7,0},{0,1},{1,2},{2,3},{3,4},{4,5},{5,6},{6,7},{15,8},{8,9},{9,10... | collective-permute-start | bytes 110600 | tf_op jit(solution)/shard_map/ppermute | solution.py:57
  28.6 17.0 %collective-permute-start.3 = (f32[2,8,384]{2,1,0:T(8,128)S(1)}, f32[2,8,384]{2,1,0:T(8,128)S(1)}, u32[]{:S(2)}, u32[]{:S(2)}) collective-permute-start(f32[2,8,384]{2,1,0:T(8,128)S(1)} %get-tuple-element.59), channel_id=1, source_target_pairs={{0,120},{8,16},{16,8},{24,32},{32,24},{40,48},{48,40},{56,64},{64,... | collective-permute-start | bytes 73736 | tf_op jit(solution)/shard_map/ppermute | solution.py:62
  37.1 8.5 %collective-permute-start.4 = (f32[2,8,384]{2,1,0:T(8,128)S(1)}, f32[2,8,384]{2,1,0:T(8,128)S(1)}, u32[]{:S(2)}, u32[]{:S(2)}) collective-permute-start(f32[2,8,384]{2,1,0:T(8,128)S(1)} %get-tuple-element.58), channel_id=1, source_target_pairs={{0,8},{8,0},{16,24},{24,16},{32,40},{40,32},{48,56},{56,48},{64,72... | collective-permute-start | bytes 73736 | tf_op jit(solution)/shard_map/ppermute | solution.py:62
  39.8 23.0 %collective-permute-start.9 = (f32[2,2,24,768]{3,2,1,0:T(8,128)}, f32[2,2,24,768]{3,2,1,0:T(8,128)S(1)}, u32[]{:S(2)}, u32[]{:S(2)}) collective-permute-start(f32[2,2,24,768]{3,2,1,0:T(8,128)} %get-tuple-element.49), channel_id=1, source_target_pairs={{384,0},{0,128},{128,256},{256,384},{385,1},{1,129},{129,257},{257... | collective-permute-start | bytes 884744 | tf_op jit(solution)/shard_map/ppermute | solution.py:57
  42.0 20.9 %collective-permute-start.10 = (f32[2,2,24,768]{3,2,1,0:T(8,128)S(1)}, f32[2,2,24,768]{3,2,1,0:T(8,128)S(1)}, u32[]{:S(2)}, u32[]{:S(2)}) collective-permute-start(f32[2,2,24,768]{3,2,1,0:T(8,128)S(1)} %get-tuple-element.48), channel_id=1, source_target_pairs={{128,0},{256,128},{384,256},{0,384},{129,1},{257,129},{385,257},{1... | collective-permute-start | bytes 884744 | tf_op jit(solution)/shard_map/ppermute | solution.py:57
  46.2 12.0 %collective-permute-start.5 = (f32[2,16,384]{2,1,0:T(8,128)S(1)}, f32[2,16,384]{2,1,0:T(8,128)S(1)}, u32[]{:S(2)}, u32[]{:S(2)}) collective-permute-start(f32[2,16,384]{2,1,0:T(8,128)S(1)} %get-tuple-element.30), channel_id=1, source_target_pairs={{0,120},{8,16},{16,8},{24,32},{32,24},{40,48},{48,40},{56,64},{64,... | collective-permute-start | bytes 147464 | tf_op jit(solution)/shard_map/ppermute | solution.py:62
  50.8 7.4 %collective-permute-start.6 = (f32[2,16,384]{2,1,0:T(8,128)S(1)}, f32[2,16,384]{2,1,0:T(8,128)S(1)}, u32[]{:S(2)}, u32[]{:S(2)}) collective-permute-start(f32[2,16,384]{2,1,0:T(8,128)S(1)} %get-tuple-element.30), channel_id=1, source_target_pairs={{0,8},{8,0},{16,24},{24,16},{32,40},{40,32},{48,56},{56,48},{64,72... | collective-permute-start | bytes 147464 | tf_op jit(solution)/shard_map/ppermute | solution.py:62
  58.9 8.8 %collective-permute-start.7 = (f32[112,384]{1,0:T(8,128)}, f32[112,384]{1,0:T(8,128)S(1)}, u32[]{:S(2)}, u32[]{:S(2)}) collective-permute-start(f32[112,384]{1,0:T(8,128)} %pad_maximum_fusion), channel_id=1, source_target_pairs={{0,7},{1,2},{2,1},{3,4},{4,3},{5,6},{6,5},{7,0},{8,15},{9,10},{10,... | collective-permute-start | bytes 516104 | tf_op jit(solution)/shard_map/ppermute | solution.py:62
  60.9 6.9 %collective-permute-start.8 = (f32[112,384]{1,0:T(8,128)}, f32[112,384]{1,0:T(8,128)S(1)}, u32[]{:S(2)}, u32[]{:S(2)}) collective-permute-start(f32[112,384]{1,0:T(8,128)} %pad_maximum_fusion), channel_id=1, source_target_pairs={{0,1},{1,0},{2,3},{3,2},{4,5},{5,4},{6,7},{7,6},{8,9},{9,8},{10,11... | collective-permute-start | bytes 516104 | tf_op jit(solution)/shard_map/ppermute | solution.py:62
  69.7 12.0 %collective-permute-start.11 = (f32[2,16,384]{2,1,0:T(8,128)S(1)}, f32[2,16,384]{2,1,0:T(8,128)S(1)}, u32[]{:S(2)}, u32[]{:S(2)}) collective-permute-start(f32[2,16,384]{2,1,0:T(8,128)S(1)} %shard_map.83), channel_id=1, source_target_pairs={{0,120},{8,16},{16,8},{24,32},{32,24},{40,48},{48,40},{56,64},{64,... | collective-permute-start | bytes 147464 | tf_op jit(solution)/shard_map/ppermute | solution.py:62
  75.5 6.1 %collective-permute-start.12 = (f32[2,16,384]{2,1,0:T(8,128)S(1)}, f32[2,16,384]{2,1,0:T(8,128)S(1)}, u32[]{:S(2)}, u32[]{:S(2)}) collective-permute-start(f32[2,16,384]{2,1,0:T(8,128)S(1)} %shard_map.83), channel_id=1, source_target_pairs={{0,8},{8,0},{16,24},{24,16},{32,40},{40,32},{48,56},{56,48},{64,72... | collective-permute-start | bytes 147464 | tf_op jit(solution)/shard_map/ppermute | solution.py:62
  81.7 8.3 %collective-permute-start.13 = (f32[96,384]{1,0:T(8,128)S(1)}, f32[96,384]{1,0:T(8,128)S(1)}, u32[]{:S(2)}, u32[]{:S(2)}) collective-permute-start(f32[96,384]{1,0:T(8,128)S(1)} %bitcast.35), channel_id=1, source_target_pairs={{0,7},{1,2},{2,1},{3,4},{4,3},{5,6},{6,5},{7,0},{8,15},{9,10},{10,... | collective-permute-start | bytes 442376 | tf_op jit(solution)/shard_map/ppermute | solution.py:62
  83.9 6.1 %collective-permute-start.14 = (f32[96,384]{1,0:T(8,128)S(1)}, f32[96,384]{1,0:T(8,128)S(1)}, u32[]{:S(2)}, u32[]{:S(2)}) collective-permute-start(f32[96,384]{1,0:T(8,128)S(1)} %bitcast.36), channel_id=1, source_target_pairs={{0,1},{1,0},{2,3},{3,2},{4,5},{5,4},{6,7},{7,6},{8,9},{9,8},{10,11... | collective-permute-start | bytes 442376 | tf_op jit(solution)/shard_map/ppermute | solution.py:62
  91.9 11.8 %collective-permute-start.15 = (f32[2,16,256]{2,1,0:T(8,128)S(1)}, f32[2,16,256]{2,1,0:T(8,128)S(1)}, u32[]{:S(2)}, u32[]{:S(2)}) collective-permute-start(f32[2,16,256]{2,1,0:T(8,128)S(1)} %shard_map.84), channel_id=1, source_target_pairs={{0,120},{8,16},{16,8},{24,32},{32,24},{40,48},{48,40},{56,64},{64,... | collective-permute-start | bytes 98312 | tf_op jit(solution)/shard_map/ppermute | solution.py:62
  97.8 6.0 %collective-permute-start.16 = (f32[2,16,256]{2,1,0:T(8,128)S(1)}, f32[2,16,256]{2,1,0:T(8,128)S(1)}, u32[]{:S(2)}, u32[]{:S(2)}) collective-permute-start(f32[2,16,256]{2,1,0:T(8,128)S(1)} %shard_map.84), channel_id=1, source_target_pairs={{0,8},{8,0},{16,24},{24,16},{32,40},{40,32},{48,56},{56,48},{64,72... | collective-permute-start | bytes 98312 | tf_op jit(solution)/shard_map/ppermute | solution.py:62
  103.8 7.7 %collective-permute-start.17 = (f32[96,256]{1,0:T(8,128)S(1)}, f32[96,256]{1,0:T(8,128)S(1)}, u32[]{:S(2)}, u32[]{:S(2)}) collective-permute-start(f32[96,256]{1,0:T(8,128)S(1)} %bitcast.39), channel_id=1, source_target_pairs={{0,7},{1,2},{2,1},{3,4},{4,3},{5,6},{6,5},{7,0},{8,15},{9,10},{10,... | collective-permute-start | bytes 294920 | tf_op jit(solution)/shard_map/ppermute | solution.py:62
  105.7 5.8 %collective-permute-start.18 = (f32[96,256]{1,0:T(8,128)S(1)}, f32[96,256]{1,0:T(8,128)S(1)}, u32[]{:S(2)}, u32[]{:S(2)}) collective-permute-start(f32[96,256]{1,0:T(8,128)S(1)} %bitcast.40), channel_id=1, source_target_pairs={{0,1},{1,0},{2,3},{3,2},{4,5},{5,4},{6,7},{7,6},{8,9},{9,8},{10,11... | collective-permute-start | bytes 294920 | tf_op jit(solution)/shard_map/ppermute | solution.py:62

commit v7 on v6

--- a/solution.py
+++ b/solution.py
@@ -109,11 +109,6 @@
     return jax.ShapeDtypeStruct(dims, dtype)
 
 
-def pick(rows_ref, value):
-    rows_ref[...] = value
-    return [rows_ref[3 * edge : 3 * edge + 3] for edge in WIDE_EDGES]
-
-
 def take_sums(step, disp_ref, weights, held):
     ones = jnp.ones((128, 128), BF16)
     group = (lanes((4, 512)) % 128) // 32
@@ -131,7 +126,7 @@
         held[step, z, 0:12] = jnp.concatenate(pieces, axis=0)
 
 
-def take_operator(matrix_ref, place_ref, ah_ref, al_ref, sent_ref, packed, stacked, full):
+def take_operator(step, matrix_ref, place_ref, ah_ref, al_ref, halves, packed, stacked, full):
     for offset in range(27):
         start, tile = 36 * (offset % 9) % 128, 3 * (offset // 9) + 36 * (offset % 9) // 128
         size = min(36, 128 - start)
@@ -155,13 +150,18 @@
         high, low = total[40 * z : 40 * z + 40], total[80 + 40 * z : 120 + 40 * z]
         ah_ref[z, 0] = high.astype(BF16)
         al_ref[z, 0] = low.astype(BF16)
-        for place, value in enumerate(pick(full, high + low)):
-            sent_ref[0, z, 3 * place : 3 * place + 3] = value
+        full[...] = high + low
+        for half, half_ref in enumerate(halves):
+
+            @pl.when(step // 2 == half)
+            def _(half_ref=half_ref, z=z):
+                for place, edge in enumerate(WIDE_EDGES):
+                    half_ref[0, z, 3 * place : 3 * place + 3] = full[3 * edge : 3 * edge + 3]
 
 
 def start_kernel(
     disp_ref, weight_ref, block_ref, choice_ref, matrix_ref, place_ref,
-    sums_ref, ah_ref, al_ref, bh_ref, bl_ref, sent_ref,
+    sums_ref, ah_ref, al_ref, bh_ref, bl_ref, near_ref, far_ref,
     weights, inner, rows, held, packed, stacked, full,
 ):
     step = pl.program_id(0)
@@ -182,7 +182,7 @@
                 sums_ref[z, 48 + 3 * place : 51 + 3 * place] = rows[3 * edge : 3 * edge + 3]
 
     take_sums(step, disp_ref, weights, held)
-    take_operator(matrix_ref, place_ref, ah_ref, al_ref, sent_ref, packed, stacked, full)
+    take_operator(step, matrix_ref, place_ref, ah_ref, al_ref, (near_ref, far_ref), packed, stacked, full)
     for z in range(2):
         high, low = split(inner[step, pl.ds(z, 36, stride=2), :])
         pad = jnp.zeros((4, 128), BF16)
@@ -198,10 +198,10 @@
 
 def start(displacement, weights, block, matrix):
     outs = (shape(2, 72, 128),) + (shape(2, 4, 40, 768, dtype=BF16),) * 2
-    outs = outs + (shape(2, 4, 40, 128, dtype=BF16),) * 2 + (shape(4, 2, 24, 768),)
+    outs = outs + (shape(2, 4, 40, 128, dtype=BF16),) * 2 + (shape(2, 2, 24, 768),) * 2
     wide = pl.BlockSpec((2, 1, 40, 768), lambda i: (0, i, 0, 0))
     slim = pl.BlockSpec((2, 1, 40, 128), lambda i: (0, i, 0, 0))
-    sums, ah, al, bh, bl, sent = call(
+    sums, ah, al, bh, bl, near, far = call(
         start_kernel,
         outs,
         (
@@ -229,12 +229,13 @@
             wide,
             slim,
             slim,
-            pl.BlockSpec((1, 2, 24, 768), lambda i: (i, 0, 0, 0)),
+            pl.BlockSpec((1, 2, 24, 768), lambda i: (jnp.minimum(i, 1), 0, 0, 0)),
+            pl.BlockSpec((1, 2, 24, 768), lambda i: (jnp.maximum(i - 2, 0), 0, 0, 0)),
         ),
     )(*streamed(displacement, weights, block, jnp.asarray(choice(), BF16), matrix, jnp.asarray(placement(), BF16)))
     return (
         sums, ah.reshape(2, 160, 768), al.reshape(2, 160, 768),
-        bh.reshape(2, 160, 128), bl.reshape(2, 160, 128), sent,
+        bh.reshape(2, 160, 128), bl.reshape(2, 160, 128), near, far,
     )
 
 
@@ -297,10 +298,9 @@
         wide_ref[z, 15:24] = pltpu.roll(rows[0:16], 288, 1)[6:15, 0:256]
 
 
-def merge_kernel(own_ref, left_ref, right_ref, ah_ref, al_ref):
-    for z in range(2):
-        cells = [left_ref[0, z], left_ref[1, z]] + [own_ref[x, z] for x in range(4)]
-        cells = cells + [right_ref[0, z], right_ref[1, z]]
+def merge_kernel(near_ref, far_ref, left_ref, right_ref, ah_ref, al_ref):
+    for z in range(2):
+        cells = [ref[x, z] for ref in (left_ref, near_ref, far_ref, right_ref) for x in range(2)]
         ah_ref[z], al_ref[z] = split(jnp.concatenate(cells, axis=0))
 
 
@@ -323,8 +323,19 @@
 
 def gathered(odd_ref, own_ref, first_ref, second_ref):
     left, right = sides_of(odd_ref, first_ref, second_ref)
-    all_z = jnp.concatenate([left, own_ref[0], own_ref[1], right], axis=0)
+    all_z = jnp.concatenate([left, own_ref[0:96], right], axis=0)
     return views(all_z[:, 0:128], all_z[:, 128:256])
+
+
+def layers_kernel(even_ref, x_ref, first_ref, second_ref, *rest):
+    out_ref = rest[-1]
+    even = jnp.full(x_ref.shape[1:], even_ref[0], jnp.int32) == 1
+    for z in range(2):
+        out_ref[48 * z : 48 * z + 16] = x_ref[z]
+        out_ref[48 * z + 16 : 48 * z + 32] = jnp.where(even, first_ref[z], second_ref[z])
+        out_ref[48 * z + 32 : 48 * z + 48] = jnp.where(even, second_ref[z], first_ref[z])
+    if len(rest) == 2:
+        out_ref[96:112] = rest[0][0]
 
 
 def sides_of(odd_ref, first_ref, second_ref):
@@ -334,7 +345,7 @@
 
 def sweep_kernel(top, odd_ref, own_ref, first_ref, second_ref, g_ref, ah_ref, al_ref, bh_ref, bl_ref, x_ref, rows, closed):
     left, right = sides_of(odd_ref, first_ref, second_ref)
-    seen = jnp.concatenate([left, own_ref[0], own_ref[1], right[0:96]], axis=0)
+    seen = jnp.concatenate([left, own_ref[0:96], right[0:96]], axis=0)
     look = [pltpu.roll(seen, 384 - 32 * start, 1)[:, 0:256] for start in (1, 2, 3, 4)]
     pairs = [split(view) for view in look]
     rows[24:32] = jnp.zeros((8, 256), F32)
@@ -416,22 +427,24 @@
     weights = jnp.transpose(dof_weight[:, 0], (0, 2, 1, 3)).reshape(4, 24, 128)
     matrix = jnp.transpose(coarse_matrix[:, 0], (0, 2, 3, 1, 4)).reshape(4, 27, 72, 36)
     block = jnp.transpose(block_inverse[:, 0], (0, 2, 1, 3)).reshape(4, 72, 36)
-    mine, ah, al, bh, bl, sent = start(displacement[:, 0], weights, block, matrix)
-    left = shifted(mine, "gx", 1)
-    right = shifted(mine, "gx", -1)
-    rows_left = shifted(sent[2:4], "gx", 1)
-    rows_right = shifted(sent[0:2], "gx", -1)
+    mine, ah, al, bh, bl, low_x, high_x = start(displacement[:, 0], weights, block, matrix)
+    pair = []
+    for which in range(2):
+        pair.append(matched(mine, "gx", which))
+    left, right = ordered(lax.axis_index("gx") % 2 == 0, pair)
     sides = (mine, left, right)
     sums, up = call(sum_x_kernel, (shape(2, 32, 384), shape(24, 384)))(*sides)
     left = shifted(up, "gz", 1)
     lower, upper, middle = call(sum_z_kernel, (shape(2, 8, 384),) * 3)(sums, left)
     even = lax.axis_index("gy") % 2 == 0
+    even_row = even.astype(jnp.int32).reshape(1)
     odd = (lax.axis_index("gz") % 2).astype(jnp.int32).reshape(1)
     sent_down, sent_up = ordered(even, (lower, upper))
     pair = []
     for which, value in enumerate((sent_down, sent_up)):
         pair.append(matched(value, "gy", which))
     below, above = ordered(even, pair)
+    rows_left = shifted(after(high_x, upper), "gx", 1)
     g, near, x, near_high, near_low = call(
         first_kernel,
         (shape(2, 16, 384), shape(2, 24, 256), shape(2, 16, 384)) + (shape(2, 192, 32, dtype=BF16),) * 2,
@@ -442,16 +455,16 @@
         for which in range(2):
             pair.append(matched(x, "gy", which))
         if sweep == 0:
-            rows_left = after(rows_left, *pair)
+            rows_right = shifted(after(low_x, x), "gx", -1)
+            rows_right = after(rows_right, *pair)
             wide = (shape(2, 192, 768, dtype=BF16),) * 2
-            operator = call(merge_kernel, wide, flops=10_000_000)(sent, rows_left, rows_right)
-        own = jnp.concatenate([x, *ordered(even, pair)], axis=1)
-        moving = own.reshape(96, own.shape[2])
-        if sweep == 0:
-            moving = jnp.concatenate([moving, g[0]], axis=0)
+            operator = call(merge_kernel, wide, flops=10_000_000)(low_x, high_x, rows_left, rows_right)
+        pieces = (x, *pair, g) if sweep == 0 else (x, *pair)
+        rows = shape(112 if sweep == 0 else 96, x.shape[2])
+        own = call(layers_kernel, rows, scalar=True, count=len(pieces))(even_row, *pieces)
         pair = []
         for which in range(2):
-            pair.append(matched(moving, "gz", which))
+            pair.append(matched(own, "gz", which))
         if sweep == 0:
             every, average = call(
                 average_kernel,

time: 114 us -> 116 us (1.018)
  starting transfers between devices: 61.6 us -> 64.6 us
    ppermute x14 -> x16, starting transfers between devices: 44.2 us -> 55.7 us  [matched(): lax.ppermute(block, axis, [(i, (i - 1 if i % 2 == which else i + 1) % cou...]
    ppermute x5 -> x3, starting transfers between devices: 17.4 us -> 8.97 us  [shifted(): lax.ppermute(block, axis, [((i - distance) % count, i) for i in range(cou...]
    ppermute x14 -> x16, waiting for transfers between devices: 25.6 us -> 31.7 us  [matched(): lax.ppermute(block, axis, [(i, (i - 1 if i % 2 == which else i + 1) % cou...]
    ppermute x5 -> x3, waiting for transfers between devices: 10.7 us -> 5.14 us  [shifted(): lax.ppermute(block, axis, [((i - distance) % count, i) for i in range(cou...]
  transfers between devices with their start and end apart: 19 -> 19, of which waited for: 8 -> 11; matrix products, arithmetic and copies ran while one was open for 2% -> 1% of each run, Pallas kernels for 1% -> 0%
where the time goes in v7:
time: 116 us; the launch traced here: 115 us
  starting transfers between devices  64.6 us (56%)
  waiting for transfers between devices  36.8 us (32%)
  Pallas kernels  12.2 us (11%)
    ppermute x16, starting transfers between devices, matched(): lax.ppermute(block, axis, [(i, (i - 1 if i % 2 == which else i + 1) % cou...  55.7 us
    ppermute x16, waiting for transfers between devices, matched(): lax.ppermute(block, axis, [(i, (i - 1 if i % 2 == which else i + 1) % cou...  31.7 us
    ppermute x3, starting transfers between devices, shifted(): lax.ppermute(block, axis, [((i - distance) % count, i) for i in range(cou...  8.97 us
    pallas_call x1, Pallas kernels, start(): call(start_kernel, outs, (pltpu.VMEM((4, 24, 128), F32), pltpu.VMEM((4, 7...  5.67 us
    ppermute x3, waiting for transfers between devices, shifted(): lax.ppermute(block, axis, [((i - distance) % count, i) for i in range(cou...  5.14 us
    pallas_call x2, Pallas kernels, steps(): call(functools.partial(sweep_kernel, 5 - sweep), shape(2, 16, 384 if swee...  3.83 us
  transfers between devices with their start and end apart: 19, of which 11 were waited for; matrix products, arithmetic and copies ran while one was open for 1% of the time, Pallas kernels for 0%

profile of v7, /device:TPU:6, one launch (start us, length us, event | category | flops | bytes accessed | tf_op | source)
XLA Modules:
  0.0 115.3 jit_solution(2709298724441238309)
XLA Ops:
  0.6 5.7 %shard_map.77 = (f32[2,72,128]{2,1,0:T(8,128)S(1)}, bf16[2,4,40,768]{3,2,1,0:T(8,128)(2,1)S(1)}, bf16[2,4,40,768]{3,2,1,0:T(8,128)(2,1)S(1)}, bf16[2,4,40,128]{3...) custom-call(bf16[4,2,12,3,32,128]{5,4,3,2,1,0:T(8,128)(2,1)} %bitcas, ...), custom_call_target="tpu_custom_call" | custom-call | flops 40000000 | bytes 1000000 | tf_op jit(solution)/shard_map/pallas_call | solution.py:204
  6.3 7.7 %collective-permute-start = (f32[2,72,128]{2,1,0:T(8,128)S(1)}, f32[2,72,128]{2,1,0:T(8,128)S(1)}, u32[]{:S(2)}, u32[]{:S(2)}) collective-permute-start(f32[2,72,128]{2,1,0:T(8,128)S(1)} %get-tuple-element.26.sums_ref.own_ref), channel_id=1, source_target_pairs={{0,384},{128,256},{256,128},{384,0},{1,385},{129,257},{257,129},{3... | collective-permute-start | bytes 221192 | tf_op jit(solution)/shard_map/ppermute | solution.py:62
  14.0 1.9 %collective-permute-start.1 = (f32[2,72,128]{2,1,0:T(8,128)S(1)}, f32[2,72,128]{2,1,0:T(8,128)S(1)}, u32[]{:S(2)}, u32[]{:S(2)}) collective-permute-start(f32[2,72,128]{2,1,0:T(8,128)S(1)} %get-tuple-element.26.sums_ref.own_ref), channel_id=1, source_target_pairs={{0,128},{128,0},{256,384},{384,256},{1,129},{129,1},{257,385},{385... | collective-permute-start | bytes 221192 | tf_op jit(solution)/shard_map/ppermute | solution.py:62
  16.4 3.9 %collective-permute-done.1 = f32[2,72,128]{2,1,0:T(8,128)S(1)} collective-permute-done((f32[2,72,128]{2,1,0:T(8,128)S(1)}, f32[2,72,128]{2,1,0:T(8,128)S(1)}, u32[]{:S(2)}, u32[]{:S(2)}) %collective-permute-start.1) | collective-permute-done | bytes 73760 | tf_op jit(solution)/shard_map/ppermute | solution.py:62
  20.4 1.9 %collective-permute-start.2 = (f32[24,384]{1,0:T(8,128)S(1)}, f32[24,384]{1,0:T(8,128)S(1)}, u32[]{:S(2)}, u32[]{:S(2)}) collective-permute-start(f32[24,384]{1,0:T(8,128)S(1)} %get-tuple-element.28), channel_id=1, source_target_pairs={{7,0},{0,1},{1,2},{2,3},{3,4},{4,5},{5,6},{6,7},{15,8},{8,9},{9,10... | collective-permute-start | bytes 110600 | tf_op jit(solution)/shard_map/ppermute | solution.py:57
  22.3 5.1 %collective-permute-done.2.left_ref = f32[24,384]{1,0:T(8,128)S(1)} collective-permute-done((f32[24,384]{1,0:T(8,128)S(1)}, f32[24,384]{1,0:T(8,128)S(1)}, u32[]{:S(2)}, u32[]{:S(2)}) %collective-permute-start.2) | collective-permute-done | bytes 36896 | tf_op jit(solution)/shard_map/ppermute | solution.py:57
  27.5 8.5 %collective-permute-start.3 = (f32[2,8,384]{2,1,0:T(8,128)S(1)}, f32[2,8,384]{2,1,0:T(8,128)S(1)}, u32[]{:S(2)}, u32[]{:S(2)}) collective-permute-start(f32[2,8,384]{2,1,0:T(8,128)S(1)} %get-tuple-element.59), channel_id=1, source_target_pairs={{0,120},{8,16},{16,8},{24,32},{32,24},{40,48},{48,40},{56,64},{64,... | collective-permute-start | bytes 73736 | tf_op jit(solution)/shard_map/ppermute | solution.py:62
  36.0 1.9 %collective-permute-start.4 = (f32[2,8,384]{2,1,0:T(8,128)S(1)}, f32[2,8,384]{2,1,0:T(8,128)S(1)}, u32[]{:S(2)}, u32[]{:S(2)}) collective-permute-start(f32[2,8,384]{2,1,0:T(8,128)S(1)} %get-tuple-element.58), channel_id=1, source_target_pairs={{0,8},{8,0},{16,24},{24,16},{32,40},{40,32},{48,56},{56,48},{64,72... | collective-permute-start | bytes 73736 | tf_op jit(solution)/shard_map/ppermute | solution.py:62
  39.3 2.4 %collective-permute-done.4 = f32[2,8,384]{2,1,0:T(8,128)S(1)} collective-permute-done((f32[2,8,384]{2,1,0:T(8,128)S(1)}, f32[2,8,384]{2,1,0:T(8,128)S(1)}, u32[]{:S(2)}, u32[]{:S(2)}) %collective-permute-start.4) | collective-permute-done | bytes 24608 | tf_op jit(solution)/shard_map/ppermute | solution.py:62
  42.3 2.8 %collective-permute-start.10 = (f32[2,2,24,768]{3,2,1,0:T(8,128)S(1)}, f32[2,2,24,768]{3,2,1,0:T(8,128)S(1)}, u32[]{:S(2)}, u32[]{:S(2)}) collective-permute-start(f32[2,2,24,768]{3,2,1,0:T(8,128)S(1)} %get-tuple-element.39.near_ref), channel_id=1, source_target_pairs={{128,0},{256,128},{384,256},{0,384},{129,1},{257,129},{385,257},{1... | collective-permute-start | bytes 884744 | tf_op jit(solution)/shard_map/ppermute | solution.py:57
  45.1 4.3 %collective-permute-start.9 = (f32[2,2,24,768]{3,2,1,0:T(8,128)S(1)}, f32[2,2,24,768]{3,2,1,0:T(8,128)S(1)}, u32[]{:S(2)}, u32[]{:S(2)}) collective-permute-start(f32[2,2,24,768]{3,2,1,0:T(8,128)S(1)} %get-tuple-element.38.far_ref), channel_id=1, source_target_pairs={{384,0},{0,128},{128,256},{256,384},{385,1},{1,129},{129,257},{257... | collective-permute-start | bytes 884744 | tf_op jit(solution)/shard_map/ppermute | solution.py:57
  49.4 6.0 %collective-permute-start.5 = (f32[2,16,384]{2,1,0:T(8,128)S(1)}, f32[2,16,384]{2,1,0:T(8,128)S(1)}, u32[]{:S(2)}, u32[]{:S(2)}) collective-permute-start(f32[2,16,384]{2,1,0:T(8,128)S(1)} %get-tuple-element.33.x_ref), channel_id=1, source_target_pairs={{0,120},{8,16},{16,8},{24,32},{32,24},{40,48},{48,40},{56,64},{64,... | collective-permute-start | bytes 147464 | tf_op jit(solution)/shard_map/ppermute | solution.py:62
  55.4 1.9 %collective-permute-start.6 = (f32[2,16,384]{2,1,0:T(8,128)S(1)}, f32[2,16,384]{2,1,0:T(8,128)S(1)}, u32[]{:S(2)}, u32[]{:S(2)}) collective-permute-start(f32[2,16,384]{2,1,0:T(8,128)S(1)} %get-tuple-element.33.x_ref), channel_id=1, source_target_pairs={{0,8},{8,0},{16,24},{24,16},{32,40},{40,32},{48,56},{56,48},{64,72... | collective-permute-start | bytes 147464 | tf_op jit(solution)/shard_map/ppermute | solution.py:62
  57.3 4.0 %collective-permute-done.5.first_ref = f32[2,16,384]{2,1,0:T(8,128)S(1)} collective-permute-done((f32[2,16,384]{2,1,0:T(8,128)S(1)}, f32[2,16,384]{2,1,0:T(8,128)S(1)}, u32[]{:S(2)}, u32[]{:S(2)}) %collective-permute-start.5) | collective-permute-done | bytes 49184 | tf_op jit(solution)/shard_map/ppermute | solution.py:62
  61.4 1.9 %collective-permute-start.7 = (f32[112,384]{1,0:T(8,128)S(1)}, f32[112,384]{1,0:T(8,128)S(1)}, u32[]{:S(2)}, u32[]{:S(2)}) collective-permute-start(f32[112,384]{1,0:T(8,128)S(1)} %shard_map.81.own_ref), channel_id=1, source_target_pairs={{0,7},{1,2},{2,1},{3,4},{4,3},{5,6},{6,5},{7,0},{8,15},{9,10},{10,... | collective-permute-start | bytes 516104 | tf_op jit(solution)/shard_map/ppermute | solution.py:62
  63.3 1.9 %collective-permute-start.8 = (f32[112,384]{1,0:T(8,128)S(1)}, f32[112,384]{1,0:T(8,128)S(1)}, u32[]{:S(2)}, u32[]{:S(2)}) collective-permute-start(f32[112,384]{1,0:T(8,128)S(1)} %shard_map.81.own_ref), channel_id=1, source_target_pairs={{0,1},{1,0},{2,3},{3,2},{4,5},{5,4},{6,7},{7,6},{8,9},{9,8},{10,11... | collective-permute-start | bytes 516104 | tf_op jit(solution)/shard_map/ppermute | solution.py:62
  65.5 4.5 %collective-permute-done.7.first_ref = f32[112,384]{1,0:T(8,128)S(1)} collective-permute-done((f32[112,384]{1,0:T(8,128)S(1)}, f32[112,384]{1,0:T(8,128)S(1)}, u32[]{:S(2)}, u32[]{:S(2)}) %collective-permute-start.7) | collective-permute-done | bytes 172064 | tf_op jit(solution)/shard_map/ppermute | solution.py:62
  70.0 1.9 %shard_map.84.x_ref = f32[2,16,384]{2,1,0:T(8,128)S(1)} custom-call(s32[1]{0:T(128)} %bitcast.odd_ref, f32[112,384]{1,0:T(8,128)S(1)} %shard_map.81.own_ref, f32[112,384]{1,0:T(8,128)S(1)} %collective-permute-done.7.first_ref, f32[112,384]{1,0:T(8,128)S(1)} %collective-permute-done.8.second_ref, f32[2,24,256]{2,1,0:T(8,128)S(1)} %get-tuple-element.35.g_ref, ...), custom_call_target="tpu_custom_call" | custom-call | flops 20000000 | bytes 1000000 | tf_op jit(solution)/shard_map/pallas_call | solution.py:477
  71.9 6.0 %collective-permute-start.11 = (f32[2,16,384]{2,1,0:T(8,128)S(1)}, f32[2,16,384]{2,1,0:T(8,128)S(1)}, u32[]{:S(2)}, u32[]{:S(2)}) collective-permute-start(f32[2,16,384]{2,1,0:T(8,128)S(1)} %shard_map.84.x_ref), channel_id=1, source_target_pairs={{0,120},{8,16},{16,8},{24,32},{32,24},{40,48},{48,40},{56,64},{64,... | collective-permute-start | bytes 147464 | tf_op jit(solution)/shard_map/ppermute | solution.py:62
  77.9 1.9 %collective-permute-start.12 = (f32[2,16,384]{2,1,0:T(8,128)S(1)}, f32[2,16,384]{2,1,0:T(8,128)S(1)}, u32[]{:S(2)}, u32[]{:S(2)}) collective-permute-start(f32[2,16,384]{2,1,0:T(8,128)S(1)} %shard_map.84.x_ref), channel_id=1, source_target_pairs={{0,8},{8,0},{16,24},{24,16},{32,40},{40,32},{48,56},{56,48},{64,72... | collective-permute-start | bytes 147464 | tf_op jit(solution)/shard_map/ppermute | solution.py:62
  79.9 4.1 %collective-permute-done.11.first_ref = f32[2,16,384]{2,1,0:T(8,128)S(1)} collective-permute-done((f32[2,16,384]{2,1,0:T(8,128)S(1)}, f32[2,16,384]{2,1,0:T(8,128)S(1)}, u32[]{:S(2)}, u32[]{:S(2)}) %collective-permute-start.11) | collective-permute-done | bytes 49184 | tf_op jit(solution)/shard_map/ppermute | solution.py:62
  83.9 2.2 %collective-permute-start.13 = (f32[96,384]{1,0:T(8,128)S(1)}, f32[96,384]{1,0:T(8,128)S(1)}, u32[]{:S(2)}, u32[]{:S(2)}) collective-permute-start(f32[96,384]{1,0:T(8,128)S(1)} %shard_map.85.own_ref), channel_id=1, source_target_pairs={{0,7},{1,2},{2,1},{3,4},{4,3},{5,6},{6,5},{7,0},{8,15},{9,10},{10,... | collective-permute-start | bytes 442376 | tf_op jit(solution)/shard_map/ppermute | solution.py:62
  86.1 1.9 %collective-permute-start.14 = (f32[96,384]{1,0:T(8,128)S(1)}, f32[96,384]{1,0:T(8,128)S(1)}, u32[]{:S(2)}, u32[]{:S(2)}) collective-permute-start(f32[96,384]{1,0:T(8,128)S(1)} %shard_map.85.own_ref), channel_id=1, source_target_pairs={{0,1},{1,0},{2,3},{3,2},{4,5},{5,4},{6,7},{7,6},{8,9},{9,8},{10,11... | collective-permute-start | bytes 442376 | tf_op jit(solution)/shard_map/ppermute | solution.py:62
  88.0 4.1 %collective-permute-done.13.first_ref = f32[96,384]{1,0:T(8,128)S(1)} collective-permute-done((f32[96,384]{1,0:T(8,128)S(1)}, f32[96,384]{1,0:T(8,128)S(1)}, u32[]{:S(2)}, u32[]{:S(2)}) %collective-permute-start.13) | collective-permute-done | bytes 147488 | tf_op jit(solution)/shard_map/ppermute | solution.py:62
  92.2 1.9 %shard_map.86.x_ref = f32[2,16,256]{2,1,0:T(8,128)S(1)} custom-call(s32[1]{0:T(128)} %bitcast.odd_ref, f32[96,384]{1,0:T(8,128)S(1)} %shard_map.85.own_ref, f32[96,384]{1,0:T(8,128)S(1)} %collective-permute-done.13.first_ref, f32[96,384]{1,0:T(8,128)S(1)} %collective-permute-done.14.second_ref, f32[2,24,256]{2,1,0:T(8,128)S(1)} %get-tuple-element.35.g_ref, ...), custom_call_target="tpu_custom_call" | custom-call | flops 20000000 | bytes 1000000 | tf_op jit(solution)/shard_map/pallas_call | solution.py:477
  94.1 6.0 %collective-permute-start.15 = (f32[2,16,256]{2,1,0:T(8,128)S(1)}, f32[2,16,256]{2,1,0:T(8,128)S(1)}, u32[]{:S(2)}, u32[]{:S(2)}) collective-permute-start(f32[2,16,256]{2,1,0:T(8,128)S(1)} %shard_map.86.x_ref), channel_id=1, source_target_pairs={{0,120},{8,16},{16,8},{24,32},{32,24},{40,48},{48,40},{56,64},{64,... | collective-permute-start | bytes 98312 | tf_op jit(solution)/shard_map/ppermute | solution.py:62
  100.2 1.9 %collective-permute-start.16 = (f32[2,16,256]{2,1,0:T(8,128)S(1)}, f32[2,16,256]{2,1,0:T(8,128)S(1)}, u32[]{:S(2)}, u32[]{:S(2)}) collective-permute-start(f32[2,16,256]{2,1,0:T(8,128)S(1)} %shard_map.86.x_ref), channel_id=1, source_target_pairs={{0,8},{8,0},{16,24},{24,16},{32,40},{40,32},{48,56},{56,48},{64,72... | collective-permute-start | bytes 98312 | tf_op jit(solution)/shard_map/ppermute | solution.py:62
  102.1 3.9 %collective-permute-done.15.first_ref = f32[2,16,256]{2,1,0:T(8,128)S(1)} collective-permute-done((f32[2,16,256]{2,1,0:T(8,128)S(1)}, f32[2,16,256]{2,1,0:T(8,128)S(1)}, u32[]{:S(2)}, u32[]{:S(2)}) %collective-permute-start.15) | collective-permute-done | bytes 32800 | tf_op jit(solution)/shard_map/ppermute | solution.py:62
  106.0 1.9 %collective-permute-start.17 = (f32[96,256]{1,0:T(8,128)S(1)}, f32[96,256]{1,0:T(8,128)S(1)}, u32[]{:S(2)}, u32[]{:S(2)}) collective-permute-start(f32[96,256]{1,0:T(8,128)S(1)} %shard_map.87.own_ref), channel_id=1, source_target_pairs={{0,7},{1,2},{2,1},{3,4},{4,3},{5,6},{6,5},{7,0},{8,15},{9,10},{10,... | collective-permute-start | bytes 294920 | tf_op jit(solution)/shard_map/ppermute | solution.py:62
  107.9 1.9 %collective-permute-start.18 = (f32[96,256]{1,0:T(8,128)S(1)}, f32[96,256]{1,0:T(8,128)S(1)}, u32[]{:S(2)}, u32[]{:S(2)}) collective-permute-start(f32[96,256]{1,0:T(8,128)S(1)} %shard_map.87.own_ref), channel_id=1, source_target_pairs={{0,1},{1,0},{2,3},{3,2},{4,5},{5,4},{6,7},{7,6},{8,9},{9,8},{10,11... | collective-permute-start | bytes 294920 | tf_op jit(solution)/shard_map/ppermute | solution.py:62
  110.7 3.0 %collective-permute-done.17.first_ref = f32[96,256]{1,0:T(8,128)S(1)} collective-permute-done((f32[96,256]{1,0:T(8,128)S(1)}, f32[96,256]{1,0:T(8,128)S(1)}, u32[]{:S(2)}, u32[]{:S(2)}) %collective-permute-start.17) | collective-permute-done | bytes 98336 | tf_op jit(solution)/shard_map/ppermute | solution.py:62
  113.7 1.6 %shard_map.88 = f32[4,2,32,36]{3,2,1,0:T(8,128)} custom-call(s32[1]{0:T(128)} %bitcast.odd_ref, f32[96,256]{1,0:T(8,128)S(1)} %shard_map.87.own_ref, f32[96,256]{1,0:T(8,128)S(1)} %collective-permute-done.17.first_ref, f32[96,256]{1,0:T(8,128)S(1)} %collective-permute-done.18.second_ref, f32[2,48,128]{2,1,0:T(8,128)S(1)} %get-tuple-element.45.wide_ref, ...), custom_call_target="tpu_custom_call" | custom-call | flops 10000000 | bytes 1000000 | tf_op jit(solution)/shard_map/pallas_call | solution.py:485
  (22 shorter events, 3.6 us)
Async XLA Ops:
  6.3 10.1 %collective-permute-start = (f32[2,72,128]{2,1,0:T(8,128)S(1)}, f32[2,72,128]{2,1,0:T(8,128)S(1)}, u32[]{:S(2)}, u32[]{:S(2)}) collective-permute-start(f32[2,72,128]{2,1,0:T(8,128)S(1)} %get-tuple-element.26.sums_ref.own_ref), channel_id=1, source_target_pairs={{0,384},{128,256},{256,128},{384,0},{1,385},{129,257},{257,129},{3... | collective-permute-start | bytes 221192 | tf_op jit(solution)/shard_map/ppermute | solution.py:62
  14.0 6.2 %collective-permute-start.1 = (f32[2,72,128]{2,1,0:T(8,128)S(1)}, f32[2,72,128]{2,1,0:T(8,128)S(1)}, u32[]{:S(2)}, u32[]{:S(2)}) collective-permute-start(f32[2,72,128]{2,1,0:T(8,128)S(1)} %get-tuple-element.26.sums_ref.own_ref), channel_id=1, source_target_pairs={{0,128},{128,0},{256,384},{384,256},{1,129},{129,1},{257,385},{385... | collective-permute-start | bytes 221192 | tf_op jit(solution)/shard_map/ppermute | solution.py:62
  20.4 7.1 %collective-permute-start.2 = (f32[24,384]{1,0:T(8,128)S(1)}, f32[24,384]{1,0:T(8,128)S(1)}, u32[]{:S(2)}, u32[]{:S(2)}) collective-permute-start(f32[24,384]{1,0:T(8,128)S(1)} %get-tuple-element.28), channel_id=1, source_target_pairs={{7,0},{0,1},{1,2},{2,3},{3,4},{4,5},{5,6},{6,7},{15,8},{8,9},{9,10... | collective-permute-start | bytes 110600 | tf_op jit(solution)/shard_map/ppermute | solution.py:57
  27.5 11.8 %collective-permute-start.3 = (f32[2,8,384]{2,1,0:T(8,128)S(1)}, f32[2,8,384]{2,1,0:T(8,128)S(1)}, u32[]{:S(2)}, u32[]{:S(2)}) collective-permute-start(f32[2,8,384]{2,1,0:T(8,128)S(1)} %get-tuple-element.59), channel_id=1, source_target_pairs={{0,120},{8,16},{16,8},{24,32},{32,24},{40,48},{48,40},{56,64},{64,... | collective-permute-start | bytes 73736 | tf_op jit(solution)/shard_map/ppermute | solution.py:62
  36.0 5.7 %collective-permute-start.4 = (f32[2,8,384]{2,1,0:T(8,128)S(1)}, f32[2,8,384]{2,1,0:T(8,128)S(1)}, u32[]{:S(2)}, u32[]{:S(2)}) collective-permute-start(f32[2,8,384]{2,1,0:T(8,128)S(1)} %get-tuple-element.58), channel_id=1, source_target_pairs={{0,8},{8,0},{16,24},{24,16},{32,40},{40,32},{48,56},{56,48},{64,72... | collective-permute-start | bytes 73736 | tf_op jit(solution)/shard_map/ppermute | solution.py:62
  42.3 23.0 %collective-permute-start.10 = (f32[2,2,24,768]{3,2,1,0:T(8,128)S(1)}, f32[2,2,24,768]{3,2,1,0:T(8,128)S(1)}, u32[]{:S(2)}, u32[]{:S(2)}) collective-permute-start(f32[2,2,24,768]{3,2,1,0:T(8,128)S(1)} %get-tuple-element.39.near_ref), channel_id=1, source_target_pairs={{128,0},{256,128},{384,256},{0,384},{129,1},{257,129},{385,257},{1... | collective-permute-start | bytes 884744 | tf_op jit(solution)/shard_map/ppermute | solution.py:57
  45.1 20.2 %collective-permute-start.9 = (f32[2,2,24,768]{3,2,1,0:T(8,128)S(1)}, f32[2,2,24,768]{3,2,1,0:T(8,128)S(1)}, u32[]{:S(2)}, u32[]{:S(2)}) collective-permute-start(f32[2,2,24,768]{3,2,1,0:T(8,128)S(1)} %get-tuple-element.38.far_ref), channel_id=1, source_target_pairs={{384,0},{0,128},{128,256},{256,384},{385,1},{1,129},{129,257},{257... | collective-permute-start | bytes 884744 | tf_op jit(solution)/shard_map/ppermute | solution.py:57
  49.4 12.0 %collective-permute-start.5 = (f32[2,16,384]{2,1,0:T(8,128)S(1)}, f32[2,16,384]{2,1,0:T(8,128)S(1)}, u32[]{:S(2)}, u32[]{:S(2)}) collective-permute-start(f32[2,16,384]{2,1,0:T(8,128)S(1)} %get-tuple-element.33.x_ref), channel_id=1, source_target_pairs={{0,120},{8,16},{16,8},{24,32},{32,24},{40,48},{48,40},{56,64},{64,... | collective-permute-start | bytes 147464 | tf_op jit(solution)/shard_map/ppermute | solution.py:62
  55.4 6.0 %collective-permute-start.6 = (f32[2,16,384]{2,1,0:T(8,128)S(1)}, f32[2,16,384]{2,1,0:T(8,128)S(1)}, u32[]{:S(2)}, u32[]{:S(2)}) collective-permute-start(f32[2,16,384]{2,1,0:T(8,128)S(1)} %get-tuple-element.33.x_ref), channel_id=1, source_target_pairs={{0,8},{8,0},{16,24},{24,16},{32,40},{40,32},{48,56},{56,48},{64,72... | collective-permute-start | bytes 147464 | tf_op jit(solution)/shard_map/ppermute | solution.py:62
  61.4 8.6 %collective-permute-start.7 = (f32[112,384]{1,0:T(8,128)S(1)}, f32[112,384]{1,0:T(8,128)S(1)}, u32[]{:S(2)}, u32[]{:S(2)}) collective-permute-start(f32[112,384]{1,0:T(8,128)S(1)} %shard_map.81.own_ref), channel_id=1, source_target_pairs={{0,7},{1,2},{2,1},{3,4},{4,3},{5,6},{6,5},{7,0},{8,15},{9,10},{10,... | collective-permute-start | bytes 516104 | tf_op jit(solution)/shard_map/ppermute | solution.py:62
  63.3 6.7 %collective-permute-start.8 = (f32[112,384]{1,0:T(8,128)S(1)}, f32[112,384]{1,0:T(8,128)S(1)}, u32[]{:S(2)}, u32[]{:S(2)}) collective-permute-start(f32[112,384]{1,0:T(8,128)S(1)} %shard_map.81.own_ref), channel_id=1, source_target_pairs={{0,1},{1,0},{2,3},{3,2},{4,5},{5,4},{6,7},{7,6},{8,9},{9,8},{10,11... | collective-permute-start | bytes 516104 | tf_op jit(solution)/shard_map/ppermute | solution.py:62
  71.9 12.0 %collective-permute-start.11 = (f32[2,16,384]{2,1,0:T(8,128)S(1)}, f32[2,16,384]{2,1,0:T(8,128)S(1)}, u32[]{:S(2)}, u32[]{:S(2)}) collective-permute-start(f32[2,16,384]{2,1,0:T(8,128)S(1)} %shard_map.84.x_ref), channel_id=1, source_target_pairs={{0,120},{8,16},{16,8},{24,32},{32,24},{40,48},{48,40},{56,64},{64,... | collective-permute-start | bytes 147464 | tf_op jit(solution)/shard_map/ppermute | solution.py:62
  77.9 6.0 %collective-permute-start.12 = (f32[2,16,384]{2,1,0:T(8,128)S(1)}, f32[2,16,384]{2,1,0:T(8,128)S(1)}, u32[]{:S(2)}, u32[]{:S(2)}) collective-permute-start(f32[2,16,384]{2,1,0:T(8,128)S(1)} %shard_map.84.x_ref), channel_id=1, source_target_pairs={{0,8},{8,0},{16,24},{24,16},{32,40},{40,32},{48,56},{56,48},{64,72... | collective-permute-start | bytes 147464 | tf_op jit(solution)/shard_map/ppermute | solution.py:62
  83.9 8.3 %collective-permute-start.13 = (f32[96,384]{1,0:T(8,128)S(1)}, f32[96,384]{1,0:T(8,128)S(1)}, u32[]{:S(2)}, u32[]{:S(2)}) collective-permute-start(f32[96,384]{1,0:T(8,128)S(1)} %shard_map.85.own_ref), channel_id=1, source_target_pairs={{0,7},{1,2},{2,1},{3,4},{4,3},{5,6},{6,5},{7,0},{8,15},{9,10},{10,... | collective-permute-start | bytes 442376 | tf_op jit(solution)/shard_map/ppermute | solution.py:62
  86.1 6.1 %collective-permute-start.14 = (f32[96,384]{1,0:T(8,128)S(1)}, f32[96,384]{1,0:T(8,128)S(1)}, u32[]{:S(2)}, u32[]{:S(2)}) collective-permute-start(f32[96,384]{1,0:T(8,128)S(1)} %shard_map.85.own_ref), channel_id=1, source_target_pairs={{0,1},{1,0},{2,3},{3,2},{4,5},{5,4},{6,7},{7,6},{8,9},{9,8},{10,11... | collective-permute-start | bytes 442376 | tf_op jit(solution)/shard_map/ppermute | solution.py:62
  94.1 11.8 %collective-permute-start.15 = (f32[2,16,256]{2,1,0:T(8,128)S(1)}, f32[2,16,256]{2,1,0:T(8,128)S(1)}, u32[]{:S(2)}, u32[]{:S(2)}) collective-permute-start(f32[2,16,256]{2,1,0:T(8,128)S(1)} %shard_map.86.x_ref), channel_id=1, source_target_pairs={{0,120},{8,16},{16,8},{24,32},{32,24},{40,48},{48,40},{56,64},{64,... | collective-permute-start | bytes 98312 | tf_op jit(solution)/shard_map/ppermute | solution.py:62
  100.2 5.8 %collective-permute-start.16 = (f32[2,16,256]{2,1,0:T(8,128)S(1)}, f32[2,16,256]{2,1,0:T(8,128)S(1)}, u32[]{:S(2)}, u32[]{:S(2)}) collective-permute-start(f32[2,16,256]{2,1,0:T(8,128)S(1)} %shard_map.86.x_ref), channel_id=1, source_target_pairs={{0,8},{8,0},{16,24},{24,16},{32,40},{40,32},{48,56},{56,48},{64,72... | collective-permute-start | bytes 98312 | tf_op jit(solution)/shard_map/ppermute | solution.py:62
  106.0 7.7 %collective-permute-start.17 = (f32[96,256]{1,0:T(8,128)S(1)}, f32[96,256]{1,0:T(8,128)S(1)}, u32[]{:S(2)}, u32[]{:S(2)}) collective-permute-start(f32[96,256]{1,0:T(8,128)S(1)} %shard_map.87.own_ref), channel_id=1, source_target_pairs={{0,7},{1,2},{2,1},{3,4},{4,3},{5,6},{6,5},{7,0},{8,15},{9,10},{10,... | collective-permute-start | bytes 294920 | tf_op jit(solution)/shard_map/ppermute | solution.py:62
  107.9 5.8 %collective-permute-start.18 = (f32[96,256]{1,0:T(8,128)S(1)}, f32[96,256]{1,0:T(8,128)S(1)}, u32[]{:S(2)}, u32[]{:S(2)}) collective-permute-start(f32[96,256]{1,0:T(8,128)S(1)} %shard_map.87.own_ref), channel_id=1, source_target_pairs={{0,1},{1,0},{2,3},{3,2},{4,5},{5,4},{6,7},{7,6},{8,9},{9,8},{10,11... | collective-permute-start | bytes 294920 | tf_op jit(solution)/shard_map/ppermute | solution.py:62

commit v8 on v7

--- a/solution.py
+++ b/solution.py
@@ -352,8 +352,8 @@
     for z in range(2):
         kept = jnp.concatenate([p[0][48 * z : 48 * z + 192] for p in pairs], axis=0)
         rest = jnp.concatenate([p[1][48 * z : 48 * z + 192] for p in pairs], axis=0)
-        both = dot(ah_ref[z], jnp.concatenate([kept, rest], axis=1))
-        found = by_x(both[:, 0:256] + both[:, 256:512] + dot(al_ref[z], kept), 8, 24)
+        both = dot(jnp.concatenate([ah_ref[z], al_ref[z]], axis=0), kept)
+        found = by_x(both[0:192] + both[192:384] + dot(ah_ref[z], rest), 8, 24)
         rows[0:24] = g_ref[z] - found
         found = by_x(three(bh_ref[z], bl_ref[z], rows[...]), 8, 24)
         rows[0:24] = found
@@ -459,6 +459,8 @@
             rows_right = after(rows_right, *pair)
             wide = (shape(2, 192, 768, dtype=BF16),) * 2
             operator = call(merge_kernel, wide, flops=10_000_000)(low_x, high_x, rows_left, rows_right)
+        if sweep == 1:
+            pair[0] = after(pair[0], every)
         pieces = (x, *pair, g) if sweep == 0 else (x, *pair)
         rows = shape(112 if sweep == 0 else 96, x.shape[2])
         own = call(layers_kernel, rows, scalar=True, count=len(pieces))(even_row, *pieces)

time: 116 us -> 116 us (level)
  no operation moved by 1% of the time
where the time goes in v8:
time: 116 us; the launch traced here: 115 us
  starting transfers between devices  64.6 us (56%)
  waiting for transfers between devices  36.8 us (32%)
  Pallas kernels  12.1 us (10%)
    ppermute x16, starting transfers between devices, matched(): lax.ppermute(block, axis, [(i, (i - 1 if i % 2 == which else i + 1) % cou...  55.7 us
    ppermute x16, waiting for transfers between devices, matched(): lax.ppermute(block, axis, [(i, (i - 1 if i % 2 == which else i + 1) % cou...  31.7 us
    ppermute x3, starting transfers between devices, shifted(): lax.ppermute(block, axis, [((i - distance) % count, i) for i in range(cou...  8.97 us
    pallas_call x1, Pallas kernels, start(): call(start_kernel, outs, (pltpu.VMEM((4, 24, 128), F32), pltpu.VMEM((4, 7...  5.67 us
    ppermute x3, waiting for transfers between devices, shifted(): lax.ppermute(block, axis, [((i - distance) % count, i) for i in range(cou...  5.14 us
    pallas_call x2, Pallas kernels, steps(): call(functools.partial(sweep_kernel, 5 - sweep), shape(2, 16, 384 if swee...  3.72 us
  transfers between devices with their start and end apart: 19, of which 11 were waited for; matrix products, arithmetic and copies ran while one was open for 1% of the time, Pallas kernels for 0%

profile of v8, /device:TPU:6, one launch (start us, length us, event | category | flops | bytes accessed | tf_op | source)
XLA Modules:
  0.0 115.2 jit_solution(12965491154326418054)
XLA Ops:
  0.6 5.7 %shard_map.77 = (f32[2,72,128]{2,1,0:T(8,128)S(1)}, bf16[2,4,40,768]{3,2,1,0:T(8,128)(2,1)S(1)}, bf16[2,4,40,768]{3,2,1,0:T(8,128)(2,1)S(1)}, bf16[2,4,40,128]{3...) custom-call(bf16[4,2,12,3,32,128]{5,4,3,2,1,0:T(8,128)(2,1)} %bitcas, ...), custom_call_target="tpu_custom_call" | custom-call | flops 40000000 | bytes 1000000 | tf_op jit(solution)/shard_map/pallas_call | solution.py:204
  6.3 7.7 %collective-permute-start = (f32[2,72,128]{2,1,0:T(8,128)S(1)}, f32[2,72,128]{2,1,0:T(8,128)S(1)}, u32[]{:S(2)}, u32[]{:S(2)}) collective-permute-start(f32[2,72,128]{2,1,0:T(8,128)S(1)} %get-tuple-element.27.sums_ref.own_ref), channel_id=1, source_target_pairs={{0,384},{128,256},{256,128},{384,0},{1,385},{129,257},{257,129},{3... | collective-permute-start | bytes 221192 | tf_op jit(solution)/shard_map/ppermute | solution.py:62
  14.0 1.9 %collective-permute-start.1 = (f32[2,72,128]{2,1,0:T(8,128)S(1)}, f32[2,72,128]{2,1,0:T(8,128)S(1)}, u32[]{:S(2)}, u32[]{:S(2)}) collective-permute-start(f32[2,72,128]{2,1,0:T(8,128)S(1)} %get-tuple-element.27.sums_ref.own_ref), channel_id=1, source_target_pairs={{0,128},{128,0},{256,384},{384,256},{1,129},{129,1},{257,385},{385... | collective-permute-start | bytes 221192 | tf_op jit(solution)/shard_map/ppermute | solution.py:62
  16.4 3.9 %collective-permute-done.1 = f32[2,72,128]{2,1,0:T(8,128)S(1)} collective-permute-done((f32[2,72,128]{2,1,0:T(8,128)S(1)}, f32[2,72,128]{2,1,0:T(8,128)S(1)}, u32[]{:S(2)}, u32[]{:S(2)}) %collective-permute-start.1) | collective-permute-done | bytes 73760 | tf_op jit(solution)/shard_map/ppermute | solution.py:62
  20.4 1.9 %collective-permute-start.2 = (f32[24,384]{1,0:T(8,128)S(1)}, f32[24,384]{1,0:T(8,128)S(1)}, u32[]{:S(2)}, u32[]{:S(2)}) collective-permute-start(f32[24,384]{1,0:T(8,128)S(1)} %get-tuple-element.29), channel_id=1, source_target_pairs={{7,0},{0,1},{1,2},{2,3},{3,4},{4,5},{5,6},{6,7},{15,8},{8,9},{9,10... | collective-permute-start | bytes 110600 | tf_op jit(solution)/shard_map/ppermute | solution.py:57
  22.3 5.1 %collective-permute-done.2.left_ref = f32[24,384]{1,0:T(8,128)S(1)} collective-permute-done((f32[24,384]{1,0:T(8,128)S(1)}, f32[24,384]{1,0:T(8,128)S(1)}, u32[]{:S(2)}, u32[]{:S(2)}) %collective-permute-start.2) | collective-permute-done | bytes 36896 | tf_op jit(solution)/shard_map/ppermute | solution.py:57
  27.5 8.5 %collective-permute-start.3 = (f32[2,8,384]{2,1,0:T(8,128)S(1)}, f32[2,8,384]{2,1,0:T(8,128)S(1)}, u32[]{:S(2)}, u32[]{:S(2)}) collective-permute-start(f32[2,8,384]{2,1,0:T(8,128)S(1)} %get-tuple-element.61), channel_id=1, source_target_pairs={{0,120},{8,16},{16,8},{24,32},{32,24},{40,48},{48,40},{56,64},{64,... | collective-permute-start | bytes 73736 | tf_op jit(solution)/shard_map/ppermute | solution.py:62
  36.0 1.9 %collective-permute-start.4 = (f32[2,8,384]{2,1,0:T(8,128)S(1)}, f32[2,8,384]{2,1,0:T(8,128)S(1)}, u32[]{:S(2)}, u32[]{:S(2)}) collective-permute-start(f32[2,8,384]{2,1,0:T(8,128)S(1)} %get-tuple-element.60), channel_id=1, source_target_pairs={{0,8},{8,0},{16,24},{24,16},{32,40},{40,32},{48,56},{56,48},{64,72... | collective-permute-start | bytes 73736 | tf_op jit(solution)/shard_map/ppermute | solution.py:62
  39.3 2.4 %collective-permute-done.4 = f32[2,8,384]{2,1,0:T(8,128)S(1)} collective-permute-done((f32[2,8,384]{2,1,0:T(8,128)S(1)}, f32[2,8,384]{2,1,0:T(8,128)S(1)}, u32[]{:S(2)}, u32[]{:S(2)}) %collective-permute-start.4) | collective-permute-done | bytes 24608 | tf_op jit(solution)/shard_map/ppermute | solution.py:62
  42.3 2.8 %collective-permute-start.10 = (f32[2,2,24,768]{3,2,1,0:T(8,128)S(1)}, f32[2,2,24,768]{3,2,1,0:T(8,128)S(1)}, u32[]{:S(2)}, u32[]{:S(2)}) collective-permute-start(f32[2,2,24,768]{3,2,1,0:T(8,128)S(1)} %get-tuple-element.40.near_ref), channel_id=1, source_target_pairs={{128,0},{256,128},{384,256},{0,384},{129,1},{257,129},{385,257},{1... | collective-permute-start | bytes 884744 | tf_op jit(solution)/shard_map/ppermute | solution.py:57
  45.1 4.3 %collective-permute-start.9 = (f32[2,2,24,768]{3,2,1,0:T(8,128)S(1)}, f32[2,2,24,768]{3,2,1,0:T(8,128)S(1)}, u32[]{:S(2)}, u32[]{:S(2)}) collective-permute-start(f32[2,2,24,768]{3,2,1,0:T(8,128)S(1)} %get-tuple-element.39.far_ref), channel_id=1, source_target_pairs={{384,0},{0,128},{128,256},{256,384},{385,1},{1,129},{129,257},{257... | collective-permute-start | bytes 884744 | tf_op jit(solution)/shard_map/ppermute | solution.py:57
  49.4 6.0 %collective-permute-start.5 = (f32[2,16,384]{2,1,0:T(8,128)S(1)}, f32[2,16,384]{2,1,0:T(8,128)S(1)}, u32[]{:S(2)}, u32[]{:S(2)}) collective-permute-start(f32[2,16,384]{2,1,0:T(8,128)S(1)} %get-tuple-element.34.x_ref), channel_id=1, source_target_pairs={{0,120},{8,16},{16,8},{24,32},{32,24},{40,48},{48,40},{56,64},{64,... | collective-permute-start | bytes 147464 | tf_op jit(solution)/shard_map/ppermute | solution.py:62
  55.4 1.9 %collective-permute-start.6 = (f32[2,16,384]{2,1,0:T(8,128)S(1)}, f32[2,16,384]{2,1,0:T(8,128)S(1)}, u32[]{:S(2)}, u32[]{:S(2)}) collective-permute-start(f32[2,16,384]{2,1,0:T(8,128)S(1)} %get-tuple-element.34.x_ref), channel_id=1, source_target_pairs={{0,8},{8,0},{16,24},{24,16},{32,40},{40,32},{48,56},{56,48},{64,72... | collective-permute-start | bytes 147464 | tf_op jit(solution)/shard_map/ppermute | solution.py:62
  57.3 4.0 %collective-permute-done.5.first_ref = f32[2,16,384]{2,1,0:T(8,128)S(1)} collective-permute-done((f32[2,16,384]{2,1,0:T(8,128)S(1)}, f32[2,16,384]{2,1,0:T(8,128)S(1)}, u32[]{:S(2)}, u32[]{:S(2)}) %collective-permute-start.5) | collective-permute-done | bytes 49184 | tf_op jit(solution)/shard_map/ppermute | solution.py:62
  61.4 1.9 %collective-permute-start.7 = (f32[112,384]{1,0:T(8,128)S(1)}, f32[112,384]{1,0:T(8,128)S(1)}, u32[]{:S(2)}, u32[]{:S(2)}) collective-permute-start(f32[112,384]{1,0:T(8,128)S(1)} %shard_map.81.own_ref), channel_id=1, source_target_pairs={{0,7},{1,2},{2,1},{3,4},{4,3},{5,6},{6,5},{7,0},{8,15},{9,10},{10,... | collective-permute-start | bytes 516104 | tf_op jit(solution)/shard_map/ppermute | solution.py:62
  63.3 1.9 %collective-permute-start.8 = (f32[112,384]{1,0:T(8,128)S(1)}, f32[112,384]{1,0:T(8,128)S(1)}, u32[]{:S(2)}, u32[]{:S(2)}) collective-permute-start(f32[112,384]{1,0:T(8,128)S(1)} %shard_map.81.own_ref), channel_id=1, source_target_pairs={{0,1},{1,0},{2,3},{3,2},{4,5},{5,4},{6,7},{7,6},{8,9},{9,8},{10,11... | collective-permute-start | bytes 516104 | tf_op jit(solution)/shard_map/ppermute | solution.py:62
  65.5 4.5 %collective-permute-done.7.first_ref = f32[112,384]{1,0:T(8,128)S(1)} collective-permute-done((f32[112,384]{1,0:T(8,128)S(1)}, f32[112,384]{1,0:T(8,128)S(1)}, u32[]{:S(2)}, u32[]{:S(2)}) %collective-permute-start.7) | collective-permute-done | bytes 172064 | tf_op jit(solution)/shard_map/ppermute | solution.py:62
  70.0 1.8 %shard_map.84.x_ref = f32[2,16,384]{2,1,0:T(8,128)S(1)} custom-call(s32[1]{0:T(128)} %bitcast.odd_ref, f32[112,384]{1,0:T(8,128)S(1)} %shard_map.81.own_ref, f32[112,384]{1,0:T(8,128)S(1)} %collective-permute-done.7.first_ref, f32[112,384]{1,0:T(8,128)S(1)} %collective-permute-done.8.second_ref, f32[2,24,256]{2,1,0:T(8,128)S(1)} %get-tuple-element.36.g_ref, ...), custom_call_target="tpu_custom_call" | custom-call | flops 20000000 | bytes 1000000 | tf_op jit(solution)/shard_map/pallas_call | solution.py:479
  71.8 6.0 %collective-permute-start.11 = (f32[2,16,384]{2,1,0:T(8,128)S(1)}, f32[2,16,384]{2,1,0:T(8,128)S(1)}, u32[]{:S(2)}, u32[]{:S(2)}) collective-permute-start(f32[2,16,384]{2,1,0:T(8,128)S(1)} %shard_map.84.x_ref), channel_id=1, source_target_pairs={{0,120},{8,16},{16,8},{24,32},{32,24},{40,48},{48,40},{56,64},{64,... | collective-permute-start | bytes 147464 | tf_op jit(solution)/shard_map/ppermute | solution.py:62
  77.9 1.9 %collective-permute-start.12 = (f32[2,16,384]{2,1,0:T(8,128)S(1)}, f32[2,16,384]{2,1,0:T(8,128)S(1)}, u32[]{:S(2)}, u32[]{:S(2)}) collective-permute-start(f32[2,16,384]{2,1,0:T(8,128)S(1)} %shard_map.84.x_ref), channel_id=1, source_target_pairs={{0,8},{8,0},{16,24},{24,16},{32,40},{40,32},{48,56},{56,48},{64,72... | collective-permute-start | bytes 147464 | tf_op jit(solution)/shard_map/ppermute | solution.py:62
  80.0 3.9 %collective-permute-done.11.first_ref = f32[2,16,384]{2,1,0:T(8,128)S(1)} collective-permute-done((f32[2,16,384]{2,1,0:T(8,128)S(1)}, f32[2,16,384]{2,1,0:T(8,128)S(1)}, u32[]{:S(2)}, u32[]{:S(2)}) %collective-permute-start.11) | collective-permute-done | bytes 49184 | tf_op jit(solution)/shard_map/ppermute | solution.py:62
  83.9 2.2 %collective-permute-start.13 = (f32[96,384]{1,0:T(8,128)S(1)}, f32[96,384]{1,0:T(8,128)S(1)}, u32[]{:S(2)}, u32[]{:S(2)}) collective-permute-start(f32[96,384]{1,0:T(8,128)S(1)} %shard_map.85.own_ref), channel_id=1, source_target_pairs={{0,7},{1,2},{2,1},{3,4},{4,3},{5,6},{6,5},{7,0},{8,15},{9,10},{10,... | collective-permute-start | bytes 442376 | tf_op jit(solution)/shard_map/ppermute | solution.py:62
  86.1 1.9 %collective-permute-start.14 = (f32[96,384]{1,0:T(8,128)S(1)}, f32[96,384]{1,0:T(8,128)S(1)}, u32[]{:S(2)}, u32[]{:S(2)}) collective-permute-start(f32[96,384]{1,0:T(8,128)S(1)} %shard_map.85.own_ref), channel_id=1, source_target_pairs={{0,1},{1,0},{2,3},{3,2},{4,5},{5,4},{6,7},{7,6},{8,9},{9,8},{10,11... | collective-permute-start | bytes 442376 | tf_op jit(solution)/shard_map/ppermute | solution.py:62
  88.0 4.1 %collective-permute-done.13.first_ref = f32[96,384]{1,0:T(8,128)S(1)} collective-permute-done((f32[96,384]{1,0:T(8,128)S(1)}, f32[96,384]{1,0:T(8,128)S(1)}, u32[]{:S(2)}, u32[]{:S(2)}) %collective-permute-start.13) | collective-permute-done | bytes 147488 | tf_op jit(solution)/shard_map/ppermute | solution.py:62
  92.1 1.9 %shard_map.86.x_ref = f32[2,16,256]{2,1,0:T(8,128)S(1)} custom-call(s32[1]{0:T(128)} %bitcast.odd_ref, f32[96,384]{1,0:T(8,128)S(1)} %shard_map.85.own_ref, f32[96,384]{1,0:T(8,128)S(1)} %collective-permute-done.13.first_ref, f32[96,384]{1,0:T(8,128)S(1)} %collective-permute-done.14.second_ref, f32[2,24,256]{2,1,0:T(8,128)S(1)} %get-tuple-element.36.g_ref, ...), custom_call_target="tpu_custom_call" | custom-call | flops 20000000 | bytes 1000000 | tf_op jit(solution)/shard_map/pallas_call | solution.py:479
  94.0 6.0 %collective-permute-start.15 = (f32[2,16,256]{2,1,0:T(8,128)S(1)}, f32[2,16,256]{2,1,0:T(8,128)S(1)}, u32[]{:S(2)}, u32[]{:S(2)}) collective-permute-start(f32[2,16,256]{2,1,0:T(8,128)S(1)} %shard_map.86.x_ref), channel_id=1, source_target_pairs={{0,120},{8,16},{16,8},{24,32},{32,24},{40,48},{48,40},{56,64},{64,... | collective-permute-start | bytes 98312 | tf_op jit(solution)/shard_map/ppermute | solution.py:62
  100.0 1.9 %collective-permute-start.16 = (f32[2,16,256]{2,1,0:T(8,128)S(1)}, f32[2,16,256]{2,1,0:T(8,128)S(1)}, u32[]{:S(2)}, u32[]{:S(2)}) collective-permute-start(f32[2,16,256]{2,1,0:T(8,128)S(1)} %shard_map.86.x_ref), channel_id=1, source_target_pairs={{0,8},{8,0},{16,24},{24,16},{32,40},{40,32},{48,56},{56,48},{64,72... | collective-permute-start | bytes 98312 | tf_op jit(solution)/shard_map/ppermute | solution.py:62
  102.0 3.9 %collective-permute-done.15.first_ref = f32[2,16,256]{2,1,0:T(8,128)S(1)} collective-permute-done((f32[2,16,256]{2,1,0:T(8,128)S(1)}, f32[2,16,256]{2,1,0:T(8,128)S(1)}, u32[]{:S(2)}, u32[]{:S(2)}) %collective-permute-start.15) | collective-permute-done | bytes 32800 | tf_op jit(solution)/shard_map/ppermute | solution.py:62
  105.9 1.9 %collective-permute-start.17 = (f32[96,256]{1,0:T(8,128)S(1)}, f32[96,256]{1,0:T(8,128)S(1)}, u32[]{:S(2)}, u32[]{:S(2)}) collective-permute-start(f32[96,256]{1,0:T(8,128)S(1)} %shard_map.87.own_ref), channel_id=1, source_target_pairs={{0,7},{1,2},{2,1},{3,4},{4,3},{5,6},{6,5},{7,0},{8,15},{9,10},{10,... | collective-permute-start | bytes 294920 | tf_op jit(solution)/shard_map/ppermute | solution.py:62
  107.8 1.9 %collective-permute-start.18 = (f32[96,256]{1,0:T(8,128)S(1)}, f32[96,256]{1,0:T(8,128)S(1)}, u32[]{:S(2)}, u32[]{:S(2)}) collective-permute-start(f32[96,256]{1,0:T(8,128)S(1)} %shard_map.87.own_ref), channel_id=1, source_target_pairs={{0,1},{1,0},{2,3},{3,2},{4,5},{5,4},{6,7},{7,6},{8,9},{9,8},{10,11... | collective-permute-start | bytes 294920 | tf_op jit(solution)/shard_map/ppermute | solution.py:62
  110.5 3.1 %collective-permute-done.17.first_ref = f32[96,256]{1,0:T(8,128)S(1)} collective-permute-done((f32[96,256]{1,0:T(8,128)S(1)}, f32[96,256]{1,0:T(8,128)S(1)}, u32[]{:S(2)}, u32[]{:S(2)}) %collective-permute-start.17) | collective-permute-done | bytes 98336 | tf_op jit(solution)/shard_map/ppermute | solution.py:62
  113.6 1.6 %shard_map.88 = f32[4,2,32,36]{3,2,1,0:T(8,128)} custom-call(s32[1]{0:T(128)} %bitcast.odd_ref, f32[96,256]{1,0:T(8,128)S(1)} %shard_map.87.own_ref, f32[96,256]{1,0:T(8,128)S(1)} %collective-permute-done.17.first_ref, f32[96,256]{1,0:T(8,128)S(1)} %collective-permute-done.18.second_ref, f32[2,48,128]{2,1,0:T(8,128)S(1)} %get-tuple-element.46.wide_ref, ...), custom_call_target="tpu_custom_call" | custom-call | flops 10000000 | bytes 1000000 | tf_op jit(solution)/shard_map/pallas_call | solution.py:487
  (22 shorter events, 3.6 us)
Async XLA Ops:
  6.3 10.1 %collective-permute-start = (f32[2,72,128]{2,1,0:T(8,128)S(1)}, f32[2,72,128]{2,1,0:T(8,128)S(1)}, u32[]{:S(2)}, u32[]{:S(2)}) collective-permute-start(f32[2,72,128]{2,1,0:T(8,128)S(1)} %get-tuple-element.27.sums_ref.own_ref), channel_id=1, source_target_pairs={{0,384},{128,256},{256,128},{384,0},{1,385},{129,257},{257,129},{3... | collective-permute-start | bytes 221192 | tf_op jit(solution)/shard_map/ppermute | solution.py:62
  14.0 6.2 %collective-permute-start.1 = (f32[2,72,128]{2,1,0:T(8,128)S(1)}, f32[2,72,128]{2,1,0:T(8,128)S(1)}, u32[]{:S(2)}, u32[]{:S(2)}) collective-permute-start(f32[2,72,128]{2,1,0:T(8,128)S(1)} %get-tuple-element.27.sums_ref.own_ref), channel_id=1, source_target_pairs={{0,128},{128,0},{256,384},{384,256},{1,129},{129,1},{257,385},{385... | collective-permute-start | bytes 221192 | tf_op jit(solution)/shard_map/ppermute | solution.py:62
  20.4 7.1 %collective-permute-start.2 = (f32[24,384]{1,0:T(8,128)S(1)}, f32[24,384]{1,0:T(8,128)S(1)}, u32[]{:S(2)}, u32[]{:S(2)}) collective-permute-start(f32[24,384]{1,0:T(8,128)S(1)} %get-tuple-element.29), channel_id=1, source_target_pairs={{7,0},{0,1},{1,2},{2,3},{3,4},{4,5},{5,6},{6,7},{15,8},{8,9},{9,10... | collective-permute-start | bytes 110600 | tf_op jit(solution)/shard_map/ppermute | solution.py:57
  27.5 11.8 %collective-permute-start.3 = (f32[2,8,384]{2,1,0:T(8,128)S(1)}, f32[2,8,384]{2,1,0:T(8,128)S(1)}, u32[]{:S(2)}, u32[]{:S(2)}) collective-permute-start(f32[2,8,384]{2,1,0:T(8,128)S(1)} %get-tuple-element.61), channel_id=1, source_target_pairs={{0,120},{8,16},{16,8},{24,32},{32,24},{40,48},{48,40},{56,64},{64,... | collective-permute-start | bytes 73736 | tf_op jit(solution)/shard_map/ppermute | solution.py:62
  36.0 5.7 %collective-permute-start.4 = (f32[2,8,384]{2,1,0:T(8,128)S(1)}, f32[2,8,384]{2,1,0:T(8,128)S(1)}, u32[]{:S(2)}, u32[]{:S(2)}) collective-permute-start(f32[2,8,384]{2,1,0:T(8,128)S(1)} %get-tuple-element.60), channel_id=1, source_target_pairs={{0,8},{8,0},{16,24},{24,16},{32,40},{40,32},{48,56},{56,48},{64,72... | collective-permute-start | bytes 73736 | tf_op jit(solution)/shard_map/ppermute | solution.py:62
  42.3 23.0 %collective-permute-start.10 = (f32[2,2,24,768]{3,2,1,0:T(8,128)S(1)}, f32[2,2,24,768]{3,2,1,0:T(8,128)S(1)}, u32[]{:S(2)}, u32[]{:S(2)}) collective-permute-start(f32[2,2,24,768]{3,2,1,0:T(8,128)S(1)} %get-tuple-element.40.near_ref), channel_id=1, source_target_pairs={{128,0},{256,128},{384,256},{0,384},{129,1},{257,129},{385,257},{1... | collective-permute-start | bytes 884744 | tf_op jit(solution)/shard_map/ppermute | solution.py:57
  45.1 20.2 %collective-permute-start.9 = (f32[2,2,24,768]{3,2,1,0:T(8,128)S(1)}, f32[2,2,24,768]{3,2,1,0:T(8,128)S(1)}, u32[]{:S(2)}, u32[]{:S(2)}) collective-permute-start(f32[2,2,24,768]{3,2,1,0:T(8,128)S(1)} %get-tuple-element.39.far_ref), channel_id=1, source_target_pairs={{384,0},{0,128},{128,256},{256,384},{385,1},{1,129},{129,257},{257... | collective-permute-start | bytes 884744 | tf_op jit(solution)/shard_map/ppermute | solution.py:57
  49.4 12.0 %collective-permute-start.5 = (f32[2,16,384]{2,1,0:T(8,128)S(1)}, f32[2,16,384]{2,1,0:T(8,128)S(1)}, u32[]{:S(2)}, u32[]{:S(2)}) collective-permute-start(f32[2,16,384]{2,1,0:T(8,128)S(1)} %get-tuple-element.34.x_ref), channel_id=1, source_target_pairs={{0,120},{8,16},{16,8},{24,32},{32,24},{40,48},{48,40},{56,64},{64,... | collective-permute-start | bytes 147464 | tf_op jit(solution)/shard_map/ppermute | solution.py:62
  55.4 6.0 %collective-permute-start.6 = (f32[2,16,384]{2,1,0:T(8,128)S(1)}, f32[2,16,384]{2,1,0:T(8,128)S(1)}, u32[]{:S(2)}, u32[]{:S(2)}) collective-permute-start(f32[2,16,384]{2,1,0:T(8,128)S(1)} %get-tuple-element.34.x_ref), channel_id=1, source_target_pairs={{0,8},{8,0},{16,24},{24,16},{32,40},{40,32},{48,56},{56,48},{64,72... | collective-permute-start | bytes 147464 | tf_op jit(solution)/shard_map/ppermute | solution.py:62
  61.4 8.6 %collective-permute-start.7 = (f32[112,384]{1,0:T(8,128)S(1)}, f32[112,384]{1,0:T(8,128)S(1)}, u32[]{:S(2)}, u32[]{:S(2)}) collective-permute-start(f32[112,384]{1,0:T(8,128)S(1)} %shard_map.81.own_ref), channel_id=1, source_target_pairs={{0,7},{1,2},{2,1},{3,4},{4,3},{5,6},{6,5},{7,0},{8,15},{9,10},{10,... | collective-permute-start | bytes 516104 | tf_op jit(solution)/shard_map/ppermute | solution.py:62
  63.3 6.7 %collective-permute-start.8 = (f32[112,384]{1,0:T(8,128)S(1)}, f32[112,384]{1,0:T(8,128)S(1)}, u32[]{:S(2)}, u32[]{:S(2)}) collective-permute-start(f32[112,384]{1,0:T(8,128)S(1)} %shard_map.81.own_ref), channel_id=1, source_target_pairs={{0,1},{1,0},{2,3},{3,2},{4,5},{5,4},{6,7},{7,6},{8,9},{9,8},{10,11... | collective-permute-start | bytes 516104 | tf_op jit(solution)/shard_map/ppermute | solution.py:62
  71.8 12.0 %collective-permute-start.11 = (f32[2,16,384]{2,1,0:T(8,128)S(1)}, f32[2,16,384]{2,1,0:T(8,128)S(1)}, u32[]{:S(2)}, u32[]{:S(2)}) collective-permute-start(f32[2,16,384]{2,1,0:T(8,128)S(1)} %shard_map.84.x_ref), channel_id=1, source_target_pairs={{0,120},{8,16},{16,8},{24,32},{32,24},{40,48},{48,40},{56,64},{64,... | collective-permute-start | bytes 147464 | tf_op jit(solution)/shard_map/ppermute | solution.py:62
  77.9 6.0 %collective-permute-start.12 = (f32[2,16,384]{2,1,0:T(8,128)S(1)}, f32[2,16,384]{2,1,0:T(8,128)S(1)}, u32[]{:S(2)}, u32[]{:S(2)}) collective-permute-start(f32[2,16,384]{2,1,0:T(8,128)S(1)} %shard_map.84.x_ref), channel_id=1, source_target_pairs={{0,8},{8,0},{16,24},{24,16},{32,40},{40,32},{48,56},{56,48},{64,72... | collective-permute-start | bytes 147464 | tf_op jit(solution)/shard_map/ppermute | solution.py:62
  83.9 8.3 %collective-permute-start.13 = (f32[96,384]{1,0:T(8,128)S(1)}, f32[96,384]{1,0:T(8,128)S(1)}, u32[]{:S(2)}, u32[]{:S(2)}) collective-permute-start(f32[96,384]{1,0:T(8,128)S(1)} %shard_map.85.own_ref), channel_id=1, source_target_pairs={{0,7},{1,2},{2,1},{3,4},{4,3},{5,6},{6,5},{7,0},{8,15},{9,10},{10,... | collective-permute-start | bytes 442376 | tf_op jit(solution)/shard_map/ppermute | solution.py:62
  86.1 6.1 %collective-permute-start.14 = (f32[96,384]{1,0:T(8,128)S(1)}, f32[96,384]{1,0:T(8,128)S(1)}, u32[]{:S(2)}, u32[]{:S(2)}) collective-permute-start(f32[96,384]{1,0:T(8,128)S(1)} %shard_map.85.own_ref), channel_id=1, source_target_pairs={{0,1},{1,0},{2,3},{3,2},{4,5},{5,4},{6,7},{7,6},{8,9},{9,8},{10,11... | collective-permute-start | bytes 442376 | tf_op jit(solution)/shard_map/ppermute | solution.py:62
  94.0 11.8 %collective-permute-start.15 = (f32[2,16,256]{2,1,0:T(8,128)S(1)}, f32[2,16,256]{2,1,0:T(8,128)S(1)}, u32[]{:S(2)}, u32[]{:S(2)}) collective-permute-start(f32[2,16,256]{2,1,0:T(8,128)S(1)} %shard_map.86.x_ref), channel_id=1, source_target_pairs={{0,120},{8,16},{16,8},{24,32},{32,24},{40,48},{48,40},{56,64},{64,... | collective-permute-start | bytes 98312 | tf_op jit(solution)/shard_map/ppermute | solution.py:62
  100.0 5.8 %collective-permute-start.16 = (f32[2,16,256]{2,1,0:T(8,128)S(1)}, f32[2,16,256]{2,1,0:T(8,128)S(1)}, u32[]{:S(2)}, u32[]{:S(2)}) collective-permute-start(f32[2,16,256]{2,1,0:T(8,128)S(1)} %shard_map.86.x_ref), channel_id=1, source_target_pairs={{0,8},{8,0},{16,24},{24,16},{32,40},{40,32},{48,56},{56,48},{64,72... | collective-permute-start | bytes 98312 | tf_op jit(solution)/shard_map/ppermute | solution.py:62
  105.9 7.7 %collective-permute-start.17 = (f32[96,256]{1,0:T(8,128)S(1)}, f32[96,256]{1,0:T(8,128)S(1)}, u32[]{:S(2)}, u32[]{:S(2)}) collective-permute-start(f32[96,256]{1,0:T(8,128)S(1)} %shard_map.87.own_ref), channel_id=1, source_target_pairs={{0,7},{1,2},{2,1},{3,4},{4,3},{5,6},{6,5},{7,0},{8,15},{9,10},{10,... | collective-permute-start | bytes 294920 | tf_op jit(solution)/shard_map/ppermute | solution.py:62
  107.8 5.8 %collective-permute-start.18 = (f32[96,256]{1,0:T(8,128)S(1)}, f32[96,256]{1,0:T(8,128)S(1)}, u32[]{:S(2)}, u32[]{:S(2)}) collective-permute-start(f32[96,256]{1,0:T(8,128)S(1)} %shard_map.87.own_ref), channel_id=1, source_target_pairs={{0,1},{1,0},{2,3},{3,2},{4,5},{5,4},{6,7},{7,6},{8,9},{9,8},{10,11... | collective-permute-start | bytes 294920 | tf_op jit(solution)/shard_map/ppermute | solution.py:62
